TPU v7x, 256 devices: a whole 4x4x8 slice. The times are simulated.
256 devices in a mesh: band: 32 (over z, x_hi, core), lane: 8 (over y, x_lo).
Axes of the slice: x: 4 (x_hi: 2, x_lo: 2; x = x_hi * 2 + x_lo), y: 4, z: 8, core: 2. Of those that a mesh axis runs over, the one named last changes fastest.
Arguments:
- load_terms: float32 [2048, 512, 256], P('band', 'lane'), may hold values from -6 to 6
- start_values: float32 [2048, 512, 256], P('band', 'lane'), may hold values from -6 to 6
- reaction_rate: float32 [2048, 512, 256], P('band', 'lane'), may hold values from 0.1 to 0.9
Outputs:
- solution: float32 [2048, 512, 256], P('band', 'lane')
- remaining: float32 [2048, 512, 256], P('band', 'lane')
All inputs are finite; a program needn't handle non-finite values.
Results may differ from a plain program's by a relative error of at most 0.0003.
Values sent between devices are 32-bit elements.
No kernel may reach another device: no remote copies, remote signals or barrier semaphores. Data moves between devices by JAX's collectives and lax.ppermute only.
A program may use at most 128 MiB of HBM per device.

v0:
```python
import jax
import jax.numpy as jnp
from jax import lax
from jax.sharding import PartitionSpec as P

RATIO = 2
BEFORE = 3
AFTER = 2
INNER = 13


def extended(value, sides, width, wrap):
    edges = {}
    for axis, dim in sides:
        devices, length = lax.axis_size(axis), value.shape[dim]
        up = [(i, (i + 1) % devices) for i in range(devices if wrap else devices - 1)]
        last = lax.slice_in_dim(value, length - width, length, axis=dim)
        leading = lax.slice_in_dim(value, 0, width, axis=dim)
        edges[dim] = lax.ppermute(last, axis, up), lax.ppermute(
            leading, axis, [(b, a) for a, b in up]
        )
    done = []
    for _, dim in sides:
        low, high = edges[dim]
        around = [(width, width) if d in done else (0, 0) for d in range(value.ndim)]
        value = jnp.concatenate([jnp.pad(low, around), value, jnp.pad(high, around)], axis=dim)
        done.append(dim)
    return value


def padded_2(block, sides, width, periodic):
    for axis, dim in sides:
        count = lax.axis_size(axis)
        forward = [(i, i + 1) for i in range(count - 1)]
        if periodic:
            forward.append((count - 1, 0))
        backward = [(target, source) for source, target in forward]
        low = lax.ppermute(
            lax.slice_in_dim(block, block.shape[dim] - width, None, axis=dim), axis, forward
        )
        high = lax.ppermute(lax.slice_in_dim(block, 0, width, axis=dim), axis, backward)
        block = jnp.concatenate([low, block, high], axis=dim)
    return block


def cross_sum(padded):
    inner_y, inner_x = (padded.shape[0] - 2, padded.shape[1] - 2)
    middle_rows = lax.slice_in_dim(padded, 1, 1 + inner_y, axis=0)
    middle_columns = lax.slice_in_dim(padded, 1, 1 + inner_x, axis=1)
    return (
        lax.slice_in_dim(middle_columns, 0, inner_y, axis=0)
        + lax.slice_in_dim(middle_columns, 2, 2 + inner_y, axis=0)
        + lax.slice_in_dim(middle_rows, 0, inner_x, axis=1)
        + lax.slice_in_dim(middle_rows, 2, 2 + inner_x, axis=1)
    )


def smooth_step(padded, values, load, mass_here):
    return values + 0.8 * (load + cross_sum(padded) - (4.0 + mass_here) * values) / (
        4.0 + mass_here
    )


def block_means(values):
    cut = values.reshape(
        values.shape[0] // RATIO, RATIO, values.shape[1] // RATIO, RATIO, values.shape[2]
    )
    return jnp.mean(cut, axis=(1, 3))


def spread_blocks(values):
    return jnp.repeat(jnp.repeat(values, RATIO, axis=0), RATIO, axis=1)


def strip_rim(values):
    return lax.slice_in_dim(
        lax.slice_in_dim(values, 1, values.shape[0] - 1, axis=0), 1, values.shape[1] - 1, axis=1
    )


def body(load_terms, start_values, reaction_rate):
    values = start_values
    for sweep in range(BEFORE):
        values = smooth_step(
            extended(values, (("band", 0), ("lane", 1)), 1, False),
            values,
            load_terms,
            reaction_rate,
        )
    defect = (
        load_terms
        + cross_sum(extended(values, (("band", 0), ("lane", 1)), 1, False))
        - (4.0 + reaction_rate) * values
    )
    coarse_load, coarse_mass = (block_means(defect) * RATIO, block_means(reaction_rate) * RATIO)
    coarse_values = 0.8 * coarse_load / (4.0 + coarse_mass)
    depth = 2
    load_mass = padded_2(
        jnp.concatenate([coarse_load, coarse_mass], axis=2), (("band", 0), ("lane", 1)), 2, False
    )
    wide_load, wide_mass = jnp.split(load_mass, 2, axis=2)
    place_y = (
        lax.axis_index("band") * coarse_load.shape[0]
        - depth
        + jnp.arange(coarse_load.shape[0] + 2 * depth)
    )
    place_x = (
        lax.axis_index("lane") * coarse_load.shape[1]
        - depth
        + jnp.arange(coarse_load.shape[1] + 2 * depth)
    )
    inside_y = (place_y >= 0) & (place_y < coarse_load.shape[0] * lax.axis_size("band"))
    inside_x = (place_x >= 0) & (place_x < coarse_load.shape[1] * lax.axis_size("lane"))
    inside = (inside_y[:, None] & inside_x[None, :])[:, :, None]
    for group in range((INNER - 1) // 2):
        wide_values = padded_2(coarse_values, (("band", 0), ("lane", 1)), 2, False)
        once = smooth_step(
            wide_values, strip_rim(wide_values), strip_rim(wide_load), strip_rim(wide_mass)
        )
        once = jnp.where(strip_rim(inside), once, 0.0)
        middle = strip_rim(once)
        coarse_values = smooth_step(once, middle, coarse_load, coarse_mass)
    values = values + spread_blocks(coarse_values)
    for sweep in range(AFTER):
        values = smooth_step(
            extended(values, (("band", 0), ("lane", 1)), 1, False),
            values,
            load_terms,
            reaction_rate,
        )
    solution = values
    remaining = (
        load_terms
        + cross_sum(extended(solution, (("band", 0), ("lane", 1)), 1, False))
        - (4.0 + reaction_rate) * solution
    )
    return (solution, remaining)


def solution(mesh):
    return jax.shard_map(
        body,
        mesh=mesh,
        in_specs=(P("band", "lane", None), P("band", "lane", None), P("band", "lane", None)),
        out_specs=(P("band", "lane", None), P("band", "lane", None)),
        check_vma=False,
    )
```

profile of v0, /device:TPU:109, one launch (start us, length us, event | category | flops | bytes accessed | tf_op | source)
XLA Modules:
  0.0 378.5 jit_solution(2018704563848098932)
XLA Ops:
  4.1 6.6 %collective-permute-start = (f32[1,64,256]{2,1,0:T(8,128)S(1)}, f32[1,64,256]{2,1,0:T(8,128)S(1)}, u32[]{:S(2)}, u32[]{:S(2)}) collective-permute-start(f32[1,64,256]{2,1,0:T(8,128)S(1)} %get-tuple-element.32), channel_id=1, source_target_pairs={{0,8},{8,16},{16,24},{24,32},{32,40},{40,48},{48,56},{56,64},{64,7... | collective-permute-start | bytes 196616 | tf_op jit(solution)/shard_map/ppermute | solution.py:19
  23.0 6.5 %fusion.59 = f32[64,64,256]{2,1,0:T(8,128)S(1)} fusion(f32[64,64,256]{2,1,0:T(8,128)} %param.4, f32[64,64,256]{2,1,0:T(8,128)S(1)} %copy-done.2, f32[66,64,256]{2,1,0:T(8,128)S(1)} %constant_dynamic-update-slice_fusion, f32[64,1,256]{2,1,0:T(1,128)S(1)} %collective-permute-done.3, f32[64,1,256]{2,1,0:T(1,128)S(1)} %collective-permute-done.2, ...), kind=kLoop, calls=%fused_computation.108 | loop fusion | flops 20971520 | bytes 21364736 | tf_op jit(solution)/shard_map/add | solution.py:59
  40.9 7.2 %collective-permute-done.5 = f32[1,64,256]{2,1,0:T(8,128)S(1)} collective-permute-done((f32[1,64,256]{2,1,0:T(8,128)S(1)}, f32[1,64,256]{2,1,0:T(8,128)S(1)}, u32[]{:S(2)}, u32[]{:S(2)}) %collective-permute-start.5) | collective-permute-done | bytes 65568 | tf_op jit(solution)/shard_map/ppermute | solution.py:19
  48.0 5.7 %fusion.50 = f32[64,64,256]{2,1,0:T(8,128)S(1)} fusion(f32[64,64,256]{2,1,0:T(8,128)S(1)} %fusion.59, f32[64,64,256]{2,1,0:T(8,128)S(1)} %copy-done.2, f32[64,1,256]{2,1,0:T(1,128)S(1)} %collective-permute-done.7, f32[1,64,256]{2,1,0:T(8,128)S(1)} %collective-permute-done.5, f32[1,64,256]{2,1,0:T(8,128)S(1)} %collective-permute-done.4, ...), kind=kLoop, calls=%fused_computation.91 | loop fusion | flops 25165824 | bytes 17039360 | tf_op jit(solution)/shard_map/add | solution.py:59
  64.5 7.2 %collective-permute-done.9 = f32[1,64,256]{2,1,0:T(8,128)S(1)} collective-permute-done((f32[1,64,256]{2,1,0:T(8,128)S(1)}, f32[1,64,256]{2,1,0:T(8,128)S(1)}, u32[]{:S(2)}, u32[]{:S(2)}) %collective-permute-start.9) | collective-permute-done | bytes 65568 | tf_op jit(solution)/shard_map/ppermute | solution.py:19
  71.7 5.7 %fusion.40 = f32[64,64,256]{2,1,0:T(8,128)S(1)} fusion(f32[64,64,256]{2,1,0:T(8,128)S(1)} %fusion.50, f32[64,64,256]{2,1,0:T(8,128)S(1)} %copy-done.2, f32[64,1,256]{2,1,0:T(1,128)S(1)} %collective-permute-done.11, f32[1,64,256]{2,1,0:T(8,128)S(1)} %collective-permute-done.9, f32[1,64,256]{2,1,0:T(8,128)S(1)} %collective-permute-done.8, ...), kind=kLoop, calls=%fused_computation.73 | loop fusion | flops 25165824 | bytes 17039360 | tf_op jit(solution)/shard_map/add | solution.py:59
  90.3 5.8 %reshape.32 = f32[32,2,32,2,256]{4,3,2,1,0:T(2,128)} reshape(f32[64,64,256]{2,1,0:T(8,128)} %param.5) | data formatting | bytes 8388608 | tf_op jit(solution)/shard_map/reshape | solution.py:65
  96.1 5.5 %reduce_sum.19 = f32[32,32,256]{2,1,0:T(8,128)S(1)} reduce(f32[32,2,32,2,256]{4,3,2,1,0:T(2,128)} %reshape.32, f32[]{:T(128)} %constant.13.clone.1), dimensions={1,3}, to_apply=%region_1.2 | reduce | flops 786432 | bytes 5242884 | tf_op jit(solution)/shard_map/reduce_sum | solution.py:68
  101.6 13.6 %fusion.30 = f32[64,64,256]{2,1,0:T(8,128)} fusion(f32[64,64,256]{2,1,0:T(8,128)} %param.3, f32[64,1,256]{2,1,0:T(1,128)S(1)} %collective-permute-done.15, f32[1,64,256]{2,1,0:T(8,128)S(1)} %collective-permute-done.13, f32[64,64,256]{2,1,0:T(8,128)} %copy-done.4, f32[1,64,256]{2,1,0:T(8,128)S(1)} %collective-permute-done.12, ...), kind=kLoop, calls=%fused_computation.55 | loop fusion | flops 22020096 | bytes 17039360 | tf_op jit(solution)/shard_map/sub | solution.py:91
  115.2 5.8 %reshape.31 = f32[32,2,32,2,256]{4,3,2,1,0:T(2,128)} reshape(f32[64,64,256]{2,1,0:T(8,128)} %fusion.30) | data formatting | bytes 8388608 | tf_op jit(solution)/shard_map/reshape | solution.py:65
  121.0 5.5 %reduce_sum.18 = f32[32,32,256]{2,1,0:T(8,128)S(1)} reduce(f32[32,2,32,2,256]{4,3,2,1,0:T(2,128)} %reshape.31, f32[]{:T(128)} %constant.13.clone.1), dimensions={1,3}, to_apply=%region_0.1 | reduce | flops 786432 | bytes 5242884 | tf_op jit(solution)/shard_map/reduce_sum | solution.py:68
  126.9 7.3 %collective-permute-start.16 = (f32[2,32,256]{2,1,0:T(8,128)S(1)}, f32[2,32,256]{2,1,0:T(8,128)S(1)}, u32[]{:S(2)}, u32[]{:S(2)}) collective-permute-start(f32[2,32,256]{2,1,0:T(8,128)S(1)} %get-tuple-element.62), channel_id=1, source_target_pairs={{0,8},{8,16},{16,24},{24,32},{32,40},{40,48},{48,56},{56,64},{64,7... | collective-permute-start | bytes 196616 | tf_op jit(solution)/shard_map/ppermute | solution.py:38
  136.2 7.3 %collective-permute-start.20 = (f32[2,32,512]{2,1,0:T(8,128)S(1)}, f32[2,32,512]{2,1,0:T(8,128)S(1)}, u32[]{:S(2)}, u32[]{:S(2)}) collective-permute-start(f32[2,32,512]{2,1,0:T(8,128)S(1)} %get-tuple-element.35), channel_id=1, source_target_pairs={{0,8},{8,16},{16,24},{24,32},{32,40},{40,48},{48,56},{56,64},{64,7... | collective-permute-start | bytes 393224 | tf_op jit(solution)/shard_map/ppermute | solution.py:38
  166.8 7.4 %collective-permute-start.24 = (f32[2,32,256]{2,1,0:T(8,128)S(1)}, f32[2,32,256]{2,1,0:T(8,128)S(1)}, u32[]{:S(2)}, u32[]{:S(2)}) collective-permute-start(f32[2,32,256]{2,1,0:T(8,128)S(1)} %get-tuple-element.57), channel_id=1, source_target_pairs={{0,8},{8,16},{16,24},{24,32},{32,40},{40,48},{48,56},{56,64},{64,7... | collective-permute-start | bytes 196616 | tf_op jit(solution)/shard_map/ppermute | solution.py:38
  176.1 7.3 %collective-permute-done.25 = f32[2,32,256]{2,1,0:T(8,128)S(1)} collective-permute-done((f32[2,32,256]{2,1,0:T(8,128)S(1)}, f32[2,32,256]{2,1,0:T(8,128)S(1)}, u32[]{:S(2)}, u32[]{:S(2)}) %collective-permute-start.25) | collective-permute-done | bytes 65568 | tf_op jit(solution)/shard_map/ppermute | solution.py:41
  183.4 5.1 %collective-permute-start.26 = (f32[36,2,256]{2,1,0:T(2,128)S(1)}, f32[36,2,256]{2,1,0:T(2,128)S(1)}, u32[]{:S(2)}, u32[]{:S(2)}) collective-permute-start(f32[36,2,256]{2,1,0:T(2,128)S(1)} %get-tuple-element.45), channel_id=1, source_target_pairs={{0,1},{1,2},{2,3},{3,4},{4,5},{5,6},{6,7},{8,9},{9,10},{10,11},{11... | collective-permute-start | bytes 221192 | tf_op jit(solution)/shard_map/ppermute | solution.py:38
  201.6 7.3 %collective-permute-done.29 = f32[2,32,256]{2,1,0:T(8,128)S(1)} collective-permute-done((f32[2,32,256]{2,1,0:T(8,128)S(1)}, f32[2,32,256]{2,1,0:T(8,128)S(1)}, u32[]{:S(2)}, u32[]{:S(2)}) %collective-permute-start.29) | collective-permute-done | bytes 65568 | tf_op jit(solution)/shard_map/ppermute | solution.py:41
  224.4 7.3 %collective-permute-done.33 = f32[2,32,256]{2,1,0:T(8,128)S(1)} collective-permute-done((f32[2,32,256]{2,1,0:T(8,128)S(1)}, f32[2,32,256]{2,1,0:T(8,128)S(1)}, u32[]{:S(2)}, u32[]{:S(2)}) %collective-permute-start.33) | collective-permute-done | bytes 65568 | tf_op jit(solution)/shard_map/ppermute | solution.py:41
  231.7 5.1 %collective-permute-start.34 = (f32[36,2,256]{2,1,0:T(2,128)S(1)}, f32[36,2,256]{2,1,0:T(2,128)S(1)}, u32[]{:S(2)}, u32[]{:S(2)}) collective-permute-start(f32[36,2,256]{2,1,0:T(2,128)S(1)} %get-tuple-element.41), channel_id=1, source_target_pairs={{0,1},{1,2},{2,3},{3,4},{4,5},{5,6},{6,7},{8,9},{9,10},{10,11},{11... | collective-permute-start | bytes 221192 | tf_op jit(solution)/shard_map/ppermute | solution.py:38
  249.9 7.3 %collective-permute-done.37 = f32[2,32,256]{2,1,0:T(8,128)S(1)} collective-permute-done((f32[2,32,256]{2,1,0:T(8,128)S(1)}, f32[2,32,256]{2,1,0:T(8,128)S(1)}, u32[]{:S(2)}, u32[]{:S(2)}) %collective-permute-start.37) | collective-permute-done | bytes 65568 | tf_op jit(solution)/shard_map/ppermute | solution.py:41
  272.9 7.3 %collective-permute-done.41 = f32[2,32,256]{2,1,0:T(8,128)S(1)} collective-permute-done((f32[2,32,256]{2,1,0:T(8,128)S(1)}, f32[2,32,256]{2,1,0:T(8,128)S(1)}, u32[]{:S(2)}, u32[]{:S(2)}) %collective-permute-start.41) | collective-permute-done | bytes 65568 | tf_op jit(solution)/shard_map/ppermute | solution.py:41
  282.7 4.7 %collective-permute-start.43 = (f32[36,2,256]{2,1,0:T(2,128)S(1)}, f32[36,2,256]{2,1,0:T(2,128)S(1)}, u32[]{:S(2)}, u32[]{:S(2)}) collective-permute-start(f32[36,2,256]{2,1,0:T(2,128)S(1)} %get-tuple-element.38), channel_id=1, source_target_pairs={{1,0},{2,1},{3,2},{4,3},{5,4},{6,5},{7,6},{9,8},{10,9},{11,10},{12... | collective-permute-start | bytes 221192 | tf_op jit(solution)/shard_map/ppermute | solution.py:41
  295.1 6.1 %reshape.34 = f32[64,64,256]{2,1,0:T(8,128)} reshape(f32[64,32,2,256]{3,2,1,0:T(2,128)} %broadcast_in_dim.47) | data formatting | bytes 8388608 | tf_op jit(solution)/shard_map/reshape | solution.py:72
  301.2 4.4 %add.461 = f32[64,64,256]{2,1,0:T(8,128)S(1)} add(f32[64,64,256]{2,1,0:T(8,128)} %copy-done.4, f32[64,64,256]{2,1,0:T(8,128)} %reshape.34) | non-fusion elementwise | flops 1048576 | bytes 12582912 | tf_op jit(solution)/shard_map/add | solution.py:123
  307.9 4.5 %collective-permute-start.47 = (f32[64,1,256]{2,1,0:T(1,128)S(1)}, f32[64,1,256]{2,1,0:T(1,128)S(1)}, u32[]{:S(2)}, u32[]{:S(2)}) collective-permute-start(f32[64,1,256]{2,1,0:T(1,128)S(1)} %get-tuple-element.14), channel_id=1, source_target_pairs={{1,0},{2,1},{3,2},{4,3},{5,4},{6,5},{7,6},{9,8},{10,9},{11,10},{12... | collective-permute-start | bytes 196616 | tf_op jit(solution)/shard_map/ppermute | solution.py:19
  317.0 7.2 %collective-permute-done.45 = f32[1,64,256]{2,1,0:T(8,128)S(1)} collective-permute-done((f32[1,64,256]{2,1,0:T(8,128)S(1)}, f32[1,64,256]{2,1,0:T(8,128)S(1)}, u32[]{:S(2)}, u32[]{:S(2)}) %collective-permute-start.45) | collective-permute-done | bytes 65568 | tf_op jit(solution)/shard_map/ppermute | solution.py:19
  324.3 5.7 %fusion.23 = f32[64,64,256]{2,1,0:T(8,128)S(1)} fusion(f32[64,64,256]{2,1,0:T(8,128)S(1)} %add.461, f32[64,64,256]{2,1,0:T(8,128)S(1)} %copy-done.3, f32[64,1,256]{2,1,0:T(1,128)S(1)} %collective-permute-done.47, f32[1,64,256]{2,1,0:T(8,128)S(1)} %collective-permute-done.45, f32[1,64,256]{2,1,0:T(8,128)S(1)} %collective-permute-done.44, ...), kind=kLoop, calls=%fused_computation.40 | loop fusion | flops 25165824 | bytes 17039360 | tf_op jit(solution)/shard_map/add | solution.py:59
  332.0 4.3 %collective-permute-start.51 = (f32[64,1,256]{2,1,0:T(1,128)S(1)}, f32[64,1,256]{2,1,0:T(1,128)S(1)}, u32[]{:S(2)}, u32[]{:S(2)}) collective-permute-start(f32[64,1,256]{2,1,0:T(1,128)S(1)} %get-tuple-element.10), channel_id=1, source_target_pairs={{1,0},{2,1},{3,2},{4,3},{5,4},{6,5},{7,6},{9,8},{10,9},{11,10},{12... | collective-permute-start | bytes 196616 | tf_op jit(solution)/shard_map/ppermute | solution.py:19
  340.7 7.2 %collective-permute-done.49 = f32[1,64,256]{2,1,0:T(8,128)S(1)} collective-permute-done((f32[1,64,256]{2,1,0:T(8,128)S(1)}, f32[1,64,256]{2,1,0:T(8,128)S(1)}, u32[]{:S(2)}, u32[]{:S(2)}) %collective-permute-start.49) | collective-permute-done | bytes 65568 | tf_op jit(solution)/shard_map/ppermute | solution.py:19
  347.9 5.7 %fusion.13 = f32[64,64,256]{2,1,0:T(8,128)S(1)} fusion(f32[64,64,256]{2,1,0:T(8,128)S(1)} %fusion.23, f32[64,64,256]{2,1,0:T(8,128)S(1)} %copy-done.3, f32[64,1,256]{2,1,0:T(1,128)S(1)} %collective-permute-done.51, f32[1,64,256]{2,1,0:T(8,128)S(1)} %collective-permute-done.49, f32[1,64,256]{2,1,0:T(8,128)S(1)} %collective-permute-done.48, ...), kind=kLoop, calls=%fused_computation.22 | loop fusion | flops 25165824 | bytes 17039360 | tf_op jit(solution)/shard_map/add | solution.py:59
  364.4 7.2 %collective-permute-done.53 = f32[1,64,256]{2,1,0:T(8,128)S(1)} collective-permute-done((f32[1,64,256]{2,1,0:T(8,128)S(1)}, f32[1,64,256]{2,1,0:T(8,128)S(1)}, u32[]{:S(2)}, u32[]{:S(2)}) %collective-permute-start.53) | collective-permute-done | bytes 65568 | tf_op jit(solution)/shard_map/ppermute | solution.py:19
  371.6 6.4 %fusion.3 = f32[64,64,256]{2,1,0:T(8,128)} fusion(f32[64,64,256]{2,1,0:T(8,128)S(1)} %copy-done.3, f32[64,1,256]{2,1,0:T(1,128)S(1)} %collective-permute-done.55, f32[1,64,256]{2,1,0:T(8,128)S(1)} %collective-permute-done.53, f32[64,64,256]{2,1,0:T(8,128)S(1)} %fusion.13, f32[1,64,256]{2,1,0:T(8,128)S(1)} %collective-permute-done.52, ...), kind=kLoop, calls=%fused_computation.4 | loop fusion | flops 22020096 | bytes 17039360 | tf_op jit(solution)/shard_map/sub | solution.py:133
  (162 shorter events, 169.2 us)
Async XLA Ops:
  1.5 19.9 %collective-permute-start.1 = (f32[1,64,256]{2,1,0:T(8,128)S(1)}, f32[1,64,256]{2,1,0:T(8,128)S(1)}, u32[]{:S(2)}, u32[]{:S(2)}) collective-permute-start(f32[1,64,256]{2,1,0:T(8,128)S(1)} %get-tuple-element.31), channel_id=1, source_target_pairs={{8,0},{16,8},{24,16},{32,24},{40,32},{48,40},{56,48},{64,56},{72,6... | collective-permute-start | bytes 196616 | tf_op jit(solution)/shard_map/ppermute | solution.py:19
  4.1 14.1 %collective-permute-start = (f32[1,64,256]{2,1,0:T(8,128)S(1)}, f32[1,64,256]{2,1,0:T(8,128)S(1)}, u32[]{:S(2)}, u32[]{:S(2)}) collective-permute-start(f32[1,64,256]{2,1,0:T(8,128)S(1)} %get-tuple-element.32), channel_id=1, source_target_pairs={{0,8},{8,16},{16,24},{24,32},{32,40},{40,48},{48,56},{56,64},{64,7... | collective-permute-start | bytes 196616 | tf_op jit(solution)/shard_map/ppermute | solution.py:19
  12.0 9.4 %collective-permute-start.2 = (f32[64,1,256]{2,1,0:T(1,128)S(1)}, f32[64,1,256]{2,1,0:T(1,128)S(1)}, u32[]{:S(2)}, u32[]{:S(2)}) collective-permute-start(f32[64,1,256]{2,1,0:T(1,128)S(1)} %get-tuple-element.29), channel_id=1, source_target_pairs={{0,1},{1,2},{2,3},{3,4},{4,5},{5,6},{6,7},{8,9},{9,10},{10,11},{11... | collective-permute-start | bytes 196616 | tf_op jit(solution)/shard_map/ppermute | solution.py:19
  29.6 11.3 %collective-permute-start.6 = (f32[64,1,256]{2,1,0:T(1,128)S(1)}, f32[64,1,256]{2,1,0:T(1,128)S(1)}, u32[]{:S(2)}, u32[]{:S(2)}) collective-permute-start(f32[64,1,256]{2,1,0:T(1,128)S(1)} %get-tuple-element.25), channel_id=1, source_target_pairs={{0,1},{1,2},{2,3},{3,4},{4,5},{5,6},{6,7},{8,9},{9,10},{10,11},{11... | collective-permute-start | bytes 196616 | tf_op jit(solution)/shard_map/ppermute | solution.py:19
  31.6 9.2 %collective-permute-start.7 = (f32[64,1,256]{2,1,0:T(1,128)S(1)}, f32[64,1,256]{2,1,0:T(1,128)S(1)}, u32[]{:S(2)}, u32[]{:S(2)}) collective-permute-start(f32[64,1,256]{2,1,0:T(1,128)S(1)} %get-tuple-element.26), channel_id=1, source_target_pairs={{1,0},{2,1},{3,2},{4,3},{5,4},{6,5},{7,6},{9,8},{10,9},{11,10},{12... | collective-permute-start | bytes 196616 | tf_op jit(solution)/shard_map/ppermute | solution.py:19
  38.8 9.2 %collective-permute-start.5 = (f32[1,64,256]{2,1,0:T(8,128)S(1)}, f32[1,64,256]{2,1,0:T(8,128)S(1)}, u32[]{:S(2)}, u32[]{:S(2)}) collective-permute-start(f32[1,64,256]{2,1,0:T(8,128)S(1)} %get-tuple-element.28), channel_id=1, source_target_pairs={{8,0},{16,8},{24,16},{32,24},{40,32},{48,40},{56,48},{64,56},{72,6... | collective-permute-start | bytes 196616 | tf_op jit(solution)/shard_map/ppermute | solution.py:19
  53.9 10.6 %collective-permute-start.10 = (f32[64,1,256]{2,1,0:T(1,128)S(1)}, f32[64,1,256]{2,1,0:T(1,128)S(1)}, u32[]{:S(2)}, u32[]{:S(2)}) collective-permute-start(f32[64,1,256]{2,1,0:T(1,128)S(1)} %get-tuple-element.21), channel_id=1, source_target_pairs={{0,1},{1,2},{2,3},{3,4},{4,5},{5,6},{6,7},{8,9},{9,10},{10,11},{11... | collective-permute-start | bytes 196616 | tf_op jit(solution)/shard_map/ppermute | solution.py:19
  62.5 9.2 %collective-permute-start.9 = (f32[1,64,256]{2,1,0:T(8,128)S(1)}, f32[1,64,256]{2,1,0:T(8,128)S(1)}, u32[]{:S(2)}, u32[]{:S(2)}) collective-permute-start(f32[1,64,256]{2,1,0:T(8,128)S(1)} %get-tuple-element.24), channel_id=1, source_target_pairs={{8,0},{16,8},{24,16},{32,24},{40,32},{48,40},{56,48},{64,56},{72,6... | collective-permute-start | bytes 196616 | tf_op jit(solution)/shard_map/ppermute | solution.py:19
  79.4 22.1 %collective-permute-start.14 = (f32[64,1,256]{2,1,0:T(1,128)S(1)}, f32[64,1,256]{2,1,0:T(1,128)S(1)}, u32[]{:S(2)}, u32[]{:S(2)}) collective-permute-start(f32[64,1,256]{2,1,0:T(1,128)S(1)} %get-tuple-element.17), channel_id=1, source_target_pairs={{0,1},{1,2},{2,3},{3,4},{4,5},{5,6},{6,7},{8,9},{9,10},{10,11},{11... | collective-permute-start | bytes 196616 | tf_op jit(solution)/shard_map/ppermute | solution.py:19
  81.8 19.8 %collective-permute-start.15 = (f32[64,1,256]{2,1,0:T(1,128)S(1)}, f32[64,1,256]{2,1,0:T(1,128)S(1)}, u32[]{:S(2)}, u32[]{:S(2)}) collective-permute-start(f32[64,1,256]{2,1,0:T(1,128)S(1)} %get-tuple-element.18), channel_id=1, source_target_pairs={{1,0},{2,1},{3,2},{4,3},{5,4},{6,5},{7,6},{9,8},{10,9},{11,10},{12... | collective-permute-start | bytes 196616 | tf_op jit(solution)/shard_map/ppermute | solution.py:19
  85.6 15.9 %collective-permute-start.12 = (f32[1,64,256]{2,1,0:T(8,128)S(1)}, f32[1,64,256]{2,1,0:T(8,128)S(1)}, u32[]{:S(2)}, u32[]{:S(2)}) collective-permute-start(f32[1,64,256]{2,1,0:T(8,128)S(1)} %get-tuple-element.19), channel_id=1, source_target_pairs={{0,8},{8,16},{16,24},{24,32},{32,40},{40,48},{48,56},{56,64},{64,7... | collective-permute-start | bytes 196616 | tf_op jit(solution)/shard_map/ppermute | solution.py:19
  88.1 13.5 %collective-permute-start.13 = (f32[1,64,256]{2,1,0:T(8,128)S(1)}, f32[1,64,256]{2,1,0:T(8,128)S(1)}, u32[]{:S(2)}, u32[]{:S(2)}) collective-permute-start(f32[1,64,256]{2,1,0:T(8,128)S(1)} %get-tuple-element.20), channel_id=1, source_target_pairs={{8,0},{16,8},{24,16},{32,24},{40,32},{48,40},{56,48},{64,56},{72,6... | collective-permute-start | bytes 196616 | tf_op jit(solution)/shard_map/ppermute | solution.py:19
  126.9 18.5 %collective-permute-start.16 = (f32[2,32,256]{2,1,0:T(8,128)S(1)}, f32[2,32,256]{2,1,0:T(8,128)S(1)}, u32[]{:S(2)}, u32[]{:S(2)}) collective-permute-start(f32[2,32,256]{2,1,0:T(8,128)S(1)} %get-tuple-element.62), channel_id=1, source_target_pairs={{0,8},{8,16},{16,24},{24,32},{32,40},{40,48},{48,56},{56,64},{64,7... | collective-permute-start | bytes 196616 | tf_op jit(solution)/shard_map/ppermute | solution.py:38
  134.2 11.2 %collective-permute-start.17 = (f32[2,32,256]{2,1,0:T(8,128)S(1)}, f32[2,32,256]{2,1,0:T(8,128)S(1)}, u32[]{:S(2)}, u32[]{:S(2)}) collective-permute-start(f32[2,32,256]{2,1,0:T(8,128)S(1)} %get-tuple-element.63), channel_id=1, source_target_pairs={{8,0},{16,8},{24,16},{32,24},{40,32},{48,40},{56,48},{64,56},{72,6... | collective-permute-start | bytes 196616 | tf_op jit(solution)/shard_map/ppermute | solution.py:41
  136.2 15.5 %collective-permute-start.20 = (f32[2,32,512]{2,1,0:T(8,128)S(1)}, f32[2,32,512]{2,1,0:T(8,128)S(1)}, u32[]{:S(2)}, u32[]{:S(2)}) collective-permute-start(f32[2,32,512]{2,1,0:T(8,128)S(1)} %get-tuple-element.35), channel_id=1, source_target_pairs={{0,8},{8,16},{16,24},{24,32},{32,40},{40,48},{48,56},{56,64},{64,7... | collective-permute-start | bytes 393224 | tf_op jit(solution)/shard_map/ppermute | solution.py:38
  143.4 9.9 %collective-permute-start.21 = (f32[2,32,512]{2,1,0:T(8,128)S(1)}, f32[2,32,512]{2,1,0:T(8,128)S(1)}, u32[]{:S(2)}, u32[]{:S(2)}) collective-permute-start(f32[2,32,512]{2,1,0:T(8,128)S(1)} %get-tuple-element.36), channel_id=1, source_target_pairs={{8,0},{16,8},{24,16},{32,24},{40,32},{48,40},{56,48},{64,56},{72,6... | collective-permute-start | bytes 393224 | tf_op jit(solution)/shard_map/ppermute | solution.py:41
  145.5 14.4 %collective-permute-start.18 = (f32[36,2,256]{2,1,0:T(2,128)S(1)}, f32[36,2,256]{2,1,0:T(2,128)S(1)}, u32[]{:S(2)}, u32[]{:S(2)}) collective-permute-start(f32[36,2,256]{2,1,0:T(2,128)S(1)} %get-tuple-element.47), channel_id=1, source_target_pairs={{0,1},{1,2},{2,3},{3,4},{4,5},{5,6},{6,7},{8,9},{9,10},{10,11},{11... | collective-permute-start | bytes 221192 | tf_op jit(solution)/shard_map/ppermute | solution.py:38
  147.9 12.0 %collective-permute-start.19 = (f32[36,2,256]{2,1,0:T(2,128)S(1)}, f32[36,2,256]{2,1,0:T(2,128)S(1)}, u32[]{:S(2)}, u32[]{:S(2)}) collective-permute-start(f32[36,2,256]{2,1,0:T(2,128)S(1)} %get-tuple-element.48), channel_id=1, source_target_pairs={{1,0},{2,1},{3,2},{4,3},{5,4},{6,5},{7,6},{9,8},{10,9},{11,10},{12... | collective-permute-start | bytes 221192 | tf_op jit(solution)/shard_map/ppermute | solution.py:41
  166.8 9.3 %collective-permute-start.24 = (f32[2,32,256]{2,1,0:T(8,128)S(1)}, f32[2,32,256]{2,1,0:T(8,128)S(1)}, u32[]{:S(2)}, u32[]{:S(2)}) collective-permute-start(f32[2,32,256]{2,1,0:T(8,128)S(1)} %get-tuple-element.57), channel_id=1, source_target_pairs={{0,8},{8,16},{16,24},{24,32},{32,40},{40,48},{48,56},{56,64},{64,7... | collective-permute-start | bytes 196616 | tf_op jit(solution)/shard_map/ppermute | solution.py:38
  174.1 9.2 %collective-permute-start.25 = (f32[2,32,256]{2,1,0:T(8,128)S(1)}, f32[2,32,256]{2,1,0:T(8,128)S(1)}, u32[]{:S(2)}, u32[]{:S(2)}) collective-permute-start(f32[2,32,256]{2,1,0:T(8,128)S(1)} %get-tuple-element.58), channel_id=1, source_target_pairs={{8,0},{16,8},{24,16},{32,24},{40,32},{48,40},{56,48},{64,56},{72,6... | collective-permute-start | bytes 196616 | tf_op jit(solution)/shard_map/ppermute | solution.py:41
  199.7 9.2 %collective-permute-start.29 = (f32[2,32,256]{2,1,0:T(8,128)S(1)}, f32[2,32,256]{2,1,0:T(8,128)S(1)}, u32[]{:S(2)}, u32[]{:S(2)}) collective-permute-start(f32[2,32,256]{2,1,0:T(8,128)S(1)} %get-tuple-element.56), channel_id=1, source_target_pairs={{8,0},{16,8},{24,16},{32,24},{40,32},{48,40},{56,48},{64,56},{72,6... | collective-permute-start | bytes 196616 | tf_op jit(solution)/shard_map/ppermute | solution.py:41
  222.4 9.2 %collective-permute-start.33 = (f32[2,32,256]{2,1,0:T(8,128)S(1)}, f32[2,32,256]{2,1,0:T(8,128)S(1)}, u32[]{:S(2)}, u32[]{:S(2)}) collective-permute-start(f32[2,32,256]{2,1,0:T(8,128)S(1)} %get-tuple-element.54), channel_id=1, source_target_pairs={{8,0},{16,8},{24,16},{32,24},{40,32},{48,40},{56,48},{64,56},{72,6... | collective-permute-start | bytes 196616 | tf_op jit(solution)/shard_map/ppermute | solution.py:41
  248.0 9.2 %collective-permute-start.37 = (f32[2,32,256]{2,1,0:T(8,128)S(1)}, f32[2,32,256]{2,1,0:T(8,128)S(1)}, u32[]{:S(2)}, u32[]{:S(2)}) collective-permute-start(f32[2,32,256]{2,1,0:T(8,128)S(1)} %get-tuple-element.52), channel_id=1, source_target_pairs={{8,0},{16,8},{24,16},{32,24},{40,32},{48,40},{56,48},{64,56},{72,6... | collective-permute-start | bytes 196616 | tf_op jit(solution)/shard_map/ppermute | solution.py:41
  270.9 9.2 %collective-permute-start.41 = (f32[2,32,256]{2,1,0:T(8,128)S(1)}, f32[2,32,256]{2,1,0:T(8,128)S(1)}, u32[]{:S(2)}, u32[]{:S(2)}) collective-permute-start(f32[2,32,256]{2,1,0:T(8,128)S(1)} %get-tuple-element.50), channel_id=1, source_target_pairs={{8,0},{16,8},{24,16},{32,24},{40,32},{48,40},{56,48},{64,56},{72,6... | collective-permute-start | bytes 196616 | tf_op jit(solution)/shard_map/ppermute | solution.py:41
  305.7 11.3 %collective-permute-start.46 = (f32[64,1,256]{2,1,0:T(1,128)S(1)}, f32[64,1,256]{2,1,0:T(1,128)S(1)}, u32[]{:S(2)}, u32[]{:S(2)}) collective-permute-start(f32[64,1,256]{2,1,0:T(1,128)S(1)} %get-tuple-element.13), channel_id=1, source_target_pairs={{0,1},{1,2},{2,3},{3,4},{4,5},{5,6},{6,7},{8,9},{9,10},{10,11},{11... | collective-permute-start | bytes 196616 | tf_op jit(solution)/shard_map/ppermute | solution.py:19
  307.9 9.2 %collective-permute-start.47 = (f32[64,1,256]{2,1,0:T(1,128)S(1)}, f32[64,1,256]{2,1,0:T(1,128)S(1)}, u32[]{:S(2)}, u32[]{:S(2)}) collective-permute-start(f32[64,1,256]{2,1,0:T(1,128)S(1)} %get-tuple-element.14), channel_id=1, source_target_pairs={{1,0},{2,1},{3,2},{4,3},{5,4},{6,5},{7,6},{9,8},{10,9},{11,10},{12... | collective-permute-start | bytes 196616 | tf_op jit(solution)/shard_map/ppermute | solution.py:19
  315.1 9.2 %collective-permute-start.45 = (f32[1,64,256]{2,1,0:T(8,128)S(1)}, f32[1,64,256]{2,1,0:T(8,128)S(1)}, u32[]{:S(2)}, u32[]{:S(2)}) collective-permute-start(f32[1,64,256]{2,1,0:T(8,128)S(1)} %get-tuple-element.16), channel_id=1, source_target_pairs={{8,0},{16,8},{24,16},{32,24},{40,32},{48,40},{56,48},{64,56},{72,6... | collective-permute-start | bytes 196616 | tf_op jit(solution)/shard_map/ppermute | solution.py:19
  330.1 10.6 %collective-permute-start.50 = (f32[64,1,256]{2,1,0:T(1,128)S(1)}, f32[64,1,256]{2,1,0:T(1,128)S(1)}, u32[]{:S(2)}, u32[]{:S(2)}) collective-permute-start(f32[64,1,256]{2,1,0:T(1,128)S(1)} %get-tuple-element.9), channel_id=1, source_target_pairs={{0,1},{1,2},{2,3},{3,4},{4,5},{5,6},{6,7},{8,9},{9,10},{10,11},{11... | collective-permute-start | bytes 196616 | tf_op jit(solution)/shard_map/ppermute | solution.py:19
  338.8 9.2 %collective-permute-start.49 = (f32[1,64,256]{2,1,0:T(8,128)S(1)}, f32[1,64,256]{2,1,0:T(8,128)S(1)}, u32[]{:S(2)}, u32[]{:S(2)}) collective-permute-start(f32[1,64,256]{2,1,0:T(8,128)S(1)} %get-tuple-element.12), channel_id=1, source_target_pairs={{8,0},{16,8},{24,16},{32,24},{40,32},{48,40},{56,48},{64,56},{72,6... | collective-permute-start | bytes 196616 | tf_op jit(solution)/shard_map/ppermute | solution.py:19
  353.8 10.6 %collective-permute-start.54 = (f32[64,1,256]{2,1,0:T(1,128)S(1)}, f32[64,1,256]{2,1,0:T(1,128)S(1)}, u32[]{:S(2)}, u32[]{:S(2)}) collective-permute-start(f32[64,1,256]{2,1,0:T(1,128)S(1)} %get-tuple-element.5), channel_id=1, source_target_pairs={{0,1},{1,2},{2,3},{3,4},{4,5},{5,6},{6,7},{8,9},{9,10},{10,11},{11... | collective-permute-start | bytes 196616 | tf_op jit(solution)/shard_map/ppermute | solution.py:19
  355.7 8.6 %collective-permute-start.55 = (f32[64,1,256]{2,1,0:T(1,128)S(1)}, f32[64,1,256]{2,1,0:T(1,128)S(1)}, u32[]{:S(2)}, u32[]{:S(2)}) collective-permute-start(f32[64,1,256]{2,1,0:T(1,128)S(1)} %get-tuple-element.6), channel_id=1, source_target_pairs={{1,0},{2,1},{3,2},{4,3},{5,4},{6,5},{7,6},{9,8},{10,9},{11,10},{12... | collective-permute-start | bytes 196616 | tf_op jit(solution)/shard_map/ppermute | solution.py:19
  362.4 9.2 %collective-permute-start.53 = (f32[1,64,256]{2,1,0:T(8,128)S(1)}, f32[1,64,256]{2,1,0:T(8,128)S(1)}, u32[]{:S(2)}, u32[]{:S(2)}) collective-permute-start(f32[1,64,256]{2,1,0:T(8,128)S(1)} %get-tuple-element.8), channel_id=1, source_target_pairs={{8,0},{16,8},{24,16},{32,24},{40,32},{48,40},{56,48},{64,56},{72,6... | collective-permute-start | bytes 196616 | tf_op jit(solution)/shard_map/ppermute | solution.py:19
  (30 other events, 221.2 us)
where the time goes:
time: 385 us; the launch traced here: 378 us
  starting transfers between devices  174 us (45%)
  waiting for transfers between devices  87.4 us (23%)
  other arithmetic  83.8 us (22%)
  local copies, waits for them, and re-layouts  31.1 us (8%)
    ppermute x14, starting transfers between devices, padded_2(): lax.ppermute(lax.slice_in_dim(block, block.shape[dim] - width, None, axis...  56.6 us
    ppermute x14, waiting for transfers between devices, padded_2(): lax.ppermute(lax.slice_in_dim(block, 0, width, axis=dim), axis, backward)  51 us
    ppermute x14, starting transfers between devices, extended(): lax.ppermute(leading, axis, [(b, a) for a, b in up])  42.2 us
    ppermute x14, starting transfers between devices, extended(): lax.ppermute(last, axis, up)  37.8 us
    ppermute x14, starting transfers between devices, padded_2(): lax.ppermute(lax.slice_in_dim(block, 0, width, axis=dim), axis, backward)  37.3 us
    ppermute x14, waiting for transfers between devices, extended(): lax.ppermute(leading, axis, [(b, a) for a, b in up])  36.1 us
    add x11, other arithmetic, smooth_step(): values + 0.8 * (load + cross_sum(padded) - (4.0 + mass_here) * values) /...  32.9 us
    sub x1, other arithmetic, body(): load_terms + cross_sum(extended(values, (('band', 0), ('lane', 1)), 1, Fa...  13.6 us
  transfers between devices with their start and end apart: 56, of which 18 were waited for; matrix products, arithmetic and copies ran while one was open for 4% of the time, Pallas kernels for 0%

commit v1 on v0

v1 whole, which is shorter than its diff:
```python
import functools

import jax
import jax.numpy as jnp
from jax import lax
from jax.experimental import pallas as pl
from jax.experimental.pallas import tpu as pltpu
from jax.sharding import PartitionSpec as P

LANES = 128
CHAINS = 1
INNER = 13
FINE = 4
TILE = 8
DEEP = 8
SECOND = 6
FIRST_SWEEPS = DEEP + 1
LAST_SWEEPS = INNER - FIRST_SWEEPS


def swaps(count, first):
    pairs = []
    for i in range(first, count - 1, 2):
        pairs += [(i, i + 1), (i + 1, i)]
    return pairs


def swap(axis, even, odd):
    count = lax.axis_size(axis)
    return (
        lax.ppermute(even, axis, swaps(count, 0)),
        lax.ppermute(odd, axis, swaps(count, 1)),
    )


def placement():
    words = []
    for axis in ("band", "lane"):
        at, count = lax.axis_index(axis), lax.axis_size(axis)
        words += [at % 2 == 0, at > 0, at < count - 1]
    return jnp.stack([w.astype(jnp.int32) for w in words])


def roll(value, shift, axis):
    return pltpu.roll(value, shift % value.shape[axis], axis)


def sublane(value):
    return lax.broadcasted_iota(jnp.int32, value.shape, value.ndim - 2)


def by_side(even, got_even, got_odd):
    low = jnp.where(even, got_odd, got_even)
    high = jnp.where(even, got_even, got_odd)
    return low, high


def weight(mass, inside):
    return jnp.where(inside, 0.8 / (4.0 + mass), 0.0)


def new_value(here, left, right, up, down, load, w):
    return 0.2 * here + w * (load + ((up + down) + (left + right)))


def lane_pack_kernel(
    place, u_first, f_first, m_first, u_last, f_last, m_last, got_e, got_o, even_ref, odd_ref
):
    even_b, low_b, high_b = place[0] == 1, place[1] == 1, place[2] == 1
    even_l = place[3] == 1
    rows = u_first.shape[0]

    def message(u_ref, f_ref, m_ref, tile, high):
        at = pl.ds(tile * TILE, TILE)
        low_rows, high_rows = by_side(even_b, got_e[:, at, :], got_o[:, at, :])
        zero = jnp.zeros((1,) + u_ref.shape[1:], jnp.float32)
        u = jnp.concatenate([low_rows[:4], u_ref[...], high_rows[:4]], axis=0)
        f = jnp.concatenate([zero, low_rows[4:7], f_ref[...], high_rows[4:7], zero], axis=0)
        m = jnp.concatenate([zero, low_rows[7:10], m_ref[...], high_rows[7:10], zero], axis=0)
        w = 0.8 / (4.0 + m)
        w = jnp.concatenate(
            [
                jnp.where(low_b, w[:4], 0.0),
                w[4 : 4 + rows],
                jnp.where(high_b, w[4 + rows :], 0.0),
            ],
            axis=0,
        )
        up = jnp.concatenate([zero, u[:-1]], axis=0)
        down = jnp.concatenate([u[1:], zero], axis=0)
        v = new_value(u, roll(u, 1, 1), roll(u, -1, 1), up, down, f, w)
        s = sublane(u)
        if high:
            return jnp.where(
                s >= 6, u, jnp.where(s >= 4, roll(v, -1, 1), jnp.where(s >= 2, roll(f, -4, 1), roll(m, -6, 1)))
            )
        return jnp.where(
            s < 2, u, jnp.where(s < 4, roll(v, 1, 1), jnp.where(s < 6, roll(f, 4, 1), roll(m, 6, 1)))
        )

    last_tile = got_e.shape[1] // TILE - 1
    low = message(u_first, f_first, m_first, 0, False)
    high = message(u_last, f_last, m_last, last_tile, True)
    even_ref[...] = jnp.where(even_l, high, low)
    odd_ref[...] = jnp.where(even_l, low, high)


def fine_fields(place, f_ref, m_ref, got_e, got_o, lane_e, lane_o, load, w):
    even_b, low_b, high_b = place[0] == 1, place[1] == 1, place[2] == 1
    even_l, low_l, high_l = place[3] == 1, place[4] == 1, place[5] == 1
    rows, columns = f_ref.shape[0], f_ref.shape[1]
    own = pl.ds(TILE, columns)

    def copy_row(r, _):
        load[FINE + r, own, :] = f_ref[r]
        w[FINE + r, own, :] = 0.8 / (4.0 + m_ref[r])
        return 0

    lax.fori_loop(0, rows, copy_row, 0, unroll=2)
    low_rows, high_rows = by_side(even_b, got_e[4:10], got_o[4:10])
    load[1:4, own, :] = low_rows[:3]
    w[1:4, own, :] = weight(low_rows[3:], low_b)
    load[pl.ds(FINE + rows, 3), own, :] = high_rows[:3]
    w[pl.ds(FINE + rows, 3), own, :] = weight(high_rows[3:], high_b)

    def lane_row(r, _):
        low, high = by_side(even_l, lane_e[r], lane_o[r])
        s = sublane(low)
        inside_row = ((r >= FINE) | low_b) & ((r < FINE + rows) | high_b)
        load[r, pl.ds(0, TILE), :] = roll(low, 4, 0)
        load[r, pl.ds(TILE + columns, TILE), :] = roll(high, -4, 0)
        w[r, pl.ds(0, TILE), :] = weight(roll(low, 6, 0), (s >= 6) & inside_row & low_l)
        w[r, pl.ds(TILE + columns, TILE), :] = weight(
            roll(high, -6, 0), (s < 2) & inside_row & high_l
        )
        return 0

    lax.fori_loop(0, rows + 2 * FINE, lane_row, 0, unroll=4)


def sweep(source, target, load, w, first, last):
    def row(r, carry):
        up, here = carry
        down = source[r + 1]
        target[r] = new_value(here, roll(here, 1, 0), roll(here, -1, 0), up, down, load[r], w[r])
        return here, down

    lax.fori_loop(first, last, row, (source[first - 1], source[first]), unroll=2)


def before_kernel(
    place, u_ref, f_ref, m_ref, got_e, got_o, lane_e, lane_o,
    v_ref, load_ref, mass_ref, a, b, load, w, pairs,
):
    even_b, even_l = place[0] == 1, place[3] == 1
    rows, columns = u_ref.shape[0], u_ref.shape[1]
    own, left, right = pl.ds(TILE, columns), pl.ds(0, TILE), pl.ds(TILE + columns, TILE)
    fine_fields(place, f_ref, m_ref, got_e, got_o, lane_e, lane_o, load, w)
    low_rows, high_rows = by_side(even_b, got_e[:4], got_o[:4])
    a[:4, own, :] = low_rows
    a[pl.ds(FINE + rows, 4), own, :] = high_rows

    def copy_row(r, _):
        a[FINE + r, own, :] = u_ref[r]
        return 0

    lax.fori_loop(0, rows, copy_row, 0, unroll=4)

    def lane_row(r, _):
        low, high = by_side(even_l, lane_e[r], lane_o[r])
        a[r, left, :] = low
        a[r, right, :] = high
        return 0

    lax.fori_loop(0, rows + 2 * FINE, lane_row, 0, unroll=4)
    end = rows + 2 * FINE
    sweep(a, b, load, w, 1, end - 1)

    def mend(r, _):
        low, high = by_side(even_l, lane_e[r], lane_o[r])
        s = sublane(low)
        b[r, left, :] = jnp.where(s == 7, b[r, left, :], roll(low, 1, 0))
        b[r, right, :] = jnp.where(s == 0, b[r, right, :], roll(high, -1, 0))
        return 0

    lax.fori_loop(1, end - 1, mend, 0, unroll=2)
    sweep(b, a, load, w, 2, end - 2)
    sweep(a, b, load, w, 3, end - 3)

    def defect_of(i, up, here, down):
        around = (up + down) + (roll(here, 1, 0) + roll(here, -1, 0))
        value = lax.slice_in_dim(load[FINE + i] + around, TILE, TILE + columns, axis=0)
        mine = lax.slice_in_dim(here, TILE, TILE + columns, axis=0)
        return mine, value - (4.0 + m_ref[i]) * mine

    even_columns, odd_columns = pl.ds(0, columns // 2, 2), pl.ds(1, columns // 2, 2)

    def restrict(k, carry):
        up, here = carry
        i = 2 * k
        middle, down = b[FINE + i + 1], b[FINE + i + 2]
        mine, first = defect_of(i, up, here, middle)
        v_ref[i] = mine
        mine, second = defect_of(i + 1, here, middle, down)
        v_ref[i + 1] = mine
        pairs[0, k] = first + second
        pairs[1, k] = m_ref[i] + m_ref[i + 1]
        load_ref[k] = 0.5 * (pairs[0, k, even_columns, :] + pairs[0, k, odd_columns, :])
        mass_ref[k] = 0.5 * (pairs[1, k, even_columns, :] + pairs[1, k, odd_columns, :])
        return middle, down

    lax.fori_loop(0, rows // 2, restrict, (b[FINE - 1], b[FINE]))


def coarse_pack_kernel(
    place, load_first, mass_first, v_first, load_last, mass_last, v_last, got_e, got_o,
    even_ref, odd_ref,
):
    even_b, even_l = place[0] == 1, place[3] == 1
    half = got_e.shape[1]
    zero = jnp.zeros((1, TILE, LANES), jnp.float32)

    def message(load_ref, mass_ref, v_ref, high):
        coarse_at = pl.ds(half - TILE if high else 0, TILE)
        low, top = by_side(even_b, got_e[: 2 * DEEP, coarse_at, :], got_o[: 2 * DEEP, coarse_at, :])
        load = jnp.concatenate([low[:DEEP], load_ref[...], top[:DEEP]], axis=0)
        mass = jnp.concatenate([low[DEEP:], mass_ref[...], top[DEEP:]], axis=0)
        fine_at = pl.ds(half - TILE if high else 0, TILE)
        rows_e = [got_e[2 * DEEP + 2 * i + (1 if high else 0), fine_at, :][None] for i in range(3)]
        rows_o = [got_o[2 * DEEP + 2 * i + (1 if high else 0), fine_at, :][None] for i in range(3)]
        low_v, top_v = by_side(
            even_b, jnp.concatenate(rows_e, axis=0), jnp.concatenate(rows_o, axis=0)
        )
        v = jnp.concatenate([zero, low_v, v_ref[...], top_v, zero], axis=0)
        split = v.shape[0] // 2
        s = sublane(v[:split])
        keep = s >= 4 if high else s < 4
        return jnp.concatenate([load, mass, jnp.where(keep, v[:split], roll(v[split:], 4, 1))], axis=0)

    low = message(load_first, mass_first, v_first, False)
    high = message(load_last, mass_last, v_last, True)
    even_ref[...] = jnp.where(even_l, high, low)
    odd_ref[...] = jnp.where(even_l, low, high)


def coarse_fields(place, load_ref, mass_ref, got_e, got_o, lane_e, lane_o, load, w):
    even_b, low_b, high_b = place[0] == 1, place[1] == 1, place[2] == 1
    even_l, low_l, high_l = place[3] == 1, place[4] == 1, place[5] == 1
    rows, columns = load_ref.shape[0], load_ref.shape[1]
    own = pl.ds(TILE, columns)

    def copy_row(r, _):
        load[DEEP + r, own, :] = load_ref[r]
        w[DEEP + r, own, :] = 0.8 / (4.0 + mass_ref[r])
        return 0

    lax.fori_loop(0, rows, copy_row, 0, unroll=4)
    low, high = by_side(even_b, got_e[: 2 * DEEP], got_o[: 2 * DEEP])
    load[:DEEP, own, :] = low[:DEEP]
    w[:DEEP, own, :] = weight(low[DEEP:], low_b)
    load[pl.ds(DEEP + rows, DEEP), own, :] = high[:DEEP]
    w[pl.ds(DEEP + rows, DEEP), own, :] = weight(high[DEEP:], high_b)
    total = rows + 2 * DEEP

    def lane_row(r, _):
        inside_row = ((r >= DEEP) | low_b) & ((r < DEEP + rows) | high_b)
        low, high = by_side(even_l, lane_e[r], lane_o[r])
        load[r, pl.ds(0, TILE), :] = low
        load[r, pl.ds(TILE + columns, TILE), :] = high
        low, high = by_side(even_l, lane_e[total + r], lane_o[total + r])
        w[r, pl.ds(0, TILE), :] = weight(low, inside_row & low_l)
        w[r, pl.ds(TILE + columns, TILE), :] = weight(high, inside_row & high_l)
        return 0

    lax.fori_loop(0, total, lane_row, 0, unroll=4)


def coarse_kernel(
    place, load_ref, mass_ref, got_e, got_o, lane_e, lane_o, x_ref, a, b, load, w
):
    rows, columns = load_ref.shape[0], load_ref.shape[1]
    coarse_fields(place, load_ref, mass_ref, got_e, got_o, lane_e, lane_o, load, w)
    total = rows + 2 * DEEP

    def first(r, _):
        a[r] = w[r] * load[r]
        return 0

    lax.fori_loop(0, total, first, 0, unroll=4)
    source, target = a, b
    for step in range(1, FIRST_SWEEPS):
        sweep(source, target, load, w, step, total - step)
        source, target = target, source

    def out(r, _):
        x_ref[r] = source[DEEP + r, pl.ds(TILE, columns), :]
        return 0

    lax.fori_loop(0, rows, out, 0, unroll=4)


def value_pack_kernel(place, x_first, x_last, got_e, got_o, even_ref, odd_ref):
    even_b, even_l = place[0] == 1, place[3] == 1
    last = got_e.shape[1] - TILE

    def message(x_ref, start):
        at = pl.ds(start, TILE)
        low, high = by_side(even_b, got_e[:, at, :], got_o[:, at, :])
        return jnp.concatenate([low, x_ref[...], high], axis=0)

    low, high = message(x_first, 0), message(x_last, last)
    even_ref[...] = jnp.where(even_l, high, low)
    odd_ref[...] = jnp.where(even_l, low, high)


def after_kernel(
    place, f_ref, m_ref, v_ref, load_ref, mass_ref, x_ref,
    fine_e, fine_o, fine_lane_e, fine_lane_o,
    coarse_e, coarse_o, coarse_lane_e, coarse_lane_o,
    value_e, value_o, value_lane_e, value_lane_o,
    *rest,
):
    u_ref, d_ref, a, b, load, w, x, y, coarse_load, coarse_w, spread = rest[-11:]
    even_b, even_l = place[0] == 1, place[3] == 1
    rows, columns = f_ref.shape[0], f_ref.shape[1]
    half_rows, half_columns = rows // 2, columns // 2
    coarse_fields(
        place, load_ref, mass_ref, coarse_e, coarse_o, coarse_lane_e, coarse_lane_o, coarse_load, coarse_w
    )
    own = pl.ds(TILE, half_columns)
    total = half_rows + 2 * DEEP
    low, high = by_side(even_b, value_e[...], value_o[...])
    x[DEEP - SECOND : DEEP, own, :] = low
    x[pl.ds(DEEP + half_rows, SECOND), own, :] = high

    def coarse_copy(r, _):
        x[DEEP + r, own, :] = x_ref[r]
        return 0

    lax.fori_loop(0, half_rows, coarse_copy, 0, unroll=4)

    def coarse_lane(r, _):
        low, high = by_side(even_l, value_lane_e[r], value_lane_o[r])
        x[DEEP - SECOND + r, pl.ds(0, TILE), :] = low
        x[DEEP - SECOND + r, pl.ds(TILE + half_columns, TILE), :] = high
        return 0

    lax.fori_loop(0, half_rows + 2 * SECOND, coarse_lane, 0, unroll=4)
    source, target = x, y
    for step in range(1, LAST_SWEEPS + 1):
        edge = DEEP - SECOND + step
        sweep(source, target, coarse_load, coarse_w, edge, total - edge)
        source, target = target, source

    fine_fields(place, f_ref, m_ref, fine_e, fine_o, fine_lane_e, fine_lane_o, load, w)

    fine_own, left, right = pl.ds(TILE, columns), pl.ds(0, TILE), pl.ds(TILE + columns, TILE)
    for i in range(3):
        for part in range(2):
            at = pl.ds(TILE + part * half_columns, half_columns)
            k = 2 * DEEP + 2 * i + part
            low, high = by_side(even_b, coarse_e[k], coarse_o[k])
            a[1 + i, at, :] = low
            a[FINE + rows + i, at, :] = high

    def fine_copy(r, _):
        a[FINE + r, fine_own, :] = v_ref[r]
        return 0

    lax.fori_loop(0, rows, fine_copy, 0, unroll=4)
    split = (rows + 2 * FINE) // 2

    def fine_lane(r, _):
        low, high = by_side(even_l, coarse_lane_e[2 * total + r], coarse_lane_o[2 * total + r])
        a[r, left, :] = low
        a[r, right, :] = high
        a[split + r, left, :] = roll(low, 4, 0)
        a[split + r, right, :] = roll(high, 4, 0)
        return 0

    lax.fori_loop(0, split, fine_lane, 0, unroll=4)

    wide = columns + 2 * TILE
    across = wide // 2
    skip = TILE - TILE // 2

    def correct(k, _):
        value = source[DEEP - 2 + k, pl.ds(skip, across), :]
        spread[k, pl.ds(0, across, 2), :] = value
        spread[k, pl.ds(1, across, 2), :] = value
        both = spread[k]
        a[2 * k] += both
        a[2 * k + 1] += both
        return 0

    lax.fori_loop(0, half_rows + 4, correct, 0, unroll=2)
    end = rows + 2 * FINE
    sweep(a, b, load, w, 2, end - 2)
    sweep(b, a, load, w, 3, end - 3)

    def remains(i, carry):
        up, here = carry
        down = a[FINE + i + 1]
        around = (up + down) + (roll(here, 1, 0) + roll(here, -1, 0))
        value = lax.slice_in_dim(load[FINE + i] + around, TILE, TILE + columns, axis=0)
        mine = lax.slice_in_dim(here, TILE, TILE + columns, axis=0)
        u_ref[i] = mine
        d_ref[i] = value - (4.0 + m_ref[i]) * mine
        return here, down

    lax.fori_loop(0, rows, remains, (a[FINE - 1], a[FINE]), unroll=2)


def call(kernel, outs, ins, args, lanes, scratch=(), aliases=None, interpret=False):
    def spec(entry):
        if entry is None:
            return pl.BlockSpec(memory_space=pl.ANY)
        shape, at, start = entry
        return pl.BlockSpec(shape + (LANES,), lambda i, at=at, start=start: at + (i + start,))

    return pl.pallas_call(
        kernel,
        grid=(lanes // LANES,),
        in_specs=[pl.BlockSpec(memory_space=pltpu.SMEM)] + [spec(e) for e in ins],
        out_specs=[spec(e) for e, _ in outs],
        out_shape=[jax.ShapeDtypeStruct(s, jnp.float32) for _, s in outs],
        scratch_shapes=[pltpu.VMEM(s + (LANES,), jnp.float32) for s in scratch],
        input_output_aliases=aliases or {},
        interpret=interpret,
        compiler_params=pltpu.CompilerParams(vmem_limit_bytes=60 * 1024 * 1024),
    )(*args)


def edge(value, even, depth):
    rows = value.shape[0]
    high = jnp.where(even, rows - depth, 0)
    low = jnp.where(even, 0, rows - depth)
    return (
        lax.dynamic_slice_in_dim(value, high, depth, axis=0),
        lax.dynamic_slice_in_dim(value, low, depth, axis=0),
    )


def joined(parts, even):
    strips = [edge(value, even, depth) for value, depth in parts]
    return tuple(jnp.concatenate([s[k] for s in strips], axis=0) for k in range(2))


def body(load_terms, start_values, reaction_rate, interpret=False):
    run = functools.partial(call, interpret=interpret)
    place = placement()
    even = lax.axis_index("band") % 2 == 0
    rows, columns, layers = load_terms.shape
    half_rows, half_columns = rows // 2, columns // 2
    lanes = layers // CHAINS
    blocks = lanes // LANES
    end = rows + 2 * FINE
    total = half_rows + 2 * DEEP
    wide = columns + 2 * TILE
    half_wide = half_columns + 2 * TILE
    last = columns // TILE - 1
    half_last = half_columns // TILE - 1
    outputs = ()
    for chain in range(CHAINS):
        start = chain * blocks

        def cut(value):
            return lax.slice_in_dim(value, chain * lanes, (chain + 1) * lanes, axis=2)

        u, f, m = start_values, load_terms, reaction_rate
        fine = swap("band", *joined([(cut(u), 4), (cut(f), 3), (cut(m), 3)], even))
        fine_spec = [((10, columns), (0, 0), 0)] * 2
        whole = ((rows, columns), (0, 0), start)
        first_tile, last_tile = ((rows, TILE), (0, 0), start), ((rows, TILE), (0, last), start)
        lane_spec = [((end, TILE), (0, 0), 0)] * 2
        fine_lane = run(
            lane_pack_kernel,
            [(e, (end, TILE, lanes)) for e in lane_spec],
            [first_tile] * 3 + [last_tile] * 3 + fine_spec,
            (place, u, f, m, u, f, m, *fine),
            lanes,
        )
        fine_lane = swap("lane", *fine_lane)
        coarse_block = ((half_rows, half_columns), (0, 0), 0)
        own_block = ((rows, columns), (0, 0), 0)
        v, load, mass = run(
            before_kernel,
            [
                (own_block, (rows, columns, lanes)),
                (coarse_block, (half_rows, half_columns, lanes)),
                (coarse_block, (half_rows, half_columns, lanes)),
            ],
            [whole] * 3 + fine_spec + lane_spec,
            (place, u, f, m, *fine, *fine_lane),
            lanes,
            scratch=[(end, wide)] * 4 + [(2, half_rows, columns)],
        )
        strips = joined([(load, DEEP), (mass, DEEP)], even)
        values = [s.reshape(6, half_columns, lanes) for s in edge(v, even, 3)]
        coarse = swap("band", *[jnp.concatenate([s, t], axis=0) for s, t in zip(strips, values)])
        coarse_spec = [((2 * DEEP + 6, half_columns), (0, 0), 0)] * 2
        lane_rows = 2 * total + end // 2
        coarse_lane_spec = [((lane_rows, TILE), (0, 0), 0)] * 2
        half_first = ((half_rows, TILE), (0, 0), 0)
        half_last_tile = ((half_rows, TILE), (0, half_last), 0)
        coarse_lane = run(
            coarse_pack_kernel,
            [(e, (lane_rows, TILE, lanes)) for e in coarse_lane_spec],
            [half_first, half_first, ((rows, TILE), (0, 0), 0)]
            + [half_last_tile, half_last_tile, ((rows, TILE), (0, last), 0)]
            + coarse_spec,
            (place, load, mass, v, load, mass, v, *coarse),
            lanes,
        )
        coarse_lane = swap("lane", *coarse_lane)
        (x,) = run(
            coarse_kernel,
            [(coarse_block, (half_rows, half_columns, lanes))],
            [coarse_block] * 2 + coarse_spec + coarse_lane_spec,
            (place, load, mass, *coarse, *coarse_lane),
            lanes,
            scratch=[(total, half_wide)] * 4,
        )
        value = swap("band", *edge(x, even, SECOND))
        value_spec = [((SECOND, half_columns), (0, 0), 0)] * 2
        value_rows = half_rows + 2 * SECOND
        value_lane_spec = [((value_rows, TILE), (0, 0), 0)] * 2
        value_lane = run(
            value_pack_kernel,
            [(e, (value_rows, TILE, lanes)) for e in value_lane_spec],
            [half_first, half_last_tile] + value_spec,
            (place, x, x, *value),
            lanes,
        )
        value_lane = swap("lane", *value_lane)
        args = (
            place, f, m, v, load, mass, x, *fine, *fine_lane, *coarse, *coarse_lane, *value, *value_lane,
        )
        ins = (
            [whole] * 2
            + [own_block]
            + [coarse_block] * 3
            + fine_spec
            + lane_spec
            + coarse_spec
            + coarse_lane_spec
            + value_spec
            + value_lane_spec
        )
        outputs = run(
            after_kernel,
            [(whole, (rows, columns, layers))] * 2,
            ins + [None] * len(outputs),
            args + tuple(outputs),
            lanes,
            scratch=[(end, wide)] * 4 + [(total, half_wide)] * 4 + [(half_rows + 4, wide)],
            aliases={len(args) + k: k for k in range(len(outputs))},
        )
    return tuple(outputs)


def solution(mesh):
    return jax.shard_map(
        body,
        mesh=mesh,
        in_specs=(P("band", "lane", None), P("band", "lane", None), P("band", "lane", None)),
        out_specs=(P("band", "lane", None), P("band", "lane", None)),
        check_vma=False,
    )
```

time: 385 us -> 209 us (0.54)
  the two profiles are of different devices: /device:TPU:109 before, /device:TPU:131 now
where the time goes in v1:
time: 209 us; the launch traced here: 208 us
  waiting for transfers between devices  115 us (55%)
  Pallas kernels  57.3 us (27%)
  starting transfers between devices  21.9 us (10%)
  local copies, waits for them, and re-layouts  12.4 us (6%)
    ppermute x6, waiting for transfers between devices, swap(): lax.ppermute(odd, axis, swaps(count, 1))  82.6 us
    pallas_call x6, Pallas kernels, call(): pl.pallas_call(kernel, grid=(lanes // LANES,), in_specs=[pl.BlockSpec(mem...  57.3 us
    ppermute x6, waiting for transfers between devices, swap(): lax.ppermute(even, axis, swaps(count, 0))  32.4 us
    ppermute x6, starting transfers between devices, swap(): lax.ppermute(odd, axis, swaps(count, 1))  20.5 us
    dynamic_slice x6, local copies, waits for them, and re-layouts, edge(): lax.dynamic_slice_in_dim(value, low, depth, axis=0)  6.59 us
    unnamed x24, local copies, waits for them, and re-layouts  5.68 us
  transfers between devices with their start and end apart: 12, of which 9 were waited for; matrix products, arithmetic and copies ran while one was open for 0% of the time, Pallas kernels for 0%

profile of v1, /device:TPU:131, one launch (start us, length us, event | category | flops | bytes accessed | tf_op | source)
XLA Modules:
  0.0 208.1 jit_solution(15487842032878570114)
XLA Ops:
  0.7 1.1 constant_dynamic-slice_fusion.10
  1.7 1.3 constant_dynamic-slice_fusion.8
  3.1 0.8 collective-permute-start
  3.9 3.7 %collective-permute-start.1 = (f32[10,64,256]{2,1,0:T(8,128)S(1)}, f32[10,64,256]{2,1,0:T(8,128)S(1)}, u32[]{:S(2)}, u32[]{:S(2)}) collective-permute-start(f32[10,64,256]{2,1,0:T(8,128)S(1)} %pad_maximum_fusion.3), channel_id=1, source_target_pairs={{8,16},{16,8},{24,32},{32,24},{40,48},{48,40},{56,64},{64,56},{72,... | collective-permute-start | bytes 1966088 | tf_op jit(solution)/shard_map/ppermute | solution.py:32
  8.2 16.6 %collective-permute-done.1.got_o.fine_o = f32[10,64,256]{2,1,0:T(8,128)S(1)} collective-permute-done((f32[10,64,256]{2,1,0:T(8,128)S(1)}, f32[10,64,256]{2,1,0:T(8,128)S(1)}, u32[]{:S(2)}, u32[]{:S(2)}) %collective-permute-start.1) | collective-permute-done | bytes 655392 | tf_op jit(solution)/shard_map/ppermute | solution.py:32
  24.8 0.8 copy-done.3
  25.6 3.5 %shard_map.50 = (f32[72,8,256]{2,1,0:T(8,128)}, f32[72,8,256]{2,1,0:T(8,128)}) custom-call(s32[6]{0:T(128)} %stack.36.place, f32[64,64,256]{2,1,0:T(8,128)} %u_ref.1, f32[64,64,256]{2,1,0:T(8,128)} %f_ref.3, f32[64,64,256]{2,1,0:T(8,128)} %m_ref.3, f32[64,64,256]{2,1,0:T(8,128)} %u_ref.1, f32[64,64,256]{2,1,0:T(8,128)} %f_ref.3, f32[64,64,256]{2,1,0:T(8,128)} %m_ref.3, ...), custom_call_target="tpu_custom_call" | custom-call | tf_op jit(solution)/shard_map/pallas_call | solution.py:421
  29.4 4.1 %collective-permute-start.3 = (f32[72,8,256]{2,1,0:T(8,128)}, f32[72,8,256]{2,1,0:T(8,128)S(1)}, u32[]{:S(2)}, u32[]{:S(2)}) collective-permute-start(f32[72,8,256]{2,1,0:T(8,128)} %get-tuple-element.12), channel_id=1, source_target_pairs={{1,2},{2,1},{3,4},{4,3},{5,6},{6,5},{9,10},{10,9},{11,12},{12,11},... | collective-permute-start | bytes 1769480 | tf_op jit(solution)/shard_map/ppermute | solution.py:32
  33.6 9.2 %collective-permute-done.2.lane_e.fine_lane_e = f32[72,8,256]{2,1,0:T(8,128)S(1)} collective-permute-done((f32[72,8,256]{2,1,0:T(8,128)}, f32[72,8,256]{2,1,0:T(8,128)S(1)}, u32[]{:S(2)}, u32[]{:S(2)}) %collective-permute-start.2) | collective-permute-done | bytes 589856 | tf_op jit(solution)/shard_map/ppermute | solution.py:31
  42.8 10.7 %collective-permute-done.3.lane_o.fine_lane_o = f32[72,8,256]{2,1,0:T(8,128)S(1)} collective-permute-done((f32[72,8,256]{2,1,0:T(8,128)}, f32[72,8,256]{2,1,0:T(8,128)S(1)}, u32[]{:S(2)}, u32[]{:S(2)}) %collective-permute-start.3) | collective-permute-done | bytes 589856 | tf_op jit(solution)/shard_map/ppermute | solution.py:32
  53.5 0.8 copy-done.7
  54.3 17.3 %shard_map.51 = (f32[64,64,256]{2,1,0:T(8,128)}, f32[32,32,256]{2,1,0:T(8,128)}, f32[32,32,256]{2,1,0:T(8,128)}) custom-call(s32[6]{0:T(128)} %stack.36.place, f32[64,64,256]{2,1,0:T(8,128)} %u_ref.1, f32[64,64,256]{2,1,0:T(8,128)} %f_ref.3, f32[64,64,256]{2,1,0:T(8,128)} %m_ref.3, f32[10,64,256]{2,1,0:T(8,128)} %copy-done.2, f32[10,64,256]{2,1,0:T(8,128)} %copy-done.3, ...), custom_call_target="tpu_custom_call" | custom-call | tf_op jit(solution)/shard_map/pallas_call | solution.py:421
  71.6 1.0 constant_dynamic-slice_fusion.2
  72.7 1.1 constant_dynamic-slice_fusion.4
  73.8 1.1 constant_dynamic-slice_fusion.3
  75.1 2.4 %collective-permute-start.5 = (f32[22,32,256]{2,1,0:T(8,128)S(1)}, f32[22,32,256]{2,1,0:T(8,128)S(1)}, u32[]{:S(2)}, u32[]{:S(2)}) collective-permute-start(f32[22,32,256]{2,1,0:T(8,128)S(1)} %pad_maximum_fusion.1), channel_id=1, source_target_pairs={{8,16},{16,8},{24,32},{32,24},{40,48},{48,40},{56,64},{64,56},{72,... | collective-permute-start | bytes 2162696 | tf_op jit(solution)/shard_map/ppermute | solution.py:32
  77.5 21.2 %collective-permute-done.5.got_o.coarse_o = f32[22,32,256]{2,1,0:T(8,128)S(1)} collective-permute-done((f32[22,32,256]{2,1,0:T(8,128)S(1)}, f32[22,32,256]{2,1,0:T(8,128)S(1)}, u32[]{:S(2)}, u32[]{:S(2)}) %collective-permute-start.5) | collective-permute-done | bytes 720928 | tf_op jit(solution)/shard_map/ppermute | solution.py:32
  98.8 0.9 copy-done.1
  99.7 3.1 %shard_map.52 = (f32[132,8,256]{2,1,0:T(8,128)}, f32[132,8,256]{2,1,0:T(8,128)}) custom-call(s32[6]{0:T(128)} %stack.36.place, f32[32,32,256]{2,1,0:T(8,128)} %get-tuple-element.14.load_first.load_last.load_ref, f32[32,32,256]{2,1,0:T(8,128)} %get-tuple-element.15.mass_first.mass_last.mass_ref, f32[64,64,256]{2,1,0:T(8,128)} %get-tuple-element.13.v_first.v_last.v_ref, ...), custom_call_target="tpu_custom_call" | custom-call | tf_op jit(solution)/shard_map/pallas_call | solution.py:421
  102.9 4.4 %collective-permute-start.7 = (f32[132,8,256]{2,1,0:T(8,128)}, f32[132,8,256]{2,1,0:T(8,128)S(1)}, u32[]{:S(2)}, u32[]{:S(2)}) collective-permute-start(f32[132,8,256]{2,1,0:T(8,128)} %get-tuple-element.17), channel_id=1, source_target_pairs={{1,2},{2,1},{3,4},{4,3},{5,6},{6,5},{9,10},{10,9},{11,12},{12,11},... | collective-permute-start | bytes 3244040 | tf_op jit(solution)/shard_map/ppermute | solution.py:32
  107.2 19.5 %collective-permute-done.6.lane_e.coarse_lane_e = f32[132,8,256]{2,1,0:T(8,128)S(1)} collective-permute-done((f32[132,8,256]{2,1,0:T(8,128)}, f32[132,8,256]{2,1,0:T(8,128)S(1)}, u32[]{:S(2)}, u32[]{:S(2)}) %collective-permute-start.6) | collective-permute-done | bytes 1081376 | tf_op jit(solution)/shard_map/ppermute | solution.py:31
  126.7 19.8 %collective-permute-done.7.lane_o.coarse_lane_o = f32[132,8,256]{2,1,0:T(8,128)S(1)} collective-permute-done((f32[132,8,256]{2,1,0:T(8,128)}, f32[132,8,256]{2,1,0:T(8,128)S(1)}, u32[]{:S(2)}, u32[]{:S(2)}) %collective-permute-start.7) | collective-permute-done | bytes 1081376 | tf_op jit(solution)/shard_map/ppermute | solution.py:32
  146.6 1.0 copy-done.5
  147.6 10.7 %shard_map.53.x_first.x_last.x_ref = f32[32,32,256]{2,1,0:T(8,128)} custom-call(s32[6]{0:T(128)} %stack.36.place, f32[32,32,256]{2,1,0:T(8,128)} %get-tuple-element.14.load_first.load_last.load_ref, f32[32,32,256]{2,1,0:T(8,128)} %get-tuple-element.15.mass_first.mass_last.mass_ref, f32[22,32,256]{2,1,0:T(8,128)} %copy-done, f32[22,32,256]{2,1,0:T(8,128)} %copy-done.1, ...), custom_call_target="tpu_custom_call" | custom-call | tf_op jit(solution)/shard_map/pallas_call | solution.py:421
  158.3 1.0 constant_dynamic-slice_fusion
  159.3 1.9 collective-permute-start.9
  161.4 6.5 %collective-permute-done.9.got_o.value_o = f32[6,32,256]{2,1,0:T(8,128)S(1)} collective-permute-done((f32[6,32,256]{2,1,0:T(8,128)S(1)}, f32[6,32,256]{2,1,0:T(8,128)S(1)}, u32[]{:S(2)}, u32[]{:S(2)}) %collective-permute-start.9) | collective-permute-done | bytes 196640 | tf_op jit(solution)/shard_map/ppermute | solution.py:32
  169.2 2.0 shard_map.54
  171.2 4.1 %collective-permute-start.11 = (f32[44,8,256]{2,1,0:T(8,128)}, f32[44,8,256]{2,1,0:T(8,128)S(1)}, u32[]{:S(2)}, u32[]{:S(2)}) collective-permute-start(f32[44,8,256]{2,1,0:T(8,128)} %get-tuple-element.19), channel_id=1, source_target_pairs={{1,2},{2,1},{3,4},{4,3},{5,6},{6,5},{9,10},{10,9},{11,12},{12,11},... | collective-permute-start | bytes 1081352 | tf_op jit(solution)/shard_map/ppermute | solution.py:32
  175.3 3.7 %collective-permute-done.10.value_lane_e = f32[44,8,256]{2,1,0:T(8,128)S(1)} collective-permute-done((f32[44,8,256]{2,1,0:T(8,128)}, f32[44,8,256]{2,1,0:T(8,128)S(1)}, u32[]{:S(2)}, u32[]{:S(2)}) %collective-permute-start.10) | collective-permute-done | bytes 360480 | tf_op jit(solution)/shard_map/ppermute | solution.py:31
  179.0 7.8 %collective-permute-done.11.value_lane_o = f32[44,8,256]{2,1,0:T(8,128)S(1)} collective-permute-done((f32[44,8,256]{2,1,0:T(8,128)}, f32[44,8,256]{2,1,0:T(8,128)S(1)}, u32[]{:S(2)}, u32[]{:S(2)}) %collective-permute-start.11) | collective-permute-done | bytes 360480 | tf_op jit(solution)/shard_map/ppermute | solution.py:32
  187.5 20.6 %shard_map.55 = (f32[64,64,256]{2,1,0:T(8,128)}, f32[64,64,256]{2,1,0:T(8,128)}) custom-call(s32[6]{0:T(128)} %stack.36.place, f32[64,64,256]{2,1,0:T(8,128)} %f_ref.3, f32[64,64,256]{2,1,0:T(8,128)} %m_ref.3, f32[64,64,256]{2,1,0:T(8,128)} %get-tuple-element.13.v_first.v_last.v_ref, f32[32,32,256]{2,1,0:T(8,128)} %get-tuple-element.14.load_first.load_last.load_ref, ...), custom_call_target="tpu_custom_call" | custom-call | tf_op jit(solution)/shard_map/pallas_call | solution.py:421
  (34 shorter events, 3.5 us)
Async XLA Ops:
  3.1 5.1 %collective-permute-start = (f32[10,64,256]{2,1,0:T(8,128)S(1)}, f32[10,64,256]{2,1,0:T(8,128)S(1)}, u32[]{:S(2)}, u32[]{:S(2)}) collective-permute-start(f32[10,64,256]{2,1,0:T(8,128)S(1)} %pad_maximum_fusion.2), channel_id=1, source_target_pairs={{0,8},{8,0},{16,24},{24,16},{32,40},{40,32},{48,56},{56,48},{64,72... | collective-permute-start | bytes 1966088 | tf_op jit(solution)/shard_map/ppermute | solution.py:31
  3.9 20.9 %collective-permute-start.1 = (f32[10,64,256]{2,1,0:T(8,128)S(1)}, f32[10,64,256]{2,1,0:T(8,128)S(1)}, u32[]{:S(2)}, u32[]{:S(2)}) collective-permute-start(f32[10,64,256]{2,1,0:T(8,128)S(1)} %pad_maximum_fusion.3), channel_id=1, source_target_pairs={{8,16},{16,8},{24,32},{32,24},{40,48},{48,40},{56,64},{64,56},{72,... | collective-permute-start | bytes 1966088 | tf_op jit(solution)/shard_map/ppermute | solution.py:32
  8.2 16.6 %copy-start.2 = (f32[10,64,256]{2,1,0:T(8,128)}, f32[10,64,256]{2,1,0:T(8,128)S(1)}, u32[]{:S(2)}) copy-start(f32[10,64,256]{2,1,0:T(8,128)S(1)} %collective-permute-done.got_e.fine_e) | copy-start | bytes 1966084
  24.8 0.8 copy-start.3
  29.1 13.7 %collective-permute-start.2 = (f32[72,8,256]{2,1,0:T(8,128)}, f32[72,8,256]{2,1,0:T(8,128)S(1)}, u32[]{:S(2)}, u32[]{:S(2)}) collective-permute-start(f32[72,8,256]{2,1,0:T(8,128)} %get-tuple-element.11), channel_id=1, source_target_pairs={{0,1},{1,0},{2,3},{3,2},{4,5},{5,4},{6,7},{7,6},{8,9},{9,8},{10,11... | collective-permute-start | bytes 1769480 | tf_op jit(solution)/shard_map/ppermute | solution.py:31
  29.4 24.0 %collective-permute-start.3 = (f32[72,8,256]{2,1,0:T(8,128)}, f32[72,8,256]{2,1,0:T(8,128)S(1)}, u32[]{:S(2)}, u32[]{:S(2)}) collective-permute-start(f32[72,8,256]{2,1,0:T(8,128)} %get-tuple-element.12), channel_id=1, source_target_pairs={{1,2},{2,1},{3,4},{4,3},{5,6},{6,5},{9,10},{10,9},{11,12},{12,11},... | collective-permute-start | bytes 1769480 | tf_op jit(solution)/shard_map/ppermute | solution.py:32
  42.8 10.7 %copy-start.6 = (f32[72,8,256]{2,1,0:T(8,128)}, f32[72,8,256]{2,1,0:T(8,128)S(1)}, u32[]{:S(2)}) copy-start(f32[72,8,256]{2,1,0:T(8,128)S(1)} %collective-permute-done.2.lane_e.fine_lane_e) | copy-start | bytes 1769476
  53.5 0.8 copy-start.7
  74.9 2.6 %collective-permute-start.4 = (f32[22,32,256]{2,1,0:T(8,128)S(1)}, f32[22,32,256]{2,1,0:T(8,128)S(1)}, u32[]{:S(2)}, u32[]{:S(2)}) collective-permute-start(f32[22,32,256]{2,1,0:T(8,128)S(1)} %pad_maximum_fusion), channel_id=1, source_target_pairs={{0,8},{8,0},{16,24},{24,16},{32,40},{40,32},{48,56},{56,48},{64,72... | collective-permute-start | bytes 2162696 | tf_op jit(solution)/shard_map/ppermute | solution.py:31
  75.1 23.7 %collective-permute-start.5 = (f32[22,32,256]{2,1,0:T(8,128)S(1)}, f32[22,32,256]{2,1,0:T(8,128)S(1)}, u32[]{:S(2)}, u32[]{:S(2)}) collective-permute-start(f32[22,32,256]{2,1,0:T(8,128)S(1)} %pad_maximum_fusion.1), channel_id=1, source_target_pairs={{8,16},{16,8},{24,32},{32,24},{40,48},{48,40},{56,64},{64,56},{72,... | collective-permute-start | bytes 2162696 | tf_op jit(solution)/shard_map/ppermute | solution.py:32
  77.5 21.3 %copy-start = (f32[22,32,256]{2,1,0:T(8,128)}, f32[22,32,256]{2,1,0:T(8,128)S(1)}, u32[]{:S(2)}) copy-start(f32[22,32,256]{2,1,0:T(8,128)S(1)} %collective-permute-done.4.got_e.coarse_e) | copy-start | bytes 2162692
  98.8 0.9 copy-start.1
  102.8 23.9 %collective-permute-start.6 = (f32[132,8,256]{2,1,0:T(8,128)}, f32[132,8,256]{2,1,0:T(8,128)S(1)}, u32[]{:S(2)}, u32[]{:S(2)}) collective-permute-start(f32[132,8,256]{2,1,0:T(8,128)} %get-tuple-element.16), channel_id=1, source_target_pairs={{0,1},{1,0},{2,3},{3,2},{4,5},{5,4},{6,7},{7,6},{8,9},{9,8},{10,11... | collective-permute-start | bytes 3244040 | tf_op jit(solution)/shard_map/ppermute | solution.py:31
  102.9 43.7 %collective-permute-start.7 = (f32[132,8,256]{2,1,0:T(8,128)}, f32[132,8,256]{2,1,0:T(8,128)S(1)}, u32[]{:S(2)}, u32[]{:S(2)}) collective-permute-start(f32[132,8,256]{2,1,0:T(8,128)} %get-tuple-element.17), channel_id=1, source_target_pairs={{1,2},{2,1},{3,4},{4,3},{5,6},{6,5},{9,10},{10,9},{11,12},{12,11},... | collective-permute-start | bytes 3244040 | tf_op jit(solution)/shard_map/ppermute | solution.py:32
  126.7 19.9 %copy-start.4 = (f32[132,8,256]{2,1,0:T(8,128)}, f32[132,8,256]{2,1,0:T(8,128)S(1)}, u32[]{:S(2)}) copy-start(f32[132,8,256]{2,1,0:T(8,128)S(1)} %collective-permute-done.6.lane_e.coarse_lane_e) | copy-start | bytes 3244036
  146.6 1.0 copy-start.5
  159.3 8.5 %collective-permute-start.9 = (f32[6,32,256]{2,1,0:T(8,128)S(1)}, f32[6,32,256]{2,1,0:T(8,128)S(1)}, u32[]{:S(2)}, u32[]{:S(2)}) collective-permute-start(f32[6,32,256]{2,1,0:T(8,128)S(1)} %get-tuple-element.28), channel_id=1, source_target_pairs={{8,16},{16,8},{24,32},{32,24},{40,48},{48,40},{56,64},{64,56},{72,... | collective-permute-start | bytes 589832 | tf_op jit(solution)/shard_map/ppermute | solution.py:32
  161.3 6.6 %collective-permute-start.8 = (f32[6,32,256]{2,1,0:T(8,128)S(1)}, f32[6,32,256]{2,1,0:T(8,128)S(1)}, u32[]{:S(2)}, u32[]{:S(2)}) collective-permute-start(f32[6,32,256]{2,1,0:T(8,128)S(1)} %get-tuple-element.29), channel_id=1, source_target_pairs={{0,8},{8,0},{16,24},{24,16},{32,40},{40,32},{48,56},{56,48},{64,72... | collective-permute-start | bytes 589832 | tf_op jit(solution)/shard_map/ppermute | solution.py:31
  167.8 0.7 copy-start.8
  168.5 0.7 copy-start.9
  171.2 7.8 %collective-permute-start.10 = (f32[44,8,256]{2,1,0:T(8,128)}, f32[44,8,256]{2,1,0:T(8,128)S(1)}, u32[]{:S(2)}, u32[]{:S(2)}) collective-permute-start(f32[44,8,256]{2,1,0:T(8,128)} %get-tuple-element.18), channel_id=1, source_target_pairs={{0,1},{1,0},{2,3},{3,2},{4,5},{5,4},{6,7},{7,6},{8,9},{9,8},{10,11... | collective-permute-start | bytes 1081352 | tf_op jit(solution)/shard_map/ppermute | solution.py:31
  171.2 15.6 %collective-permute-start.11 = (f32[44,8,256]{2,1,0:T(8,128)}, f32[44,8,256]{2,1,0:T(8,128)S(1)}, u32[]{:S(2)}, u32[]{:S(2)}) collective-permute-start(f32[44,8,256]{2,1,0:T(8,128)} %get-tuple-element.19), channel_id=1, source_target_pairs={{1,2},{2,1},{3,4},{4,3},{5,6},{6,5},{9,10},{10,9},{11,12},{12,11},... | collective-permute-start | bytes 1081352 | tf_op jit(solution)/shard_map/ppermute | solution.py:32
  179.0 7.8 %copy-start.10 = (f32[44,8,256]{2,1,0:T(8,128)}, f32[44,8,256]{2,1,0:T(8,128)S(1)}, u32[]{:S(2)}) copy-start(f32[44,8,256]{2,1,0:T(8,128)S(1)} %collective-permute-done.10.value_lane_e) | copy-start | bytes 1081348
  186.8 0.7 copy-start.11

commit v2 on v0

v2 whole, which is shorter than its diff:
```python
import functools

import jax
import jax.numpy as jnp
from jax import lax
from jax.experimental import pallas as pl
from jax.experimental.pallas import tpu as pltpu
from jax.sharding import PartitionSpec as P

LANES = 128
INNER = 13
FINE = 4
TILE = 8
DEEP = 8
SECOND = 6
FIRST_SWEEPS = DEEP + 1
LAST_SWEEPS = INNER - FIRST_SWEEPS
CHUNKS = 4
FAR = 60
MASS = 56
NEAR = 55
BEFORE = 48
AFTER = 46
COST = 500_000_000


def swaps(count, first):
    pairs = []
    for i in range(first, count - 1, 2):
        pairs += [(i, i + 1), (i + 1, i)]
    return pairs


def swap(axis, even, odd):
    count = lax.axis_size(axis)
    return (
        lax.ppermute(even, axis, swaps(count, 0)),
        lax.ppermute(odd, axis, swaps(count, 1)),
    )


def place(axis):
    at, count = lax.axis_index(axis), lax.axis_size(axis)
    return lax.rem(at, 2) == 0, at > 0, at < count - 1


def roll(value, shift, axis):
    return pltpu.roll(value, shift % value.shape[axis], axis)


def sublane(value):
    return lax.broadcasted_iota(jnp.int32, value.shape, value.ndim - 2)


def by_side(even, got_even, got_odd):
    low = jnp.where(even, got_odd, got_even)
    high = jnp.where(even, got_even, got_odd)
    return low, high


def weight(mass, inside):
    return jnp.where(inside, 0.8 / (4.0 + mass), 0.0)


def new_value(here, left, right, up, down, load, w):
    return 0.2 * here + w * (load + ((up + down) + (left + right)))


def edges(even, rows, depth):
    return jnp.where(even, rows - depth, 0), jnp.where(even, 0, rows - depth)


def first_kernel(chain, u_hbm, f_hbm, m_hbm, even_ref, odd_ref, sems):
    even_b, _, _ = place("band")
    rows = m_hbm.shape[0]
    layers = pl.ds(chain * LANES, LANES)
    copies = []
    for side, target in enumerate((even_ref, odd_ref)):
        for part, (hbm, depth, at) in enumerate(((u_hbm, 4, 0), (f_hbm, 3, 4), (m_hbm, 3, 7))):
            start = edges(even_b, rows, depth)[side]
            copy = pltpu.make_async_copy(
                hbm.at[pl.ds(start, depth), :, layers],
                target.at[pl.ds(at, depth)],
                sems.at[3 * side + part],
            )
            copy.start()
            copies.append(copy)
    for copy in copies:
        copy.wait()


def mass_kernel(chain, m_hbm, mass_ref, even_ref, odd_ref, m_own, pairs, sems):
    even_b, _, _ = place("band")
    groups, rows, columns = m_own.shape[0], m_own.shape[1], m_own.shape[2]
    copies = []
    for g in range(groups):
        copy = pltpu.make_async_copy(m_hbm.at[:, :, pl.ds(g * LANES, LANES)], m_own.at[g], sems.at[g])
        copy.start()
        copies.append(copy)
    even_columns, odd_columns = pl.ds(0, columns // 2, 2), pl.ds(1, columns // 2, 2)
    for g in range(groups):
        copies[g].wait()

        def restrict(k, _, g=g):
            pairs[k] = m_own[g, 2 * k] + m_own[g, 2 * k + 1]
            mass_ref[g, k] = 0.5 * (pairs[k, even_columns, :] + pairs[k, odd_columns, :])
            return 0

        lax.fori_loop(0, rows // 2, restrict, 0, unroll=2)
        for side, target in enumerate((even_ref, odd_ref)):
            start = edges(even_b, rows // 2, DEEP)[side]
            target[g] = mass_ref[g, pl.ds(start, DEEP)]


def fold(value, side):
    rows, depth = value.shape[0] - 2 * DEEP, DEEP
    s = sublane(value[0])
    merged = []
    for r in range(1, depth):
        other = value[depth + rows - 1 + r]
        if side:
            merged.append(jnp.where(s >= depth - r, value[r], roll(other, -r, 0))[None])
        else:
            merged.append(jnp.where(s < r, value[r], roll(other, r, 0))[None])
    return jnp.concatenate(merged + [value[depth : depth + rows]], axis=0)


def unfold(got_e, got_o, even, rows, write, first=0):
    def own(k, _):
        low, high = by_side(even, got_e(first + DEEP - 1 + k), got_o(first + DEEP - 1 + k))
        write(DEEP + k, low, high)
        return 0

    lax.fori_loop(0, rows, own, 0, unroll=4)
    for r in range(1, DEEP):
        low, high = by_side(even, got_e(first + r - 1), got_o(first + r - 1))
        write(r, low, high)
        write(DEEP + rows - 1 + r, roll(low, r, 0), roll(high, -r, 0))


def mass_pack_kernel(chain, mass_ref, got_e, got_o, even_ref, odd_ref):
    even_b, even_l = place("band")[0], place("lane")[0]
    half = mass_ref.shape[2]
    for g in range(mass_ref.shape[0]):

        def message(side, g=g):
            at = pl.ds(side * (half - TILE), TILE)
            low, high = by_side(even_b, got_e[g, :, at, :], got_o[g, :, at, :])
            return fold(jnp.concatenate([low, mass_ref[g, :, at, :], high], axis=0), side)

        low, high = message(0), message(1)
        even_ref[g] = jnp.where(even_l, high, low)
        odd_ref[g] = jnp.where(even_l, low, high)


def lane_pack_kernel(chain, u_hbm, f_hbm, m_hbm, got_e, got_o, even_ref, odd_ref, tiles, sems):
    even_b, low_b, high_b = place("band")
    even_l, _, _ = place("lane")
    rows, columns = u_hbm.shape[0], u_hbm.shape[1]
    layers = pl.ds(chain * LANES, LANES)
    copies = []
    for side, start in enumerate((0, columns - TILE)):
        for part, hbm in enumerate((u_hbm, f_hbm, m_hbm)):
            copy = pltpu.make_async_copy(
                hbm.at[:, pl.ds(start, TILE), layers],
                tiles.at[3 * side + part],
                sems.at[3 * side + part],
            )
            copy.start()
            copies.append(copy)

    def message(side):
        at = pl.ds(side * (columns - TILE), TILE)
        low_rows, high_rows = by_side(even_b, got_e[:10, at, :], got_o[:10, at, :])
        zero = jnp.zeros((1, TILE, LANES), jnp.float32)
        own = [tiles[3 * side + part] for part in range(3)]
        u = jnp.concatenate([low_rows[:4], own[0], high_rows[:4]], axis=0)
        f = jnp.concatenate([zero, low_rows[4:7], own[1], high_rows[4:7], zero], axis=0)
        m = jnp.concatenate([zero, low_rows[7:10], own[2], high_rows[7:10], zero], axis=0)
        w = 0.8 / (4.0 + m)
        w = jnp.concatenate(
            [
                jnp.where(low_b, w[:4], 0.0),
                w[4 : 4 + rows],
                jnp.where(high_b, w[4 + rows :], 0.0),
            ],
            axis=0,
        )
        up = jnp.concatenate([zero, u[:-1]], axis=0)
        down = jnp.concatenate([u[1:], zero], axis=0)
        v = new_value(u, roll(u, 1, 1), roll(u, -1, 1), up, down, f, w)
        s = sublane(u)
        if side:
            f_m = jnp.where(s >= 2, roll(f, -4, 1), roll(m, -6, 1))
            return jnp.where(s >= 6, u, jnp.where(s >= 4, roll(v, -1, 1), f_m))
        f_m = jnp.where(s < 6, roll(f, 4, 1), roll(m, 6, 1))
        return jnp.where(s < 2, u, jnp.where(s < 4, roll(v, 1, 1), f_m))

    for copy in copies:
        copy.wait()
    low, high = message(0), message(1)
    even_ref[...] = jnp.where(even_l, high, low)
    odd_ref[...] = jnp.where(even_l, low, high)


def fine_halo(rows, columns, got_e, got_o, lane_e, lane_o, load, w):
    even_b, low_b, high_b = place("band")
    even_l, low_l, high_l = place("lane")
    own = pl.ds(TILE, columns)
    low_rows, high_rows = by_side(even_b, got_e[4:10], got_o[4:10])
    load[1:4, own, :] = low_rows[:3]
    w[1:4, own, :] = weight(low_rows[3:], low_b)
    load[pl.ds(FINE + rows, 3), own, :] = high_rows[:3]
    w[pl.ds(FINE + rows, 3), own, :] = weight(high_rows[3:], high_b)

    def lane_row(r, _):
        low, high = by_side(even_l, lane_e[r], lane_o[r])
        s = sublane(low)
        inside_row = ((r >= FINE) | low_b) & ((r < FINE + rows) | high_b)
        load[r, pl.ds(0, TILE), :] = roll(low, 4, 0)
        load[r, pl.ds(TILE + columns, TILE), :] = roll(high, -4, 0)
        w[r, pl.ds(0, TILE), :] = weight(roll(low, 6, 0), (s >= 6) & inside_row & low_l)
        w[r, pl.ds(TILE + columns, TILE), :] = weight(
            roll(high, -6, 0), (s < 2) & inside_row & high_l
        )
        return 0

    lax.fori_loop(0, rows + 2 * FINE, lane_row, 0, unroll=4)


def own_weight(m_own, w):
    rows, columns = m_own.shape[0], m_own.shape[1]

    def row(r, _):
        w[FINE + r, pl.ds(TILE, columns), :] = 0.8 / (4.0 + m_own[r])
        return 0

    lax.fori_loop(0, rows, row, 0, unroll=2)


def sweep(source, target, load, w, first, last):
    def row(r, carry):
        up, here = carry
        down = source[r + 1]
        target[r] = new_value(here, roll(here, 1, 0), roll(here, -1, 0), up, down, load[r], w[r])
        return here, down

    lax.fori_loop(first, last, row, (source[first - 1], source[first]), unroll=2)


def before_kernel(
    chain, u_hbm, f_hbm, m_hbm, got_e, got_o, lane_e, lane_o,
    v_ref, load_ref, even_ref, odd_ref, a, b, load, w, m_own, pairs, sems,
):
    even_b, even_l = place("band")[0], place("lane")[0]
    rows, columns = m_own.shape[0], m_own.shape[1]
    half_columns = columns // 2
    inner, own = pl.ds(FINE, rows), pl.ds(TILE, columns)
    left, right = pl.ds(0, TILE), pl.ds(TILE + columns, TILE)
    layers = pl.ds(chain * LANES, LANES)
    copies = [
        pltpu.make_async_copy(m_hbm.at[:, :, layers], m_own, sems.at[0]),
        pltpu.make_async_copy(f_hbm.at[:, :, layers], load.at[inner, own, :], sems.at[1]),
        pltpu.make_async_copy(u_hbm.at[:, :, layers], a.at[inner, own, :], sems.at[2]),
    ]
    for copy in copies:
        copy.start()
    fine_halo(rows, columns, got_e, got_o, lane_e, lane_o, load, w)
    low_rows, high_rows = by_side(even_b, got_e[:4], got_o[:4])
    a[:4, own, :] = low_rows
    a[pl.ds(FINE + rows, 4), own, :] = high_rows

    def lane_row(r, _):
        low, high = by_side(even_l, lane_e[r], lane_o[r])
        a[r, left, :] = low
        a[r, right, :] = high
        return 0

    end = rows + 2 * FINE
    lax.fori_loop(0, end, lane_row, 0, unroll=4)
    copies[0].wait()
    own_weight(m_own, w)
    copies[1].wait()
    copies[2].wait()
    sweep(a, b, load, w, 1, end - 1)

    def mend(r, _):
        low, high = by_side(even_l, lane_e[r], lane_o[r])
        s = sublane(low)
        b[r, left, :] = jnp.where(s == 7, b[r, left, :], roll(low, 1, 0))
        b[r, right, :] = jnp.where(s == 0, b[r, right, :], roll(high, -1, 0))
        return 0

    lax.fori_loop(1, end - 1, mend, 0, unroll=2)
    sweep(b, a, load, w, 2, end - 2)
    sweep(a, b, load, w, 3, end - 3)

    def defect_of(i, up, here, down):
        around = (up + down) + (roll(here, 1, 0) + roll(here, -1, 0))
        value = lax.slice_in_dim(load[FINE + i] + around, TILE, TILE + columns, axis=0)
        mine = lax.slice_in_dim(here, TILE, TILE + columns, axis=0)
        return value - (4.0 + m_own[i]) * mine

    even_columns, odd_columns = pl.ds(0, half_columns, 2), pl.ds(1, half_columns, 2)

    def restrict(k, carry):
        up, here = carry
        i = 2 * k
        middle, down = b[FINE + i + 1], b[FINE + i + 2]
        first = defect_of(i, up, here, middle)
        second = defect_of(i + 1, here, middle, down)
        v_ref[FINE + i] = here
        v_ref[FINE + i + 1] = middle
        pairs[k] = first + second
        load_ref[k] = 0.5 * (pairs[k, even_columns, :] + pairs[k, odd_columns, :])
        return middle, down

    lax.fori_loop(0, rows // 2, restrict, (b[FINE - 1], b[FINE]))
    v_ref[FINE - 1] = b[FINE - 1]
    v_ref[FINE + rows] = b[FINE + rows]
    for side, target in enumerate((even_ref, odd_ref)):
        start = edges(even_b, rows // 2, DEEP)[side]
        target[:DEEP] = load_ref[pl.ds(start, DEEP)]
        start = FINE + (jnp.where(even_b, rows - 3, 1) if side == 0 else jnp.where(even_b, 1, rows - 3))
        for k in range(4):
            at = pl.ds(TILE + k % 2 * half_columns, half_columns)
            target[DEEP + k] = v_ref[start + k // 2, at, :]


def coarse_pack_kernel(chain, load_ref, v_ref, got_e, got_o, even_ref, odd_ref):
    even_b, even_l = place("band")[0], place("lane")[0]
    half = load_ref.shape[1]
    rows, columns = v_ref.shape[0] - 2 * FINE, v_ref.shape[1] - 2 * TILE
    zero = jnp.zeros((1, TILE, LANES), jnp.float32)

    def message(side):
        at = pl.ds(side * (half - TILE), TILE)
        low, top = by_side(even_b, got_e[:, at, :], got_o[:, at, :])
        load = fold(jnp.concatenate([low[:DEEP], load_ref[:, at, :], top[:DEEP]], axis=0), side)
        near = -1 if side else 1
        tile = pl.ds(TILE + side * (columns - TILE), TILE)
        v = v_ref[pl.ds(FINE - 1, rows + 2), tile, :]
        below = roll(low[DEEP + 2 + side][None], near, 1)
        above = roll(top[DEEP + side][None], near, 1)
        v = jnp.concatenate([zero, zero, below, v, above, zero, zero], axis=0)
        quarter = v.shape[0] // 4
        first = 5 if side else 1
        parts = [roll(v[g * quarter : (g + 1) * quarter], 2 * g - first, 1) for g in range(4)]
        s = sublane(parts[0])
        v = jnp.where(
            s < 4, jnp.where(s < 2, parts[0], parts[1]), jnp.where(s < 6, parts[2], parts[3])
        )
        return jnp.concatenate([load, v], axis=0)

    low, high = message(0), message(1)
    even_ref[...] = jnp.where(even_l, high, low)
    odd_ref[...] = jnp.where(even_l, low, high)


def coarse_fields(
    group, load_ref, mass_ref, load_e, load_o, mass_e, mass_o, load_lane_e, load_lane_o, mass_lane_e, mass_lane_o, load, w
):
    even_b, low_b, high_b = place("band")
    even_l, low_l, high_l = place("lane")
    rows, columns = load_ref.shape[0], load_ref.shape[1]
    own = pl.ds(TILE, columns)

    def copy_row(r, _):
        load[DEEP + r, own, :] = load_ref[r]
        w[DEEP + r, own, :] = 0.8 / (4.0 + mass_ref[group, r])
        return 0

    lax.fori_loop(0, rows, copy_row, 0, unroll=4)
    low, high = by_side(even_b, load_e[:DEEP], load_o[:DEEP])
    load[:DEEP, own, :] = low
    load[pl.ds(DEEP + rows, DEEP), own, :] = high
    low, high = by_side(even_b, mass_e[group], mass_o[group])
    w[:DEEP, own, :] = weight(low, low_b)
    w[pl.ds(DEEP + rows, DEEP), own, :] = weight(high, high_b)
    left, right = pl.ds(0, TILE), pl.ds(TILE + columns, TILE)

    def put_load(r, low, high):
        load[r, left, :] = low
        load[r, right, :] = high

    def put_weight(r, low, high):
        inside_row = ((r >= DEEP) | low_b) & ((r < DEEP + rows) | high_b)
        w[r, left, :] = weight(low, inside_row & low_l)
        w[r, right, :] = weight(high, inside_row & high_l)

    unfold(lambda k: load_lane_e[k], lambda k: load_lane_o[k], even_l, rows, put_load)
    unfold(lambda k: mass_lane_e[group, k], lambda k: mass_lane_o[group, k], even_l, rows, put_weight)
    zero = jnp.zeros((TILE, LANES), jnp.float32)
    for r in (0, rows + 2 * DEEP - 1):
        put_load(r, zero, zero)
        w[r, left, :] = zero
        w[r, right, :] = zero


def coarse_kernel(chain, *refs):
    fields, (x_ref, even_ref, odd_ref, a, b, load, w) = refs[:10], refs[10:]
    rows, columns = x_ref.shape[0], x_ref.shape[1]
    coarse_fields(chain, *fields, load, w)
    total = rows + 2 * DEEP

    def first(r, _):
        a[r] = w[r] * load[r]
        return 0

    lax.fori_loop(0, total, first, 0, unroll=4)
    source, target = a, b
    for step in range(1, FIRST_SWEEPS):
        sweep(source, target, load, w, step, total - step)
        source, target = target, source

    def out(r, _):
        x_ref[r] = source[DEEP + r, pl.ds(TILE, columns), :]
        return 0

    lax.fori_loop(0, rows, out, 0, unroll=4)
    for side, target in enumerate((even_ref, odd_ref)):
        start = edges(place("band")[0], rows, SECOND)[side]
        target[...] = x_ref[pl.ds(start, SECOND)]


def value_pack_kernel(chain, x_ref, got_e, got_o, even_ref, odd_ref):
    even_b, even_l = place("band")[0], place("lane")[0]
    zero = jnp.zeros((DEEP - SECOND, TILE, LANES), jnp.float32)

    def message(side):
        at = pl.ds(side * (x_ref.shape[1] - TILE), TILE)
        low, high = by_side(even_b, got_e[:, at, :], got_o[:, at, :])
        return fold(jnp.concatenate([zero, low, x_ref[:, at, :], high, zero], axis=0), side)

    low, high = message(0), message(1)
    even_ref[...] = jnp.where(even_l, high, low)
    odd_ref[...] = jnp.where(even_l, low, high)


def after_kernel(
    chain, f_hbm, m_hbm, v_ref, x_ref, fine_e, fine_o, fine_lane_e, fine_lane_o, *refs
):
    fields, (value_e, value_o, value_lane_e, value_lane_o), rest = refs[:10], refs[10:14], refs[14:]
    u_hbm, d_hbm, a, b, load, w, m_own, x, y, coarse_load, coarse_w, spread, sems = rest[-13:]
    _, _, coarse_e, coarse_o, _, _, coarse_lane_e, coarse_lane_o, _, _ = fields
    even_b, even_l = place("band")[0], place("lane")[0]
    rows, columns = m_own.shape[0], m_own.shape[1]
    half_rows, half_columns = rows // 2, columns // 2
    layers = pl.ds(chain * LANES, LANES)
    inner, fine_own = pl.ds(FINE, rows), pl.ds(TILE, columns)
    left, right = pl.ds(0, TILE), pl.ds(TILE + columns, TILE)
    copies = [
        pltpu.make_async_copy(m_hbm.at[:, :, layers], m_own, sems.at[0]),
        pltpu.make_async_copy(f_hbm.at[:, :, layers], load.at[inner, fine_own, :], sems.at[1]),
    ]
    for copy in copies:
        copy.start()
    coarse_fields(chain, *fields, coarse_load, coarse_w)
    own = pl.ds(TILE, half_columns)
    total = half_rows + 2 * DEEP
    low, high = by_side(even_b, value_e[...], value_o[...])
    x[DEEP - SECOND : DEEP, own, :] = low
    x[pl.ds(DEEP + half_rows, SECOND), own, :] = high

    def coarse_copy(r, _):
        x[DEEP + r, own, :] = x_ref[r]
        return 0

    lax.fori_loop(0, half_rows, coarse_copy, 0, unroll=4)

    def put_value(r, low, high):
        x[r, pl.ds(0, TILE), :] = low
        x[r, pl.ds(TILE + half_columns, TILE), :] = high

    unfold(lambda k: value_lane_e[k], lambda k: value_lane_o[k], even_l, half_rows, put_value)
    source, target = x, y
    for step in range(1, LAST_SWEEPS + 1):
        edge = DEEP - SECOND + step
        sweep(source, target, coarse_load, coarse_w, edge, total - edge)
        source, target = target, source

    fine_halo(rows, columns, fine_e, fine_o, fine_lane_e, fine_lane_o, load, w)
    copies[0].wait()
    own_weight(m_own, w)

    a[FINE - 1] = v_ref[FINE - 1]
    a[FINE + rows] = v_ref[FINE + rows]
    for i in range(2):
        for part in range(2):
            at = pl.ds(TILE + part * half_columns, half_columns)
            k = DEEP + 2 * i + part
            low, high = by_side(even_b, coarse_e[k], coarse_o[k])
            a[1 + i, at, :] = low
            a[FINE + rows + 1 + i, at, :] = high
    end = rows + 2 * FINE
    quarter = end // 4
    above = DEEP - 1 + half_rows

    def fine_lane(k, _):
        low, high = by_side(even_l, coarse_lane_e[above + k], coarse_lane_o[above + k])
        s = sublane(low)
        for g in range(4):
            r = g * quarter + k
            second = (r == FINE - 2) | (r == FINE + rows + 1)
            deep_low, deep_high = roll(low, 5 - 2 * g, 0), roll(high, 1 - 2 * g, 0)
            near_low = jnp.where(second, roll(deep_low, 1, 0), v_ref[r, left, :])
            near_high = jnp.where(second, roll(deep_high, -1, 0), v_ref[r, right, :])
            a[r, left, :] = jnp.where(s == TILE - 1, near_low, deep_low)
            a[r, right, :] = jnp.where(s == 0, near_high, deep_high)
        return 0

    lax.fori_loop(0, quarter, fine_lane, 0, unroll=2)
    across = columns // 2 + TILE
    skip = TILE - TILE // 2

    def spread_row(k):
        value = source[DEEP - 2 + k, pl.ds(skip, across), :]
        spread[k, pl.ds(0, across, 2), :] = value
        spread[k, pl.ds(1, across, 2), :] = value
        return spread[k]

    for k in (0, 1, half_rows + 2, half_rows + 3):
        both = spread_row(k)
        a[2 * k] += both
        a[2 * k + 1] += both

    def correct(k, _):
        both = spread_row(k)
        ends = [lax.slice_in_dim(both, s, s + TILE, axis=0) for s in (0, TILE + columns)]
        middle = lax.slice_in_dim(both, TILE, TILE + columns, axis=0)
        for part in range(2):
            r = 2 * k + part
            a[r, fine_own, :] = v_ref[r, fine_own, :] + middle
            a[r, left, :] += ends[0]
            a[r, right, :] += ends[1]
        return 0

    lax.fori_loop(2, half_rows + 2, correct, 0, unroll=2)
    copies[1].wait()
    sweep(a, b, load, w, 2, end - 2)
    sweep(b, a, load, w, 3, end - 3)
    piece = rows // CHUNKS

    def put(source, hbm, at, sem):
        copy = pltpu.make_async_copy(
            source.at[pl.ds(FINE + at, piece), fine_own, :],
            hbm.at[pl.ds(at, piece), :, layers],
            sem,
        )
        copy.start()
        return copy

    puts = [put(a, u_hbm, c * piece, sems.at[2 + c]) for c in range(CHUNKS)]

    def remains(i, carry):
        up, here = carry
        down = a[FINE + i + 1]
        around = (up + down) + (roll(here, 1, 0) + roll(here, -1, 0))
        value = lax.slice_in_dim(load[FINE + i] + around, TILE, TILE + columns, axis=0)
        mine = lax.slice_in_dim(here, TILE, TILE + columns, axis=0)
        b[FINE + i, fine_own, :] = value - (4.0 + m_own[i]) * mine
        return here, down

    carry = (a[FINE - 1], a[FINE])
    for c in range(CHUNKS):
        carry = lax.fori_loop(c * piece, (c + 1) * piece, remains, carry, unroll=2)
        puts.append(put(b, d_hbm, c * piece, sems.at[2 + CHUNKS + c]))
    for copy in puts:
        copy.wait()


def call(kernel, chain, outs, args, limit, scratch=(), sems=0, hbm=0, hbm_out=False, aliases=None, extra=0, us=1):
    far, near = pl.BlockSpec(memory_space=pltpu.HBM), pl.BlockSpec(memory_space=pltpu.VMEM)
    near_count = len(args) - hbm - extra
    return pl.pallas_call(
        functools.partial(kernel, chain),
        in_specs=[far] * hbm + [near] * near_count + [far] * extra,
        out_specs=[far if hbm_out else near] * len(outs),
        out_shape=[jax.ShapeDtypeStruct(s, jnp.float32) for s in outs],
        scratch_shapes=[pltpu.VMEM(s + (LANES,), jnp.float32) for s in scratch]
        + ([pltpu.SemaphoreType.DMA((sems,))] if sems else []),
        input_output_aliases=aliases or {},
        cost_estimate=pl.CostEstimate(flops=us * COST, bytes_accessed=0, transcendentals=0),
        compiler_params=pltpu.CompilerParams(vmem_limit_bytes=limit * 1024 * 1024),
    )(*args)


def program(f, u, m):
    rows, columns, layers = f.shape
    half_rows, half_columns = rows // 2, columns // 2
    end, total = rows + 2 * FINE, half_rows + 2 * DEEP
    folded = DEEP - 1 + half_rows
    wide, half_wide = columns + 2 * TILE, half_columns + 2 * TILE
    groups = layers // LANES
    coarse_block = (half_rows, half_columns, LANES)
    chains = range(groups)

    fines = []
    for c in chains:
        even, odd = call(first_kernel, c, [(10, columns, LANES)] * 2, (u, f, m), FAR, sems=6, hbm=3)
        fines.append(swap("band", even, odd))
    mass, even, odd = call(
        mass_kernel, 0, [(groups,) + coarse_block] + [(groups, DEEP, half_columns, LANES)] * 2, (m,), MASS,
        scratch=[(groups, rows, columns), (half_rows, columns)], sems=groups, hbm=1,
    )
    masses = swap("band", even, odd)
    fine_lanes = []
    for c in chains:
        even, odd = call(
            lane_pack_kernel, c, [(end, TILE, LANES)] * 2, (u, f, m, *fines[c]), NEAR,
            scratch=[(6, rows, TILE)], sems=6, hbm=3,
        )
        fine_lanes.append(swap("lane", even, odd))
    even, odd = call(mass_pack_kernel, 0, [(groups, folded, TILE, LANES)] * 2, (mass, *masses), 4)
    mass_lanes = swap("lane", even, odd)
    values, loads, coarses = [], [], []
    for c in chains:
        v, load, even, odd = call(
            before_kernel, c, [(end, wide, LANES), coarse_block] + [(DEEP + 4, half_columns, LANES)] * 2,
            (u, f, m, *fines[c], *fine_lanes[c]), BEFORE, us=6,
            scratch=[(end, wide)] * 4 + [(rows, columns), (half_rows, columns)], sems=3, hbm=3,
        )
        values.append(v)
        loads.append(load)
        coarses.append(swap("band", even, odd))
    coarse_lanes = []
    for c in chains:
        even, odd = call(
            coarse_pack_kernel, c, [(folded + end // 4, TILE, LANES)] * 2, (loads[c], values[c], *coarses[c]), 4,
        )
        coarse_lanes.append(swap("lane", even, odd))
    fields, xs, nexts = [], [], []
    for c in chains:
        fields.append((loads[c], mass, *coarses[c], *masses, *coarse_lanes[c], *mass_lanes))
        x, even, odd = call(
            coarse_kernel, c, [coarse_block] + [(SECOND, half_columns, LANES)] * 2, fields[c], 8, us=4,
            scratch=[(total, half_wide)] * 4,
        )
        xs.append(x)
        nexts.append(swap("band", even, odd))
    next_lanes = []
    for c in chains:
        even, odd = call(value_pack_kernel, c, [(folded, TILE, LANES)] * 2, (xs[c], *nexts[c]), 4)
        next_lanes.append(swap("lane", even, odd))
    results = ()
    for c in chains:
        args = (f, m, values[c], xs[c], *fines[c], *fine_lanes[c], *fields[c], *nexts[c], *next_lanes[c])
        results = tuple(
            call(
                after_kernel, c, [(rows, columns, layers)] * 2, args + results, AFTER, us=8,
                scratch=[(end, wide)] * 4 + [(rows, columns)] + [(total, half_wide)] * 4 + [(half_rows + 4, wide)],
                sems=2 + 2 * CHUNKS, hbm=2, hbm_out=True, extra=len(results),
                aliases={len(args) + k: k for k in range(len(results))},
            )
        )
    return results


def solution(mesh):
    return jax.shard_map(
        program,
        mesh=mesh,
        in_specs=(P("band", "lane", None), P("band", "lane", None), P("band", "lane", None)),
        out_specs=(P("band", "lane", None), P("band", "lane", None)),
        check_vma=False,
    )
```

time: 385 us -> 159 us (0.41); the launches traced: 378 us -> 158 us
  starting transfers between devices: 174 us -> 67.6 us
  other arithmetic: 83.8 us -> 0 us
  waiting for transfers between devices: 87.4 us -> 27.7 us
  Pallas kernels: 0 us -> 58.9 us
  local copies, waits for them, and re-layouts: 31.1 us -> 2.45 us
    ppermute x56 -> x28, starting transfers between devices: 174 us -> 67.6 us  [the longest x14 44 us: swap(): lax.ppermute(odd, axis, swaps(count, 1))]
    ppermute x56 -> x28, waiting for transfers between devices: 87.4 us -> 27.7 us  [the longest x14 23.7 us: swap(): lax.ppermute(odd, axis, swaps(count, 1))]
    pallas_call x0 -> x16, Pallas kernels: none -> 58.9 us  [call(): pl.pallas_call(functools.partial(kernel, chain), in_specs=[far] * hbm + [...]
    add x12 -> x0, other arithmetic: 37.3 us -> none  [the longest x11 32.9 us: smooth_step(): values + 0.8 * (load + cross_sum(padded) - (4.0 + mass_here) * values) /...]
    sub x2 -> x0, other arithmetic: 20 us -> none  [the longest x1 13.6 us: body(): load_terms + cross_sum(extended(values, (('band', 0), ('lane', 1)), 1, Fa...]
    reshape x3 -> x0, local copies, waits for them, and re-layouts: 17.7 us -> none  [the longest x2 11.6 us: block_means(): values.reshape(values.shape[0] // RATIO, RATIO, values.shape[1] // RATIO,...]
    select_n x6 -> x0, other arithmetic: 13.4 us -> none  [body(): once = jnp.where(strip_rim(inside), once, 0.0)]
    reduce_sum x2 -> x0, other arithmetic: 11 us -> none  [block_means(): return jnp.mean(cut, axis=(1, 3))]
  transfers between devices with their start and end apart: 56 -> 28, of which waited for: 18 -> 6; matrix products, arithmetic and copies ran while one was open for 4% -> 0% of each run, Pallas kernels for 0% -> 30%
where the time goes in v2:
time: 159 us; the launch traced here: 158 us
  starting transfers between devices  67.6 us (43%)
  Pallas kernels  58.9 us (37%)
  waiting for transfers between devices  27.7 us (17%)
  local copies, waits for them, and re-layouts  2.45 us (2%)
    pallas_call x16, Pallas kernels, call(): pl.pallas_call(functools.partial(kernel, chain), in_specs=[far] * hbm + [...  58.9 us
    ppermute x14, starting transfers between devices, swap(): lax.ppermute(odd, axis, swaps(count, 1))  44 us
    ppermute x14, waiting for transfers between devices, swap(): lax.ppermute(odd, axis, swaps(count, 1))  23.7 us
    ppermute x14, starting transfers between devices, swap(): lax.ppermute(even, axis, swaps(count, 0))  23.5 us
    ppermute x14, waiting for transfers between devices, swap(): lax.ppermute(even, axis, swaps(count, 0))  4.01 us
  transfers between devices with their start and end apart: 28, of which 6 were waited for; matrix products, arithmetic and copies ran while one was open for 0% of the time, Pallas kernels for 30%

profile of v2, /device:TPU:109, one launch (start us, length us, event | category | flops | bytes accessed | tf_op | source)
XLA Modules:
  0.0 157.8 jit_solution(9576487455506466738)
XLA Ops:
  0.6 2.1 %shard_map.58 = (f32[10,64,128]{2,1,0:T(8,128)}, f32[10,64,128]{2,1,0:T(8,128)}) custom-call(f32[64,64,256]{2,1,0:T(8,128)} %u_hbm.11, f32[64,64,256]{2,1,0:T(8,128)} %f_hbm.15, f32[64,64,256]{2,1,0:T(8,128)} %m_hbm.17), custom_call_target="tpu_custom_call" | custom-call | flops 500000000 | tf_op jit(solution)/shard_map/pallas_call | solution.py:575
  3.5 4.6 %collective-permute-start.17 = (f32[10,64,128]{2,1,0:T(8,128)}, f32[10,64,128]{2,1,0:T(8,128)S(1)}, u32[]{:S(2)}, u32[]{:S(2)}) collective-permute-start(f32[10,64,128]{2,1,0:T(8,128)} %get-tuple-element.60), channel_id=1, source_target_pairs={{8,16},{16,8},{24,32},{32,24},{40,48},{48,40},{56,64},{64,56},{72,... | collective-permute-start | bytes 983048 | tf_op jit(solution)/shard_map/ppermute | solution.py:38
  8.1 2.1 %shard_map.50 = (f32[10,64,128]{2,1,0:T(8,128)}, f32[10,64,128]{2,1,0:T(8,128)}) custom-call(f32[64,64,256]{2,1,0:T(8,128)} %u_hbm.11, f32[64,64,256]{2,1,0:T(8,128)} %f_hbm.15, f32[64,64,256]{2,1,0:T(8,128)} %m_hbm.17), custom_call_target="tpu_custom_call" | custom-call | flops 500000000 | tf_op jit(solution)/shard_map/pallas_call | solution.py:575
  10.3 5.0 %collective-permute-start.1 = (f32[10,64,128]{2,1,0:T(8,128)}, f32[10,64,128]{2,1,0:T(8,128)S(1)}, u32[]{:S(2)}, u32[]{:S(2)}) collective-permute-start(f32[10,64,128]{2,1,0:T(8,128)} %get-tuple-element.40), channel_id=1, source_target_pairs={{8,16},{16,8},{24,32},{32,24},{40,48},{48,40},{56,64},{64,56},{72,... | collective-permute-start | bytes 983048 | tf_op jit(solution)/shard_map/ppermute | solution.py:38
  16.8 3.7 %shard_map.59 = (f32[72,8,128]{2,1,0:T(8,128)}, f32[72,8,128]{2,1,0:T(8,128)}) custom-call(f32[64,64,256]{2,1,0:T(8,128)} %u_hbm.11, f32[64,64,256]{2,1,0:T(8,128)} %f_hbm.15, f32[64,64,256]{2,1,0:T(8,128)} %m_hbm.17, f32[10,64,128]{2,1,0:T(8,128)} %copy-done.7, f32[10,64,128]{2,1,0:T(8,128)} %copy-done.9), custom_call_target="tpu_custom_call" | custom-call | flops 500000000 | tf_op jit(solution)/shard_map/pallas_call | solution.py:575
  21.5 2.3 %collective-permute-start.19 = (f32[72,8,128]{2,1,0:T(8,128)}, f32[72,8,128]{2,1,0:T(8,128)S(1)}, u32[]{:S(2)}, u32[]{:S(2)}) collective-permute-start(f32[72,8,128]{2,1,0:T(8,128)} %get-tuple-element.62), channel_id=1, source_target_pairs={{1,2},{2,1},{3,4},{4,3},{5,6},{6,5},{9,10},{10,9},{11,12},{12,11},... | collective-permute-start | bytes 884744 | tf_op jit(solution)/shard_map/ppermute | solution.py:38
  25.3 3.7 %shard_map.51 = (f32[72,8,128]{2,1,0:T(8,128)}, f32[72,8,128]{2,1,0:T(8,128)}) custom-call(f32[64,64,256]{2,1,0:T(8,128)} %u_hbm.11, f32[64,64,256]{2,1,0:T(8,128)} %f_hbm.15, f32[64,64,256]{2,1,0:T(8,128)} %m_hbm.17, f32[10,64,128]{2,1,0:T(8,128)} %copy-done.3, f32[10,64,128]{2,1,0:T(8,128)} %copy-done.5), custom_call_target="tpu_custom_call" | custom-call | flops 500000000 | tf_op jit(solution)/shard_map/pallas_call | solution.py:575
  29.0 2.1 %collective-permute-start.2 = (f32[72,8,128]{2,1,0:T(8,128)}, f32[72,8,128]{2,1,0:T(8,128)S(1)}, u32[]{:S(2)}, u32[]{:S(2)}) collective-permute-start(f32[72,8,128]{2,1,0:T(8,128)} %get-tuple-element.41), channel_id=1, source_target_pairs={{0,1},{1,0},{2,3},{3,2},{4,5},{5,4},{6,7},{7,6},{8,9},{9,8},{10,11... | collective-permute-start | bytes 884744 | tf_op jit(solution)/shard_map/ppermute | solution.py:37
  33.1 3.7 %shard_map.53 = (f32[2,32,32,128]{3,2,1,0:T(8,128)}, f32[2,8,32,128]{3,2,1,0:T(8,128)}, f32[2,8,32,128]{3,2,1,0:T(8,128)}) custom-call(f32[64,64,256]{2,1,0:T(8,128)} %m_hbm.17), custom_call_target="tpu_custom_call" | custom-call | flops 500000000 | tf_op jit(solution)/shard_map/pallas_call | solution.py:575
  36.7 3.8 %collective-permute-start.6 = (f32[2,8,32,128]{3,2,1,0:T(8,128)}, f32[2,8,32,128]{3,2,1,0:T(8,128)S(1)}, u32[]{:S(2)}, u32[]{:S(2)}) collective-permute-start(f32[2,8,32,128]{3,2,1,0:T(8,128)} %get-tuple-element.48), channel_id=1, source_target_pairs={{0,8},{8,0},{16,24},{24,16},{32,40},{40,32},{48,56},{56,48},{64,72... | collective-permute-start | bytes 786440 | tf_op jit(solution)/shard_map/ppermute | solution.py:37
  40.5 4.0 %collective-permute-start.7 = (f32[2,8,32,128]{3,2,1,0:T(8,128)}, f32[2,8,32,128]{3,2,1,0:T(8,128)S(1)}, u32[]{:S(2)}, u32[]{:S(2)}) collective-permute-start(f32[2,8,32,128]{3,2,1,0:T(8,128)} %get-tuple-element.49), channel_id=1, source_target_pairs={{8,16},{16,8},{24,32},{32,24},{40,48},{48,40},{56,64},{64,56},{72,... | collective-permute-start | bytes 786440 | tf_op jit(solution)/shard_map/ppermute | solution.py:38
  44.6 7.7 %shard_map.60 = (f32[72,80,128]{2,1,0:T(8,128)S(1)}, f32[32,32,128]{2,1,0:T(8,128)S(1)}, f32[12,32,128]{2,1,0:T(8,128)S(1)}, f32[12,32,128]{2,1,0:T(8,128)S(1)}) custom-call(f32[64,64,256]{2,1,0:T(8,128)} %u_hbm.11, f32[64,64,256]{2,1,0:T(8,128)} %f_hbm.15, f32[64,64,256]{2,1,0:T(8,128)} %m_hbm.17, f32[10,64,128]{2,1,0:T(8,128)S(1)} %copy-done.8, ...), custom_call_target="tpu_custom_call" | custom-call | flops 3000000000 | tf_op jit(solution)/shard_map/pallas_call | solution.py:575
  52.4 6.5 %collective-permute-start.21 = (f32[12,32,128]{2,1,0:T(8,128)S(1)}, f32[12,32,128]{2,1,0:T(8,128)S(1)}, u32[]{:S(2)}, u32[]{:S(2)}) collective-permute-start(f32[12,32,128]{2,1,0:T(8,128)S(1)} %get-tuple-element.66), channel_id=1, source_target_pairs={{8,16},{16,8},{24,32},{32,24},{40,48},{48,40},{56,64},{64,56},{72,... | collective-permute-start | bytes 589832 | tf_op jit(solution)/shard_map/ppermute | solution.py:38
  58.9 7.7 %shard_map.52 = (f32[72,80,128]{2,1,0:T(8,128)S(1)}, f32[32,32,128]{2,1,0:T(8,128)S(1)}, f32[12,32,128]{2,1,0:T(8,128)S(1)}, f32[12,32,128]{2,1,0:T(8,128)S(1)}) custom-call(f32[64,64,256]{2,1,0:T(8,128)} %u_hbm.11, f32[64,64,256]{2,1,0:T(8,128)} %f_hbm.15, f32[64,64,256]{2,1,0:T(8,128)} %m_hbm.17, f32[10,64,128]{2,1,0:T(8,128)S(1)} %copy-done.4, ...), custom_call_target="tpu_custom_call" | custom-call | flops 3000000000 | tf_op jit(solution)/shard_map/pallas_call | solution.py:575
  66.8 2.5 %collective-permute-start.10 = (f32[2,39,8,128]{3,2,1,0:T(8,128)S(1)}, f32[2,39,8,128]{3,2,1,0:T(8,128)S(1)}, u32[]{:S(2)}, u32[]{:S(2)}) collective-permute-start(f32[2,39,8,128]{3,2,1,0:T(8,128)S(1)} %get-tuple-element.52), channel_id=1, source_target_pairs={{0,1},{1,0},{2,3},{3,2},{4,5},{5,4},{6,7},{7,6},{8,9},{9,8},{10,11... | collective-permute-start | bytes 958472 | tf_op jit(solution)/shard_map/ppermute | solution.py:37
  69.3 2.1 %collective-permute-start.11 = (f32[2,39,8,128]{3,2,1,0:T(8,128)S(1)}, f32[2,39,8,128]{3,2,1,0:T(8,128)S(1)}, u32[]{:S(2)}, u32[]{:S(2)}) collective-permute-start(f32[2,39,8,128]{3,2,1,0:T(8,128)S(1)} %get-tuple-element.53), channel_id=1, source_target_pairs={{1,2},{2,1},{3,4},{4,3},{5,6},{6,5},{9,10},{10,9},{11,12},{12,11},... | collective-permute-start | bytes 958472 | tf_op jit(solution)/shard_map/ppermute | solution.py:38
  71.5 3.0 %collective-permute-start.5 = (f32[12,32,128]{2,1,0:T(8,128)S(1)}, f32[12,32,128]{2,1,0:T(8,128)S(1)}, u32[]{:S(2)}, u32[]{:S(2)}) collective-permute-start(f32[12,32,128]{2,1,0:T(8,128)S(1)} %get-tuple-element.47), channel_id=1, source_target_pairs={{8,16},{16,8},{24,32},{32,24},{40,48},{48,40},{56,64},{64,56},{72,... | collective-permute-start | bytes 589832 | tf_op jit(solution)/shard_map/ppermute | solution.py:38
  74.5 2.5 %collective-permute-start.22 = (f32[57,8,128]{2,1,0:T(8,128)S(1)}, f32[57,8,128]{2,1,0:T(8,128)S(1)}, u32[]{:S(2)}, u32[]{:S(2)}) collective-permute-start(f32[57,8,128]{2,1,0:T(8,128)S(1)} %get-tuple-element.67), channel_id=1, source_target_pairs={{0,1},{1,0},{2,3},{3,2},{4,5},{5,4},{6,7},{7,6},{8,9},{9,8},{10,11... | collective-permute-start | bytes 700424 | tf_op jit(solution)/shard_map/ppermute | solution.py:37
  77.1 2.5 %collective-permute-start.23 = (f32[57,8,128]{2,1,0:T(8,128)S(1)}, f32[57,8,128]{2,1,0:T(8,128)S(1)}, u32[]{:S(2)}, u32[]{:S(2)}) collective-permute-start(f32[57,8,128]{2,1,0:T(8,128)S(1)} %get-tuple-element.68), channel_id=1, source_target_pairs={{1,2},{2,1},{3,4},{4,3},{5,6},{6,5},{9,10},{10,9},{11,12},{12,11},... | collective-permute-start | bytes 700424 | tf_op jit(solution)/shard_map/ppermute | solution.py:38
  79.6 2.6 %collective-permute-done.5.got_o.refs_3_ = f32[12,32,128]{2,1,0:T(8,128)S(1)} collective-permute-done((f32[12,32,128]{2,1,0:T(8,128)S(1)}, f32[12,32,128]{2,1,0:T(8,128)S(1)}, u32[]{:S(2)}, u32[]{:S(2)}) %collective-permute-start.5) | collective-permute-done | bytes 196640 | tf_op jit(solution)/shard_map/ppermute | solution.py:38
  83.9 2.5 %collective-permute-start.9 = (f32[57,8,128]{2,1,0:T(8,128)S(1)}, f32[57,8,128]{2,1,0:T(8,128)S(1)}, u32[]{:S(2)}, u32[]{:S(2)}) collective-permute-start(f32[57,8,128]{2,1,0:T(8,128)S(1)} %get-tuple-element.51), channel_id=1, source_target_pairs={{1,2},{2,1},{3,4},{4,3},{5,6},{6,5},{9,10},{10,9},{11,12},{12,11},... | collective-permute-start | bytes 700424 | tf_op jit(solution)/shard_map/ppermute | solution.py:38
  86.5 4.0 %collective-permute-done.22.refs_6_ = f32[57,8,128]{2,1,0:T(8,128)S(1)} collective-permute-done((f32[57,8,128]{2,1,0:T(8,128)S(1)}, f32[57,8,128]{2,1,0:T(8,128)S(1)}, u32[]{:S(2)}, u32[]{:S(2)}) %collective-permute-start.22) | collective-permute-done | bytes 233504 | tf_op jit(solution)/shard_map/ppermute | solution.py:37
  90.4 5.2 %collective-permute-done.23.refs_7_ = f32[57,8,128]{2,1,0:T(8,128)S(1)} collective-permute-done((f32[57,8,128]{2,1,0:T(8,128)S(1)}, f32[57,8,128]{2,1,0:T(8,128)S(1)}, u32[]{:S(2)}, u32[]{:S(2)}) %collective-permute-start.23) | collective-permute-done | bytes 233504 | tf_op jit(solution)/shard_map/ppermute | solution.py:38
  95.6 4.0 %shard_map.62 = (f32[32,32,128]{2,1,0:T(8,128)S(1)}, f32[6,32,128]{2,1,0:T(8,128)S(1)}, f32[6,32,128]{2,1,0:T(8,128)S(1)}) custom-call(f32[32,32,128]{2,1,0:T(8,128)S(1)} %get-tuple-element.64.load_ref.refs_0_, f32[2,32,32,128]{3,2,1,0:T(8,128)S(1)} %copy-done.2, f32[12,32,128]{2,1,0:T(8,128)S(1)} %collective-permute-done.20.got_e.refs_2_, ...), custom_call_target="tpu_custom_call" | custom-call | flops 2000000000 | tf_op jit(solution)/shard_map/pallas_call | solution.py:575
  99.6 6.3 %collective-permute-start.24 = (f32[6,32,128]{2,1,0:T(8,128)S(1)}, f32[6,32,128]{2,1,0:T(8,128)S(1)}, u32[]{:S(2)}, u32[]{:S(2)}) collective-permute-start(f32[6,32,128]{2,1,0:T(8,128)S(1)} %get-tuple-element.70), channel_id=1, source_target_pairs={{0,8},{8,0},{16,24},{24,16},{32,40},{40,32},{48,56},{56,48},{64,72... | collective-permute-start | bytes 294920 | tf_op jit(solution)/shard_map/ppermute | solution.py:37
  107.9 7.7 %collective-permute-done.25.got_o.refs_11_ = f32[6,32,128]{2,1,0:T(8,128)S(1)} collective-permute-done((f32[6,32,128]{2,1,0:T(8,128)S(1)}, f32[6,32,128]{2,1,0:T(8,128)S(1)}, u32[]{:S(2)}, u32[]{:S(2)}) %collective-permute-start.25) | collective-permute-done | bytes 98336 | tf_op jit(solution)/shard_map/ppermute | solution.py:38
  117.6 2.5 %collective-permute-start.27 = (f32[39,8,128]{2,1,0:T(8,128)S(1)}, f32[39,8,128]{2,1,0:T(8,128)S(1)}, u32[]{:S(2)}, u32[]{:S(2)}) collective-permute-start(f32[39,8,128]{2,1,0:T(8,128)S(1)} %get-tuple-element.73), channel_id=1, source_target_pairs={{1,2},{2,1},{3,4},{4,3},{5,6},{6,5},{9,10},{10,9},{11,12},{12,11},... | collective-permute-start | bytes 479240 | tf_op jit(solution)/shard_map/ppermute | solution.py:38
  120.1 4.0 %shard_map.56 = (f32[32,32,128]{2,1,0:T(8,128)S(1)}, f32[6,32,128]{2,1,0:T(8,128)S(1)}, f32[6,32,128]{2,1,0:T(8,128)S(1)}) custom-call(f32[32,32,128]{2,1,0:T(8,128)S(1)} %get-tuple-element.44.load_ref.refs_0_, f32[2,32,32,128]{3,2,1,0:T(8,128)S(1)} %copy-done.2, f32[12,32,128]{2,1,0:T(8,128)S(1)} %collective-permute-done.4.got_e.refs_2_, ...), custom_call_target="tpu_custom_call" | custom-call | flops 2000000000 | tf_op jit(solution)/shard_map/pallas_call | solution.py:575
  126.2 7.7 %collective-permute-done.13.got_o.refs_11_ = f32[6,32,128]{2,1,0:T(8,128)S(1)} collective-permute-done((f32[6,32,128]{2,1,0:T(8,128)S(1)}, f32[6,32,128]{2,1,0:T(8,128)S(1)}, u32[]{:S(2)}, u32[]{:S(2)}) %collective-permute-start.13) | collective-permute-done | bytes 98336 | tf_op jit(solution)/shard_map/ppermute | solution.py:38
  134.5 3.2 %collective-permute-start.15 = (f32[39,8,128]{2,1,0:T(8,128)S(1)}, f32[39,8,128]{2,1,0:T(8,128)S(1)}, u32[]{:S(2)}, u32[]{:S(2)}) collective-permute-start(f32[39,8,128]{2,1,0:T(8,128)S(1)} %get-tuple-element.58), channel_id=1, source_target_pairs={{1,2},{2,1},{3,4},{4,3},{5,6},{6,5},{9,10},{10,9},{11,12},{12,11},... | collective-permute-start | bytes 479240 | tf_op jit(solution)/shard_map/ppermute | solution.py:38
  137.7 10.0 %shard_map.64 = (f32[64,64,256]{2,1,0:T(8,128)}, f32[64,64,256]{2,1,0:T(8,128)}) custom-call(f32[64,64,256]{2,1,0:T(8,128)} %f_hbm.15, f32[64,64,256]{2,1,0:T(8,128)} %m_hbm.17, f32[72,80,128]{2,1,0:T(8,128)} %copy-done, f32[32,32,128]{2,1,0:T(8,128)S(1)} %get-tuple-element.69.x_ref, f32[10,64,128]{2,1,0:T(8,128)S(1)} %copy-done.8, ...), custom_call_target="tpu_custom_call" | custom-call | flops 4000000000 | tf_op jit(solution)/shard_map/pallas_call | solution.py:575
  147.8 10.0 %shard_map.65 = (f32[64,64,256]{2,1,0:T(8,128)}, f32[64,64,256]{2,1,0:T(8,128)}) custom-call(f32[64,64,256]{2,1,0:T(8,128)} %f_hbm.15, f32[64,64,256]{2,1,0:T(8,128)} %m_hbm.17, f32[72,80,128]{2,1,0:T(8,128)} %copy-done.1, f32[32,32,128]{2,1,0:T(8,128)S(1)} %get-tuple-element.54.x_ref, ...), custom_call_target="tpu_custom_call", output_to_operand_aliasing={{0}: (22, {}), {1}: (23, {})} | custom-call | flops 4000000000 | tf_op jit(solution)/shard_map/pallas_call | solution.py:575
  (62 shorter events, 15.4 us)
Async XLA Ops:
  2.7 12.6 %collective-permute-start.16 = (f32[10,64,128]{2,1,0:T(8,128)}, f32[10,64,128]{2,1,0:T(8,128)S(1)}, u32[]{:S(2)}, u32[]{:S(2)}) collective-permute-start(f32[10,64,128]{2,1,0:T(8,128)} %get-tuple-element.59), channel_id=1, source_target_pairs={{0,8},{8,0},{16,24},{24,16},{32,40},{40,32},{48,56},{56,48},{64,72... | collective-permute-start | bytes 983048 | tf_op jit(solution)/shard_map/ppermute | solution.py:37
  3.5 12.3 %collective-permute-start.17 = (f32[10,64,128]{2,1,0:T(8,128)}, f32[10,64,128]{2,1,0:T(8,128)S(1)}, u32[]{:S(2)}, u32[]{:S(2)}) collective-permute-start(f32[10,64,128]{2,1,0:T(8,128)} %get-tuple-element.60), channel_id=1, source_target_pairs={{8,16},{16,8},{24,32},{32,24},{40,48},{48,40},{56,64},{64,56},{72,... | collective-permute-start | bytes 983048 | tf_op jit(solution)/shard_map/ppermute | solution.py:38
  10.2 13.6 %collective-permute-start = (f32[10,64,128]{2,1,0:T(8,128)}, f32[10,64,128]{2,1,0:T(8,128)S(1)}, u32[]{:S(2)}, u32[]{:S(2)}) collective-permute-start(f32[10,64,128]{2,1,0:T(8,128)} %get-tuple-element.39), channel_id=1, source_target_pairs={{0,8},{8,0},{16,24},{24,16},{32,40},{40,32},{48,56},{56,48},{64,72... | collective-permute-start | bytes 983048 | tf_op jit(solution)/shard_map/ppermute | solution.py:37
  10.3 13.6 %collective-permute-start.1 = (f32[10,64,128]{2,1,0:T(8,128)}, f32[10,64,128]{2,1,0:T(8,128)S(1)}, u32[]{:S(2)}, u32[]{:S(2)}) collective-permute-start(f32[10,64,128]{2,1,0:T(8,128)} %get-tuple-element.40), channel_id=1, source_target_pairs={{8,16},{16,8},{24,32},{32,24},{40,48},{48,40},{56,64},{64,56},{72,... | collective-permute-start | bytes 983048 | tf_op jit(solution)/shard_map/ppermute | solution.py:38
  20.5 20.0 %collective-permute-start.18 = (f32[72,8,128]{2,1,0:T(8,128)}, f32[72,8,128]{2,1,0:T(8,128)S(1)}, u32[]{:S(2)}, u32[]{:S(2)}) collective-permute-start(f32[72,8,128]{2,1,0:T(8,128)} %get-tuple-element.61), channel_id=1, source_target_pairs={{0,1},{1,0},{2,3},{3,2},{4,5},{5,4},{6,7},{7,6},{8,9},{9,8},{10,11... | collective-permute-start | bytes 884744 | tf_op jit(solution)/shard_map/ppermute | solution.py:37
  21.5 23.1 %collective-permute-start.19 = (f32[72,8,128]{2,1,0:T(8,128)}, f32[72,8,128]{2,1,0:T(8,128)S(1)}, u32[]{:S(2)}, u32[]{:S(2)}) collective-permute-start(f32[72,8,128]{2,1,0:T(8,128)} %get-tuple-element.62), channel_id=1, source_target_pairs={{1,2},{2,1},{3,4},{4,3},{5,6},{6,5},{9,10},{10,9},{11,12},{12,11},... | collective-permute-start | bytes 884744 | tf_op jit(solution)/shard_map/ppermute | solution.py:38
  29.0 23.4 %collective-permute-start.2 = (f32[72,8,128]{2,1,0:T(8,128)}, f32[72,8,128]{2,1,0:T(8,128)S(1)}, u32[]{:S(2)}, u32[]{:S(2)}) collective-permute-start(f32[72,8,128]{2,1,0:T(8,128)} %get-tuple-element.41), channel_id=1, source_target_pairs={{0,1},{1,0},{2,3},{3,2},{4,5},{5,4},{6,7},{7,6},{8,9},{9,8},{10,11... | collective-permute-start | bytes 884744 | tf_op jit(solution)/shard_map/ppermute | solution.py:37
  31.1 27.8 %collective-permute-start.3 = (f32[72,8,128]{2,1,0:T(8,128)}, f32[72,8,128]{2,1,0:T(8,128)S(1)}, u32[]{:S(2)}, u32[]{:S(2)}) collective-permute-start(f32[72,8,128]{2,1,0:T(8,128)} %get-tuple-element.42), channel_id=1, source_target_pairs={{1,2},{2,1},{3,4},{4,3},{5,6},{6,5},{9,10},{10,9},{11,12},{12,11},... | collective-permute-start | bytes 884744 | tf_op jit(solution)/shard_map/ppermute | solution.py:38
  36.7 30.0 %collective-permute-start.6 = (f32[2,8,32,128]{3,2,1,0:T(8,128)}, f32[2,8,32,128]{3,2,1,0:T(8,128)S(1)}, u32[]{:S(2)}, u32[]{:S(2)}) collective-permute-start(f32[2,8,32,128]{3,2,1,0:T(8,128)} %get-tuple-element.48), channel_id=1, source_target_pairs={{0,8},{8,0},{16,24},{24,16},{32,40},{40,32},{48,56},{56,48},{64,72... | collective-permute-start | bytes 786440 | tf_op jit(solution)/shard_map/ppermute | solution.py:37
  40.5 18.4 %copy-start.4 = (f32[10,64,128]{2,1,0:T(8,128)S(1)}, f32[10,64,128]{2,1,0:T(8,128)}, u32[]{:S(2)}) copy-start(f32[10,64,128]{2,1,0:T(8,128)} %copy-done.3) | copy-start | bytes 983044
  40.5 18.4 %copy-start.6 = (f32[10,64,128]{2,1,0:T(8,128)S(1)}, f32[10,64,128]{2,1,0:T(8,128)}, u32[]{:S(2)}) copy-start(f32[10,64,128]{2,1,0:T(8,128)} %copy-done.5) | copy-start | bytes 983044
  40.5 26.2 %collective-permute-start.7 = (f32[2,8,32,128]{3,2,1,0:T(8,128)}, f32[2,8,32,128]{3,2,1,0:T(8,128)S(1)}, u32[]{:S(2)}, u32[]{:S(2)}) collective-permute-start(f32[2,8,32,128]{3,2,1,0:T(8,128)} %get-tuple-element.49), channel_id=1, source_target_pairs={{8,16},{16,8},{24,32},{32,24},{40,48},{48,40},{56,64},{64,56},{72,... | collective-permute-start | bytes 786440 | tf_op jit(solution)/shard_map/ppermute | solution.py:38
  52.2 22.2 %copy-start = (f32[72,80,128]{2,1,0:T(8,128)}, f32[72,80,128]{2,1,0:T(8,128)S(1)}, u32[]{:S(2)}) copy-start(f32[72,80,128]{2,1,0:T(8,128)S(1)} %get-tuple-element.63.v_ref) | copy-start | bytes 8847364
  52.3 19.2 %collective-permute-start.20 = (f32[12,32,128]{2,1,0:T(8,128)S(1)}, f32[12,32,128]{2,1,0:T(8,128)S(1)}, u32[]{:S(2)}, u32[]{:S(2)}) collective-permute-start(f32[12,32,128]{2,1,0:T(8,128)S(1)} %get-tuple-element.65), channel_id=1, source_target_pairs={{0,8},{8,0},{16,24},{24,16},{32,40},{40,32},{48,56},{56,48},{64,72... | collective-permute-start | bytes 589832 | tf_op jit(solution)/shard_map/ppermute | solution.py:37
  52.4 22.0 %collective-permute-start.21 = (f32[12,32,128]{2,1,0:T(8,128)S(1)}, f32[12,32,128]{2,1,0:T(8,128)S(1)}, u32[]{:S(2)}, u32[]{:S(2)}) collective-permute-start(f32[12,32,128]{2,1,0:T(8,128)S(1)} %get-tuple-element.66), channel_id=1, source_target_pairs={{8,16},{16,8},{24,32},{32,24},{40,48},{48,40},{56,64},{64,56},{72,... | collective-permute-start | bytes 589832 | tf_op jit(solution)/shard_map/ppermute | solution.py:38
  66.6 15.7 %copy-start.1 = (f32[72,80,128]{2,1,0:T(8,128)}, f32[72,80,128]{2,1,0:T(8,128)S(1)}, u32[]{:S(2)}) copy-start(f32[72,80,128]{2,1,0:T(8,128)S(1)} %get-tuple-element.43.v_ref) | copy-start | bytes 8847364
  66.6 10.5 %collective-permute-start.4 = (f32[12,32,128]{2,1,0:T(8,128)S(1)}, f32[12,32,128]{2,1,0:T(8,128)S(1)}, u32[]{:S(2)}, u32[]{:S(2)}) collective-permute-start(f32[12,32,128]{2,1,0:T(8,128)S(1)} %get-tuple-element.46), channel_id=1, source_target_pairs={{0,8},{8,0},{16,24},{24,16},{32,40},{40,32},{48,56},{56,48},{64,72... | collective-permute-start | bytes 589832 | tf_op jit(solution)/shard_map/ppermute | solution.py:37
  66.8 17.1 %collective-permute-start.10 = (f32[2,39,8,128]{3,2,1,0:T(8,128)S(1)}, f32[2,39,8,128]{3,2,1,0:T(8,128)S(1)}, u32[]{:S(2)}, u32[]{:S(2)}) collective-permute-start(f32[2,39,8,128]{3,2,1,0:T(8,128)S(1)} %get-tuple-element.52), channel_id=1, source_target_pairs={{0,1},{1,0},{2,3},{3,2},{4,5},{5,4},{6,7},{7,6},{8,9},{9,8},{10,11... | collective-permute-start | bytes 958472 | tf_op jit(solution)/shard_map/ppermute | solution.py:37
  69.3 17.1 %collective-permute-start.11 = (f32[2,39,8,128]{3,2,1,0:T(8,128)S(1)}, f32[2,39,8,128]{3,2,1,0:T(8,128)S(1)}, u32[]{:S(2)}, u32[]{:S(2)}) collective-permute-start(f32[2,39,8,128]{3,2,1,0:T(8,128)S(1)} %get-tuple-element.53), channel_id=1, source_target_pairs={{1,2},{2,1},{3,4},{4,3},{5,6},{6,5},{9,10},{10,9},{11,12},{12,11},... | collective-permute-start | bytes 958472 | tf_op jit(solution)/shard_map/ppermute | solution.py:38
  71.5 10.7 %collective-permute-start.5 = (f32[12,32,128]{2,1,0:T(8,128)S(1)}, f32[12,32,128]{2,1,0:T(8,128)S(1)}, u32[]{:S(2)}, u32[]{:S(2)}) collective-permute-start(f32[12,32,128]{2,1,0:T(8,128)S(1)} %get-tuple-element.47), channel_id=1, source_target_pairs={{8,16},{16,8},{24,32},{32,24},{40,48},{48,40},{56,64},{64,56},{72,... | collective-permute-start | bytes 589832 | tf_op jit(solution)/shard_map/ppermute | solution.py:38
  74.5 15.9 %collective-permute-start.22 = (f32[57,8,128]{2,1,0:T(8,128)S(1)}, f32[57,8,128]{2,1,0:T(8,128)S(1)}, u32[]{:S(2)}, u32[]{:S(2)}) collective-permute-start(f32[57,8,128]{2,1,0:T(8,128)S(1)} %get-tuple-element.67), channel_id=1, source_target_pairs={{0,1},{1,0},{2,3},{3,2},{4,5},{5,4},{6,7},{7,6},{8,9},{9,8},{10,11... | collective-permute-start | bytes 700424 | tf_op jit(solution)/shard_map/ppermute | solution.py:37
  77.1 18.5 %collective-permute-start.23 = (f32[57,8,128]{2,1,0:T(8,128)S(1)}, f32[57,8,128]{2,1,0:T(8,128)S(1)}, u32[]{:S(2)}, u32[]{:S(2)}) collective-permute-start(f32[57,8,128]{2,1,0:T(8,128)S(1)} %get-tuple-element.68), channel_id=1, source_target_pairs={{1,2},{2,1},{3,4},{4,3},{5,6},{6,5},{9,10},{10,9},{11,12},{12,11},... | collective-permute-start | bytes 700424 | tf_op jit(solution)/shard_map/ppermute | solution.py:38
  82.3 37.8 %collective-permute-start.8 = (f32[57,8,128]{2,1,0:T(8,128)S(1)}, f32[57,8,128]{2,1,0:T(8,128)S(1)}, u32[]{:S(2)}, u32[]{:S(2)}) collective-permute-start(f32[57,8,128]{2,1,0:T(8,128)S(1)} %get-tuple-element.50), channel_id=1, source_target_pairs={{0,1},{1,0},{2,3},{3,2},{4,5},{5,4},{6,7},{7,6},{8,9},{9,8},{10,11... | collective-permute-start | bytes 700424 | tf_op jit(solution)/shard_map/ppermute | solution.py:37
  83.9 36.2 %collective-permute-start.9 = (f32[57,8,128]{2,1,0:T(8,128)S(1)}, f32[57,8,128]{2,1,0:T(8,128)S(1)}, u32[]{:S(2)}, u32[]{:S(2)}) collective-permute-start(f32[57,8,128]{2,1,0:T(8,128)S(1)} %get-tuple-element.51), channel_id=1, source_target_pairs={{1,2},{2,1},{3,4},{4,3},{5,6},{6,5},{9,10},{10,9},{11,12},{12,11},... | collective-permute-start | bytes 700424 | tf_op jit(solution)/shard_map/ppermute | solution.py:38
  99.6 8.2 %collective-permute-start.24 = (f32[6,32,128]{2,1,0:T(8,128)S(1)}, f32[6,32,128]{2,1,0:T(8,128)S(1)}, u32[]{:S(2)}, u32[]{:S(2)}) collective-permute-start(f32[6,32,128]{2,1,0:T(8,128)S(1)} %get-tuple-element.70), channel_id=1, source_target_pairs={{0,8},{8,0},{16,24},{24,16},{32,40},{40,32},{48,56},{56,48},{64,72... | collective-permute-start | bytes 294920 | tf_op jit(solution)/shard_map/ppermute | solution.py:37
  105.9 9.6 %collective-permute-start.25 = (f32[6,32,128]{2,1,0:T(8,128)S(1)}, f32[6,32,128]{2,1,0:T(8,128)S(1)}, u32[]{:S(2)}, u32[]{:S(2)}) collective-permute-start(f32[6,32,128]{2,1,0:T(8,128)S(1)} %get-tuple-element.71), channel_id=1, source_target_pairs={{8,16},{16,8},{24,32},{32,24},{40,48},{48,40},{56,64},{64,56},{72,... | collective-permute-start | bytes 294920 | tf_op jit(solution)/shard_map/ppermute | solution.py:38
  115.6 22.1 %collective-permute-start.26 = (f32[39,8,128]{2,1,0:T(8,128)S(1)}, f32[39,8,128]{2,1,0:T(8,128)S(1)}, u32[]{:S(2)}, u32[]{:S(2)}) collective-permute-start(f32[39,8,128]{2,1,0:T(8,128)S(1)} %get-tuple-element.72), channel_id=1, source_target_pairs={{0,1},{1,0},{2,3},{3,2},{4,5},{5,4},{6,7},{7,6},{8,9},{9,8},{10,11... | collective-permute-start | bytes 479240 | tf_op jit(solution)/shard_map/ppermute | solution.py:37
  117.6 20.2 %collective-permute-start.27 = (f32[39,8,128]{2,1,0:T(8,128)S(1)}, f32[39,8,128]{2,1,0:T(8,128)S(1)}, u32[]{:S(2)}, u32[]{:S(2)}) collective-permute-start(f32[39,8,128]{2,1,0:T(8,128)S(1)} %get-tuple-element.73), channel_id=1, source_target_pairs={{1,2},{2,1},{3,4},{4,3},{5,6},{6,5},{9,10},{10,9},{11,12},{12,11},... | collective-permute-start | bytes 479240 | tf_op jit(solution)/shard_map/ppermute | solution.py:38
  124.1 2.0 %collective-permute-start.12 = (f32[6,32,128]{2,1,0:T(8,128)S(1)}, f32[6,32,128]{2,1,0:T(8,128)S(1)}, u32[]{:S(2)}, u32[]{:S(2)}) collective-permute-start(f32[6,32,128]{2,1,0:T(8,128)S(1)} %get-tuple-element.55), channel_id=1, source_target_pairs={{0,8},{8,0},{16,24},{24,16},{32,40},{40,32},{48,56},{56,48},{64,72... | collective-permute-start | bytes 294920 | tf_op jit(solution)/shard_map/ppermute | solution.py:37
  124.2 9.6 %collective-permute-start.13 = (f32[6,32,128]{2,1,0:T(8,128)S(1)}, f32[6,32,128]{2,1,0:T(8,128)S(1)}, u32[]{:S(2)}, u32[]{:S(2)}) collective-permute-start(f32[6,32,128]{2,1,0:T(8,128)S(1)} %get-tuple-element.56), channel_id=1, source_target_pairs={{8,16},{16,8},{24,32},{32,24},{40,48},{48,40},{56,64},{64,56},{72,... | collective-permute-start | bytes 294920 | tf_op jit(solution)/shard_map/ppermute | solution.py:38
  133.9 13.8 %collective-permute-start.14 = (f32[39,8,128]{2,1,0:T(8,128)S(1)}, f32[39,8,128]{2,1,0:T(8,128)S(1)}, u32[]{:S(2)}, u32[]{:S(2)}) collective-permute-start(f32[39,8,128]{2,1,0:T(8,128)S(1)} %get-tuple-element.57), channel_id=1, source_target_pairs={{0,1},{1,0},{2,3},{3,2},{4,5},{5,4},{6,7},{7,6},{8,9},{9,8},{10,11... | collective-permute-start | bytes 479240 | tf_op jit(solution)/shard_map/ppermute | solution.py:37
  134.5 13.3 %collective-permute-start.15 = (f32[39,8,128]{2,1,0:T(8,128)S(1)}, f32[39,8,128]{2,1,0:T(8,128)S(1)}, u32[]{:S(2)}, u32[]{:S(2)}) collective-permute-start(f32[39,8,128]{2,1,0:T(8,128)S(1)} %get-tuple-element.58), channel_id=1, source_target_pairs={{1,2},{2,1},{3,4},{4,3},{5,6},{6,5},{9,10},{10,9},{11,12},{12,11},... | collective-permute-start | bytes 479240 | tf_op jit(solution)/shard_map/ppermute | solution.py:38
  (7 other events, 48.4 us)

commit v3 on v2

v3 whole, which is shorter than its diff:
```python
import functools

import jax
import jax.numpy as jnp
from jax import lax
from jax.experimental import pallas as pl
from jax.experimental.pallas import tpu as pltpu
from jax.sharding import PartitionSpec as P


LANES = 128
INNER = 13
FINE = 4
TILE = 8
DEEP = 8
SECOND = 6
FIRST_SWEEPS = DEEP + 1
LAST_SWEEPS = INNER - FIRST_SWEEPS
CHUNKS = 4
FAR = 60
LOAD = 39
COST = 500_000_000


def swaps(count, first):
    pairs = []
    for i in range(first, count - 1, 2):
        pairs += [(i, i + 1), (i + 1, i)]
    return pairs


def swap(axis, even, odd):
    count = lax.axis_size(axis)
    return (
        lax.ppermute(even, axis, swaps(count, 0)),
        lax.ppermute(odd, axis, swaps(count, 1)),
    )


def place(axis):
    at, count = lax.axis_index(axis), lax.axis_size(axis)
    return lax.rem(at, 2) == 0, at > 0, at < count - 1


def roll(value, shift, axis):
    return pltpu.roll(value, shift % value.shape[axis], axis)


def sublane(value):
    return lax.broadcasted_iota(jnp.int32, value.shape, value.ndim - 2)


def by_side(even, got_even, got_odd):
    low = jnp.where(even, got_odd, got_even)
    high = jnp.where(even, got_even, got_odd)
    return low, high


def weight(mass, inside):
    return jnp.where(inside, 0.8 / (4.0 + mass), 0.0)


def new_value(here, left, right, up, down, load, w):
    return 0.2 * here + w * (load + ((up + down) + (left + right)))


def edges(even, rows, depth):
    return jnp.where(even, rows - depth, 0), jnp.where(even, 0, rows - depth)


def packed(u, f, m, v, side):
    s = sublane(u)
    if side:
        f_m = jnp.where(s >= 2, roll(f, -4, 1), roll(m, -6, 1))
        return jnp.where(s >= 6, u, jnp.where(s >= 4, roll(v, -1, 1), f_m))
    f_m = jnp.where(s < 6, roll(f, 4, 1), roll(m, 6, 1))
    return jnp.where(s < 2, u, jnp.where(s < 4, roll(v, 1, 1), f_m))


def swept(u, f, w):
    zero = jnp.zeros((1,) + u.shape[1:], jnp.float32)
    up = jnp.concatenate([zero, u[:-1]], axis=0)
    down = jnp.concatenate([u[1:], zero], axis=0)
    return new_value(u, roll(u, 1, 1), roll(u, -1, 1), up, down, f, w)


def put_sides(even, make, even_ref, odd_ref):
    low, high = make(0), make(1)
    even_ref[...] = jnp.where(even, high, low)
    odd_ref[...] = jnp.where(even, low, high)


def first_kernel(chain, u_hbm, f_hbm, m_hbm, *refs):
    even_b, even_l = place("band")[0], place("lane")[0]
    rows, columns, _ = m_hbm.shape
    arrays = (u_hbm, f_hbm, m_hbm)
    outs, (tiles, sems) = refs[:-2], refs[-2:]
    groups = len(outs) // 4
    tile_copies, copies = [], []
    for g in range(groups):
        at = pl.ds(g * LANES, LANES)
        for side in range(2):
            for part, hbm in enumerate(arrays):
                copy = pltpu.make_async_copy(
                    hbm.at[:, pl.ds(side * (columns - TILE), TILE), at],
                    tiles.at[g, 3 * side + part],
                    sems.at[12 * g + 3 * side + part],
                )
                copy.start()
                tile_copies.append(copy)
        for side, target in enumerate(outs[4 * g : 4 * g + 2]):
            for part, (hbm, depth, first) in enumerate(zip(arrays, (4, 3, 3), (0, 4, 7))):
                start = edges(even_b, rows, depth)[side]
                copy = pltpu.make_async_copy(
                    hbm.at[pl.ds(start, depth), :, at],
                    target.at[pl.ds(first, depth)],
                    sems.at[12 * g + 6 + 3 * side + part],
                )
                copy.start()
                copies.append(copy)
    for g in range(groups):
        for copy in tile_copies[6 * g : 6 * g + 6]:
            copy.wait()

        def make(side, g=g):
            u, f, m = [tiles[g, 3 * side + part] for part in range(3)]
            return packed(u, f, m, swept(u, f, 0.8 / (4.0 + m)), side)

        put_sides(even_l, make, *outs[4 * g + 2 : 4 * g + 4])
    for copy in copies:
        copy.wait()


def mass_place(group, k, half):
    return 10 + group * (DEEP // 2) + k // 2, k % 2 * half


def mass_strip(ref, group, start, width, half):
    places = [mass_place(group, k, half) for k in range(DEEP)]
    return jnp.concatenate([ref[r, pl.ds(c + start, width), :][None] for r, c in places], axis=0)


def load_kernel(chain, u_hbm, f_hbm, m_hbm, *refs):
    even_b, even_l = place("band")[0], place("lane")[0]
    owns, (mass_ref, even_ref, odd_ref, lane_e, lane_o, pairs, sems) = refs[:-7], refs[-7:]
    groups, half_rows, half = mass_ref.shape[0], mass_ref.shape[1], mass_ref.shape[2]
    rows, columns = 2 * half_rows, 2 * half
    even_columns, odd_columns = pl.ds(0, half, 2), pl.ds(1, half, 2)
    copies = [None] * len(owns)
    for g in reversed(range(groups)):
        for part, hbm in ((2, m_hbm), (1, f_hbm), (0, u_hbm)):
            k = 3 * g + part
            copies[k] = pltpu.make_async_copy(hbm.at[:, :, pl.ds(g * LANES, LANES)], owns[k], sems.at[k])
            copies[k].start()
    for g in reversed(range(groups)):
        m_ref = owns[3 * g + 2]
        copies[3 * g + 2].wait()

        def restrict(k, _, g=g, m_ref=m_ref):
            pairs[k] = m_ref[2 * k] + m_ref[2 * k + 1]
            mass_ref[g, k] = 0.5 * (pairs[k, even_columns, :] + pairs[k, odd_columns, :])
            return 0

        lax.fori_loop(0, half_rows, restrict, 0, unroll=2)
        for side, target in enumerate((even_ref, odd_ref)):
            start = edges(even_b, half_rows, DEEP)[side]
            for k in range(DEEP):
                r, c = mass_place(g, k, half)
                target[r, pl.ds(c, half), :] = mass_ref[g, start + k]
    own = owns[3 * groups - 3 :]
    for copy in copies[3 * groups - 3 : 3 * groups - 1]:
        copy.wait()
    for side, target in enumerate((even_ref, odd_ref)):
        for ref, depth, at in zip(own, (4, 3, 3), (0, 4, 7)):
            target[pl.ds(at, depth)] = ref[pl.ds(edges(even_b, rows, depth)[side], depth)]

    def make(side):
        at = pl.ds(side * (columns - TILE), TILE)
        u, f, m = [ref[:, at, :] for ref in own]
        at = pl.ds(side * (half - TILE), TILE)
        parts = [packed(u, f, m, swept(u, f, 0.8 / (4.0 + m)), side)]
        return jnp.concatenate(parts + [mass_ref[g, :, at, :] for g in range(groups)], axis=0)

    put_sides(even_l, make, lane_e, lane_o)
    for g in range(groups - 1):
        for copy in copies[3 * g : 3 * g + 2]:
            copy.wait()


def fold(low, high, side):
    depth = DEEP
    s = sublane(low[0])
    merged = []
    for r in range(1, depth):
        if side:
            merged.append(jnp.where(s >= depth - r, low[r], roll(high[r - 1], -r, 0))[None])
        else:
            merged.append(jnp.where(s < r, low[r], roll(high[r - 1], r, 0))[None])
    return jnp.concatenate(merged, axis=0)


def unfold(got_e, got_o, corner_e, corner_o, even, rows, write):
    def own(k, _):
        low, high = by_side(even, got_e(k), got_o(k))
        write(DEEP + k, low, high)
        return 0

    lax.fori_loop(0, rows, own, 0, unroll=4)
    for r in range(1, DEEP):
        low, high = by_side(even, corner_e(r - 1), corner_o(r - 1))
        write(r, low, high)
        write(DEEP + rows - 1 + r, roll(low, r, 0), roll(high, -r, 0))


CORNER = FINE + 1


def fine_corner_kernel(chain, u_ref, f_ref, m_ref, got_e, got_o, *refs):
    even_ref, odd_ref = refs[-2:]
    even_b, low_b, high_b = place("band")
    rows, columns = u_ref.shape[0], u_ref.shape[1]
    zero = jnp.zeros((1, TILE, LANES), jnp.float32)

    def make(side):
        at = pl.ds(side * (columns - TILE), TILE)
        low, high = by_side(even_b, got_e[:, at, :], got_o[:, at, :])
        parts = []
        for top, inside, halo in ((True, low_b, low), (False, high_b, high)):
            near = pl.ds(0 if top else rows - 2, 2)
            own = [ref[near, at, :] for ref in (u_ref, f_ref, m_ref)]
            h = [halo[:4], halo[4:7], halo[7:10]]
            if top:
                u, f, m = (
                    jnp.concatenate([h[0], own[0]], axis=0),
                    jnp.concatenate([zero, h[1], own[1]], axis=0),
                    jnp.concatenate([zero, h[2], own[2]], axis=0),
                )
            else:
                u, f, m = (
                    jnp.concatenate([own[0], h[0]], axis=0),
                    jnp.concatenate([own[1], h[1], zero], axis=0),
                    jnp.concatenate([own[2], h[2], zero], axis=0),
                )
            w = 0.8 / (4.0 + m)
            if top:
                w = jnp.concatenate([jnp.where(inside, w[:4], 0.0), w[4:]], axis=0)
            else:
                w = jnp.concatenate([w[:2], jnp.where(inside, w[2:], 0.0)], axis=0)
            message = packed(u, f, m, swept(u, f, w), side)
            parts.append(message[:CORNER] if top else message[1:])
        return jnp.concatenate(parts, axis=0)

    put_sides(place("lane")[0], make, even_ref, odd_ref)


def fine_lane_rows(rows, lanes, even, write):
    lane_e, lane_o, corner_e, corner_o = lanes

    def own(r, _):
        low, high = by_side(even, lane_e[r - FINE], lane_o[r - FINE])
        write(r, low, high)
        return 0

    for k in range(CORNER):
        for r, at in ((k, k), (rows + FINE - 1 + k, CORNER + k)):
            low, high = by_side(even, corner_e[at], corner_o[at])
            write(r, low, high)
    lax.fori_loop(CORNER, rows + FINE - 1, own, 0, unroll=2)


def fine_halo(rows, columns, got_e, got_o, lanes, load, w):
    even_b, low_b, high_b = place("band")
    even_l, low_l, high_l = place("lane")
    own = pl.ds(TILE, columns)
    low_rows, high_rows = by_side(even_b, got_e[4:10], got_o[4:10])
    load[1:4, own, :] = low_rows[:3]
    w[1:4, own, :] = weight(low_rows[3:], low_b)
    load[pl.ds(FINE + rows, 3), own, :] = high_rows[:3]
    w[pl.ds(FINE + rows, 3), own, :] = weight(high_rows[3:], high_b)

    def write(r, low, high):
        s = sublane(low)
        inside_row = ((r >= FINE) | low_b) & ((r < FINE + rows) | high_b)
        load[r, pl.ds(0, TILE), :] = roll(low, 4, 0)
        load[r, pl.ds(TILE + columns, TILE), :] = roll(high, -4, 0)
        w[r, pl.ds(0, TILE), :] = weight(roll(low, 6, 0), (s >= 6) & inside_row & low_l)
        w[r, pl.ds(TILE + columns, TILE), :] = weight(
            roll(high, -6, 0), (s < 2) & inside_row & high_l
        )

    fine_lane_rows(rows, lanes, even_l, write)


def own_fields(f_ref, m_ref, load, w):
    rows, columns = m_ref.shape[0], m_ref.shape[1]
    own = pl.ds(TILE, columns)

    def row(r, _):
        load[FINE + r, own, :] = f_ref[r]
        w[FINE + r, own, :] = 0.8 / (4.0 + m_ref[r])
        return 0

    lax.fori_loop(0, rows, row, 0, unroll=2)


def sweep(source, target, load, w, first, last):
    def row(r, carry):
        up, here = carry
        down = source[r + 1]
        target[r] = new_value(here, roll(here, 1, 0), roll(here, -1, 0), up, down, load[r], w[r])
        return here, down

    lax.fori_loop(first, last, row, (source[first - 1], source[first]), unroll=2)


def before_kernel(
    chain, u_ref, f_ref, m_own, got_e, got_o, lane_e, lane_o, corner_e, corner_o,
    v_ref, load_ref, even_ref, odd_ref, a, b, load, w, pairs,
):
    even_b, even_l = place("band")[0], place("lane")[0]
    rows, columns = m_own.shape[0], m_own.shape[1]
    half_columns = columns // 2
    own = pl.ds(TILE, columns)
    left, right = pl.ds(0, TILE), pl.ds(TILE + columns, TILE)
    lanes = (lane_e, lane_o, corner_e, corner_o)
    own_fields(f_ref, m_own, load, w)
    fine_halo(rows, columns, got_e, got_o, lanes, load, w)
    low_rows, high_rows = by_side(even_b, got_e[:4], got_o[:4])
    a[:4, own, :] = low_rows
    a[pl.ds(FINE + rows, 4), own, :] = high_rows

    def copy_row(r, _):
        a[FINE + r, own, :] = u_ref[r]
        return 0

    lax.fori_loop(0, rows, copy_row, 0, unroll=2)

    def put_lane(r, low, high):
        a[r, left, :] = low
        a[r, right, :] = high

    fine_lane_rows(rows, lanes, even_l, put_lane)
    end = rows + 2 * FINE
    sweep(a, b, load, w, 1, end - 1)

    def mend(r, low, high):
        s = sublane(low)
        b[r, left, :] = jnp.where(s == 7, b[r, left, :], roll(low, 1, 0))
        b[r, right, :] = jnp.where(s == 0, b[r, right, :], roll(high, -1, 0))

    fine_lane_rows(rows, lanes, even_l, mend)
    sweep(b, a, load, w, 2, end - 2)
    sweep(a, b, load, w, 3, end - 3)

    def defect_of(i, up, here, down):
        around = (up + down) + (roll(here, 1, 0) + roll(here, -1, 0))
        value = lax.slice_in_dim(load[FINE + i] + around, TILE, TILE + columns, axis=0)
        mine = lax.slice_in_dim(here, TILE, TILE + columns, axis=0)
        return value - (4.0 + m_own[i]) * mine

    even_columns, odd_columns = pl.ds(0, half_columns, 2), pl.ds(1, half_columns, 2)

    def restrict(k, carry):
        up, here = carry
        i = 2 * k
        middle, down = b[FINE + i + 1], b[FINE + i + 2]
        first = defect_of(i, up, here, middle)
        second = defect_of(i + 1, here, middle, down)
        v_ref[FINE + i] = here
        v_ref[FINE + i + 1] = middle
        pairs[k] = first + second
        load_ref[k] = 0.5 * (pairs[k, even_columns, :] + pairs[k, odd_columns, :])
        return middle, down

    lax.fori_loop(0, rows // 2, restrict, (b[FINE - 1], b[FINE]))
    v_ref[FINE - 1] = b[FINE - 1]
    v_ref[FINE + rows] = b[FINE + rows]
    for r in range(FINE - 1):
        v_ref[r] = jnp.zeros_like(b[0])
        v_ref[end - 1 - r] = jnp.zeros_like(b[0])
    for side, target in enumerate((even_ref, odd_ref)):
        start = edges(even_b, rows // 2, DEEP)[side]
        target[:DEEP] = load_ref[pl.ds(start, DEEP)]
        start = FINE + (jnp.where(even_b, rows - 3, 1) if side == 0 else jnp.where(even_b, 1, rows - 3))
        for k in range(4):
            at = pl.ds(TILE + k % 2 * half_columns, half_columns)
            target[DEEP + k] = v_ref[start + k // 2, at, :]


def coarse_pack_kernel(chain, load_ref, v_ref, got_e, got_o, mass_e, mass_o, *refs):
    even_ref, odd_ref = refs[-2:]
    even_b, even_l = place("band")[0], place("lane")[0]
    half, columns = got_e.shape[1], v_ref.shape[1] - 2 * TILE

    def make(side):
        at = pl.ds(side * (half - TILE), TILE)
        tile = pl.ds(TILE + side * (columns - TILE), TILE)
        quarter, first = v_ref.shape[0] // 4, 5 if side else 1
        turned = [
            roll(v_ref[pl.ds(g * quarter, quarter), tile, :], 2 * g - first, 1) for g in range(4)
        ]
        s = sublane(turned[0])
        v = jnp.where(
            s < 4, jnp.where(s < 2, turned[0], turned[1]), jnp.where(s < 6, turned[2], turned[3])
        )
        low, high = by_side(even_b, got_e[:, at, :], got_o[:, at, :])
        load = fold(low[:DEEP], high[:DEEP], side)
        below, above = low[DEEP + 2 + side], high[DEEP + side]
        s = sublane(below)
        keep = s >= 4 if side else s < 4
        second = jnp.where(keep, below, roll(above, 4, 0))[None]
        start = side * (half - TILE)
        low, high = by_side(
            even_b, *[mass_strip(ref, chain, start, TILE, half) for ref in (mass_e, mass_o)]
        )
        return jnp.concatenate([load_ref[:, at, :], v, load, fold(low, high, side), second], axis=0)

    put_sides(even_l, make, even_ref, odd_ref)


def coarse_fields(
    group, load_ref, mass_ref, load_e, load_o, mass_e, mass_o, load_lane_e, load_lane_o, mass_lane_e, mass_lane_o, load, w
):
    even_b, low_b, high_b = place("band")
    even_l, low_l, high_l = place("lane")
    rows, columns = load_ref.shape[0], load_ref.shape[1]
    own = pl.ds(TILE, columns)

    def copy_row(r, _):
        load[DEEP + r, own, :] = load_ref[r]
        w[DEEP + r, own, :] = 0.8 / (4.0 + mass_ref[group, r])
        return 0

    lax.fori_loop(0, rows, copy_row, 0, unroll=4)
    low, high = by_side(even_b, load_e[:DEEP], load_o[:DEEP])
    load[:DEEP, own, :] = low
    load[pl.ds(DEEP + rows, DEEP), own, :] = high
    low, high = by_side(
        even_b, *[mass_strip(ref, group, 0, columns, columns) for ref in (mass_e, mass_o)]
    )
    w[:DEEP, own, :] = weight(low, low_b)
    w[pl.ds(DEEP + rows, DEEP), own, :] = weight(high, high_b)
    left, right = pl.ds(0, TILE), pl.ds(TILE + columns, TILE)

    def put_load(r, low, high):
        load[r, left, :] = low
        load[r, right, :] = high

    def put_weight(r, low, high):
        inside_row = ((r >= DEEP) | low_b) & ((r < DEEP + rows) | high_b)
        w[r, left, :] = weight(low, inside_row & low_l)
        w[r, right, :] = weight(high, inside_row & high_l)

    first = load_lane_e.shape[0] - 2 * DEEP + 1
    second = first + DEEP - 1
    base = (2 + group) * rows
    unfold(
        lambda k: load_lane_e[k], lambda k: load_lane_o[k],
        lambda k: load_lane_e[first + k], lambda k: load_lane_o[first + k], even_l, rows, put_load,
    )
    unfold(
        lambda k: mass_lane_e[base + k], lambda k: mass_lane_o[base + k],
        lambda k: load_lane_e[second + k], lambda k: load_lane_o[second + k], even_l, rows, put_weight,
    )
    zero = jnp.zeros((TILE, LANES), jnp.float32)
    for r in (0, rows + 2 * DEEP - 1):
        put_load(r, zero, zero)
        w[r, left, :] = zero
        w[r, right, :] = zero


def coarse_kernel(chain, *refs):
    fields, (x_ref, even_ref, odd_ref, a, b, load, w) = refs[:10], refs[10:]
    rows, columns = x_ref.shape[0], x_ref.shape[1]
    coarse_fields(chain, *fields, load, w)
    total = rows + 2 * DEEP

    def first(r, _):
        a[r] = w[r] * load[r]
        return 0

    lax.fori_loop(0, total, first, 0, unroll=4)
    source, target = a, b
    for step in range(1, FIRST_SWEEPS):
        sweep(source, target, load, w, step, total - step)
        source, target = target, source

    def out(r, _):
        x_ref[r] = source[DEEP + r, pl.ds(TILE, columns), :]
        return 0

    lax.fori_loop(0, rows, out, 0, unroll=4)
    for side, target in enumerate((even_ref, odd_ref)):
        start = edges(place("band")[0], rows, SECOND)[side]
        target[...] = x_ref[pl.ds(start, SECOND)]


def value_pack_kernel(chain, x_ref, got_e, got_o, *refs):
    even_ref, odd_ref = refs[-2:]
    even_b, even_l = place("band")[0], place("lane")[0]
    zero = jnp.zeros((DEEP - SECOND, TILE, LANES), jnp.float32)

    def make(side):
        at = pl.ds(side * (got_e.shape[1] - TILE), TILE)
        low, high = by_side(even_b, got_e[:, at, :], got_o[:, at, :])
        low, high = jnp.concatenate([zero, low], axis=0), jnp.concatenate([high, zero], axis=0)
        return jnp.concatenate([x_ref[:, at, :], fold(low, high, side)], axis=0)

    put_sides(even_l, make, even_ref, odd_ref)


def after_kernel(
    chain, f_ref, m_own, v_ref, x_ref, fine_e, fine_o, lane_e, lane_o, corner_e, corner_o, *refs
):
    fields, (value_e, value_o, value_lane_e, value_lane_o), rest = refs[:10], refs[10:14], refs[14:]
    u_hbm, d_hbm, a, b, load, w, x, y, coarse_load, coarse_w, spread, sems = rest[-12:]
    coarse_e, coarse_o, _, _, coarse_lane_e, coarse_lane_o = fields[2:8]
    even_b, even_l = place("band")[0], place("lane")[0]
    rows, columns = m_own.shape[0], m_own.shape[1]
    half_rows, half_columns = rows // 2, columns // 2
    layers = pl.ds(chain * LANES, LANES)
    fine_own = pl.ds(TILE, columns)
    left, right = pl.ds(0, TILE), pl.ds(TILE + columns, TILE)
    coarse_fields(chain, *fields, coarse_load, coarse_w)
    own = pl.ds(TILE, half_columns)
    total = half_rows + 2 * DEEP
    low, high = by_side(even_b, value_e[...], value_o[...])
    x[DEEP - SECOND : DEEP, own, :] = low
    x[pl.ds(DEEP + half_rows, SECOND), own, :] = high

    def coarse_copy(r, _):
        x[DEEP + r, own, :] = x_ref[r]
        return 0

    lax.fori_loop(0, half_rows, coarse_copy, 0, unroll=4)

    def put_value(r, low, high):
        x[r, pl.ds(0, TILE), :] = low
        x[r, pl.ds(TILE + half_columns, TILE), :] = high

    unfold(
        lambda k: value_lane_e[k], lambda k: value_lane_o[k],
        lambda k: value_lane_e[half_rows + k], lambda k: value_lane_o[half_rows + k], even_l, half_rows, put_value,
    )
    source, target = x, y
    for step in range(1, LAST_SWEEPS + 1):
        edge = DEEP - SECOND + step
        sweep(source, target, coarse_load, coarse_w, edge, total - edge)
        source, target = target, source

    own_fields(f_ref, m_own, load, w)
    fine_halo(rows, columns, fine_e, fine_o, (lane_e, lane_o, corner_e, corner_o), load, w)

    a[FINE - 1] = v_ref[FINE - 1]
    a[FINE + rows] = v_ref[FINE + rows]
    for i in range(2):
        for part in range(2):
            at = pl.ds(TILE + part * half_columns, half_columns)
            k = DEEP + 2 * i + part
            low, high = by_side(even_b, coarse_e[k], coarse_o[k])
            a[1 + i, at, :] = low
            a[FINE + rows + 1 + i, at, :] = high
    end = rows + 2 * FINE
    quarter = end // 4
    first = half_rows

    def fine_lane(k, _):
        low, high = by_side(even_l, coarse_lane_e[first + k], coarse_lane_o[first + k])
        s = sublane(low)
        for g in range(4):
            r = g * quarter + k
            a[r, left, :] = jnp.where(s == TILE - 1, v_ref[r, left, :], roll(low, 5 - 2 * g, 0))
            a[r, right, :] = jnp.where(s == 0, v_ref[r, right, :], roll(high, 1 - 2 * g, 0))
        return 0

    lax.fori_loop(0, quarter, fine_lane, 0, unroll=2)
    at = coarse_lane_e.shape[0] - 1
    low, high = by_side(even_l, coarse_lane_e[at], coarse_lane_o[at])
    for r, turn in ((FINE - 2, 0), (FINE + rows + 1, 4)):
        a[r, left, :] = roll(low, turn, 0)
        a[r, right, :] = roll(high, turn, 0)
    across = columns // 2 + TILE
    skip = TILE - TILE // 2

    def spread_row(k):
        value = source[DEEP - 2 + k, pl.ds(skip, across), :]
        spread[k, pl.ds(0, across, 2), :] = value
        spread[k, pl.ds(1, across, 2), :] = value
        return spread[k]

    for k in (0, 1, half_rows + 2, half_rows + 3):
        both = spread_row(k)
        a[2 * k] += both
        a[2 * k + 1] += both

    def correct(k, _):
        both = spread_row(k)
        ends = [lax.slice_in_dim(both, s, s + TILE, axis=0) for s in (0, TILE + columns)]
        middle = lax.slice_in_dim(both, TILE, TILE + columns, axis=0)
        for part in range(2):
            r = 2 * k + part
            a[r, fine_own, :] = v_ref[r, fine_own, :] + middle
            a[r, left, :] += ends[0]
            a[r, right, :] += ends[1]
        return 0

    lax.fori_loop(2, half_rows + 2, correct, 0, unroll=2)
    sweep(a, b, load, w, 2, end - 2)
    sweep(b, a, load, w, 3, end - 3)
    piece = rows // CHUNKS

    def put(source, hbm, at, sem):
        copy = pltpu.make_async_copy(
            source.at[pl.ds(FINE + at, piece), fine_own, :],
            hbm.at[pl.ds(at, piece), :, layers],
            sem,
        )
        copy.start()
        return copy

    puts = [put(a, u_hbm, c * piece, sems.at[c]) for c in range(CHUNKS)]

    def remains(i, carry):
        up, here = carry
        down = a[FINE + i + 1]
        around = (up + down) + (roll(here, 1, 0) + roll(here, -1, 0))
        value = lax.slice_in_dim(load[FINE + i] + around, TILE, TILE + columns, axis=0)
        mine = lax.slice_in_dim(here, TILE, TILE + columns, axis=0)
        b[FINE + i, fine_own, :] = value - (4.0 + m_own[i]) * mine
        return here, down

    carry = (a[FINE - 1], a[FINE])
    for c in range(CHUNKS):
        carry = lax.fori_loop(c * piece, (c + 1) * piece, remains, carry, unroll=2)
        puts.append(put(b, d_hbm, c * piece, sems.at[CHUNKS + c]))
    for copy in puts:
        copy.wait()


def call(kernel, chain, outs, args, limit, scratch=(), sems=0, hbm=0, hbm_out=False, aliases=None, extra=0, us=1):
    far, near = pl.BlockSpec(memory_space=pltpu.HBM), pl.BlockSpec(memory_space=pltpu.VMEM)
    near_count = len(args) - hbm - extra
    return pl.pallas_call(
        functools.partial(kernel, chain),
        in_specs=[far] * hbm + [near] * near_count + [far] * extra,
        out_specs=[far if hbm_out else near] * len(outs),
        out_shape=[jax.ShapeDtypeStruct(s, jnp.float32) for s in outs],
        scratch_shapes=[pltpu.VMEM(s + (LANES,), jnp.float32) for s in scratch]
        + ([pltpu.SemaphoreType.DMA((sems,))] if sems else []),
        input_output_aliases=aliases or {},
        cost_estimate=pl.CostEstimate(flops=us * COST, bytes_accessed=0, transcendentals=0),
        compiler_params=pltpu.CompilerParams(vmem_limit_bytes=limit * 1024 * 1024),
    )(*args)


def program(f, u, m):
    rows, columns, layers = f.shape
    half_rows, half_columns = rows // 2, columns // 2
    end, total = rows + 2 * FINE, half_rows + 2 * DEEP
    wide, half_wide = columns + 2 * TILE, half_columns + 2 * TILE
    groups = layers // LANES
    block, coarse_block = (rows, columns, LANES), (half_rows, half_columns, LANES)
    chains = range(groups)

    strip, lane = (10, columns, LANES), (rows, TILE, LANES)
    fines, fine_lanes = [], []

    def send(strips):
        fines.append(swap("band", *strips[:2]))
        fine_lanes.append(swap("lane", *strips[2:]))

    first = call(
        first_kernel, 0, ([strip] * 2 + [lane] * 2) * (groups - 1), (u, f, m), FAR,
        scratch=[(groups - 1, 6, rows, TILE)], sems=12 * (groups - 1), hbm=3, us=4,
    )
    for c in range(groups - 1):
        send(first[4 * c : 4 * c + 4])
    *owns, mass, m_e, m_o, n_e, n_o = call(
        load_kernel, 0,
        [block] * 3 * groups + [(groups,) + coarse_block]
        + [(10 + groups * DEEP // 2, columns, LANES)] * 2 + [(rows + groups * half_rows, TILE, LANES)] * 2,
        (u, f, m), LOAD, scratch=[(half_rows, columns)], sems=3 * groups, hbm=3, us=8,
    )
    send((m_e, m_o, n_e, n_o))
    masses, mass_lanes = fines[-1], fine_lanes[-1]
    owns = [owns[3 * c : 3 * c + 3] for c in chains]
    fine_corners, values, loads, coarses = [], [], [], []
    for c in chains:
        strips = call(
            fine_corner_kernel, c, [(2 * CORNER, TILE, LANES)] * 2, (*owns[c], *fines[c], *loads), 4
        )
        fine_corners.append(swap("lane", *strips))
        v, load, *strips = call(
            before_kernel, c,
            [(end, wide, LANES), coarse_block] + [(DEEP + 4, half_columns, LANES)] * 2,
            (*owns[c], *fines[c], *fine_lanes[c], *fine_corners[c]), 16, us=6,
            scratch=[(end, wide)] * 4 + [(half_rows, columns)],
        )
        values.append(v)
        loads.append(load)
        coarses.append(swap("band", *strips))
    coarse_lanes = []
    lane_rows = half_rows + end // 4 + 2 * DEEP - 1
    for c in chains:
        strips = call(
            coarse_pack_kernel, c, [(lane_rows, TILE, LANES)] * 2, (loads[c], values[c], *coarses[c], *masses, *loads[c + 1 :]), 4
        )
        coarse_lanes.append(swap("lane", *strips))
    fields, xs, nexts = [], [], []
    for c in chains:
        fields.append((loads[c], mass, *coarses[c], *masses, *coarse_lanes[c], *mass_lanes))
        x, *strips = call(
            coarse_kernel, c, [coarse_block] + [(SECOND, half_columns, LANES)] * 2,
            fields[c], 8, us=4, scratch=[(total, half_wide)] * 4,
        )
        xs.append(x)
        nexts.append(swap("band", *strips))
    next_lanes = []
    for c in chains:
        strips = call(
            value_pack_kernel, c, [(half_rows + DEEP - 1, TILE, LANES)] * 2, (xs[c], *nexts[c], *xs[c + 1 :]), 4
        )
        next_lanes.append(swap("lane", *strips))
    results = ()
    for c in chains:
        args = (
            *owns[c][1:], values[c], xs[c], *fines[c], *fine_lanes[c], *fine_corners[c],
            *fields[c], *nexts[c], *next_lanes[c],
        )
        results = tuple(
            call(
                after_kernel, c, [(rows, columns, layers)] * 2, args + results, 20, us=8,
                scratch=[(end, wide)] * 4 + [(total, half_wide)] * 4 + [(half_rows + 4, wide)],
                sems=2 * CHUNKS, hbm_out=True, extra=len(results),
                aliases={len(args) + k: k for k in range(len(results))},
            )
        )
    return results


def solution(mesh):
    return jax.shard_map(
        program,
        mesh=mesh,
        in_specs=(P("band", "lane", None), P("band", "lane", None), P("band", "lane", None)),
        out_specs=(P("band", "lane", None), P("band", "lane", None)),
        check_vma=False,
    )
```

time: 159 us -> 169 us (1.063)
  waiting for transfers between devices: 27.7 us -> 42.8 us
  Pallas kernels: 58.9 us -> 47.3 us
  starting transfers between devices: 67.6 us -> 75.7 us
  local copies, waits for them, and re-layouts: 2.45 us -> 0.01 us
    ppermute x14, waiting for transfers between devices: 4.01 us -> 25.5 us  [swap(): lax.ppermute(even, axis, swaps(count, 0))]
    pallas_call x16 -> x14, Pallas kernels: 58.9 us -> 47.3 us  [call(): pl.pallas_call(functools.partial(kernel, chain), in_specs=[far] * hbm + [...]
    ppermute x14, starting transfers between devices: 23.5 us -> 31.1 us  [swap(): lax.ppermute(even, axis, swaps(count, 0))]
    ppermute x14, waiting for transfers between devices: 23.7 us -> 17.3 us  [swap(): lax.ppermute(odd, axis, swaps(count, 1))]
    unnamed x22 -> x2, local copies, waits for them, and re-layouts: 2.45 us -> 0.01 us
  transfers between devices with their start and end apart: 28 -> 28, of which waited for: 6 -> 8; matrix products, arithmetic and copies ran while one was open for 0% -> 0% of each run, Pallas kernels for 30% -> 22%
where the time goes in v3:
time: 169 us; the launch traced here: 167 us
  starting transfers between devices  75.7 us (45%)
  Pallas kernels  47.3 us (28%)
  waiting for transfers between devices  42.8 us (25%)
    pallas_call x14, Pallas kernels, call(): pl.pallas_call(functools.partial(kernel, chain), in_specs=[far] * hbm + [...  47.3 us
    ppermute x14, starting transfers between devices, swap(): lax.ppermute(odd, axis, swaps(count, 1))  44.5 us
    ppermute x14, starting transfers between devices, swap(): lax.ppermute(even, axis, swaps(count, 0))  31.1 us
    ppermute x14, waiting for transfers between devices, swap(): lax.ppermute(even, axis, swaps(count, 0))  25.5 us
    ppermute x14, waiting for transfers between devices, swap(): lax.ppermute(odd, axis, swaps(count, 1))  17.3 us
  transfers between devices with their start and end apart: 28, of which 8 were waited for; matrix products, arithmetic and copies ran while one was open for 0% of the time, Pallas kernels for 22%

profile of v3, /device:TPU:109, one launch (start us, length us, event | category | flops | bytes accessed | tf_op | source)
XLA Modules:
  0.0 166.7 jit_solution(14050710397640018747)
XLA Ops:
  0.6 2.8 %shard_map.51 = (f32[10,64,128]{2,1,0:T(8,128)}, f32[10,64,128]{2,1,0:T(8,128)}, f32[64,8,128]{2,1,0:T(8,128)}, f32[64,8,128]{2,1,0:T(8,128)}) custom-call(f32[64,64,256]{2,1,0:T(8,128)} %u_hbm.3, f32[64,64,256]{2,1,0:T(8,128)} %f_hbm.3, f32[64,64,256]{2,1,0:T(8,128)} %m_hbm.3), custom_call_target="tpu_custom_call" | custom-call | flops 2000000000 | tf_op jit(solution)/shard_map/pallas_call | solution.py:643
  4.2 4.6 %collective-permute-start.5 = (f32[10,64,128]{2,1,0:T(8,128)}, f32[10,64,128]{2,1,0:T(8,128)S(1)}, u32[]{:S(2)}, u32[]{:S(2)}) collective-permute-start(f32[10,64,128]{2,1,0:T(8,128)} %get-tuple-element.56), channel_id=1, source_target_pairs={{8,16},{16,8},{24,32},{32,24},{40,48},{48,40},{56,64},{64,56},{72,... | collective-permute-start | bytes 983048 | tf_op jit(solution)/shard_map/ppermute | solution.py:36
  10.8 1.9 %collective-permute-start.7 = (f32[64,8,128]{2,1,0:T(8,128)}, f32[64,8,128]{2,1,0:T(8,128)S(1)}, u32[]{:S(2)}, u32[]{:S(2)}) collective-permute-start(f32[64,8,128]{2,1,0:T(8,128)} %get-tuple-element.58), channel_id=1, source_target_pairs={{1,2},{2,1},{3,4},{4,3},{5,6},{6,5},{9,10},{10,9},{11,12},{12,11},... | collective-permute-start | bytes 786440 | tf_op jit(solution)/shard_map/ppermute | solution.py:36
  12.7 6.0 %shard_map.50 = (f32[64,64,128]{2,1,0:T(8,128)S(1)}, f32[64,64,128]{2,1,0:T(8,128)S(1)}, f32[64,64,128]{2,1,0:T(8,128)S(1)}, f32[64,64,128]{2,1,0:T(8,128)S(1)},...) custom-call(f32[64,64,256]{2,1,0:T(8,128)} %u_hbm.3, ...), custom_call_target="tpu_custom_call" | custom-call | flops 4000000000 | tf_op jit(solution)/shard_map/pallas_call | solution.py:643
  19.7 6.6 %collective-permute-start.1 = (f32[18,64,128]{2,1,0:T(8,128)S(1)}, f32[18,64,128]{2,1,0:T(8,128)S(1)}, u32[]{:S(2)}, u32[]{:S(2)}) collective-permute-start(f32[18,64,128]{2,1,0:T(8,128)S(1)} %get-tuple-element.49), channel_id=1, source_target_pairs={{8,16},{16,8},{24,32},{32,24},{40,48},{48,40},{56,64},{64,56},{72,... | collective-permute-start | bytes 1769480 | tf_op jit(solution)/shard_map/ppermute | solution.py:36
  27.4 2.2 %collective-permute-start.3 = (f32[128,8,128]{2,1,0:T(8,128)S(1)}, f32[128,8,128]{2,1,0:T(8,128)S(1)}, u32[]{:S(2)}, u32[]{:S(2)}) collective-permute-start(f32[128,8,128]{2,1,0:T(8,128)S(1)} %get-tuple-element.51), channel_id=1, source_target_pairs={{1,2},{2,1},{3,4},{4,3},{5,6},{6,5},{9,10},{10,9},{11,12},{12,11},... | collective-permute-start | bytes 1572872 | tf_op jit(solution)/shard_map/ppermute | solution.py:36
  29.8 2.2 %collective-permute-start.8 = (f32[10,8,128]{2,1,0:T(8,128)S(1)}, f32[10,8,128]{2,1,0:T(8,128)S(1)}, u32[]{:S(2)}, u32[]{:S(2)}) collective-permute-start(f32[10,8,128]{2,1,0:T(8,128)S(1)} %get-tuple-element.59), channel_id=1, source_target_pairs={{0,1},{1,0},{2,3},{3,2},{4,5},{5,4},{6,7},{7,6},{8,9},{9,8},{10,11... | collective-permute-start | bytes 122888 | tf_op jit(solution)/shard_map/ppermute | solution.py:35
  32.0 24.7 %collective-permute-done.8.corner_e = f32[10,8,128]{2,1,0:T(8,128)S(1)} collective-permute-done((f32[10,8,128]{2,1,0:T(8,128)S(1)}, f32[10,8,128]{2,1,0:T(8,128)S(1)}, u32[]{:S(2)}, u32[]{:S(2)}) %collective-permute-start.8) | collective-permute-done | bytes 40992 | tf_op jit(solution)/shard_map/ppermute | solution.py:35
  56.6 2.0 %collective-permute-start.9 = (f32[10,8,128]{2,1,0:T(8,128)S(1)}, f32[10,8,128]{2,1,0:T(8,128)S(1)}, u32[]{:S(2)}, u32[]{:S(2)}) collective-permute-start(f32[10,8,128]{2,1,0:T(8,128)S(1)} %get-tuple-element.60), channel_id=1, source_target_pairs={{1,2},{2,1},{3,4},{4,3},{5,6},{6,5},{9,10},{10,9},{11,12},{12,11},... | collective-permute-start | bytes 122888 | tf_op jit(solution)/shard_map/ppermute | solution.py:36
  58.7 4.4 %collective-permute-done.9.corner_o = f32[10,8,128]{2,1,0:T(8,128)S(1)} collective-permute-done((f32[10,8,128]{2,1,0:T(8,128)S(1)}, f32[10,8,128]{2,1,0:T(8,128)S(1)}, u32[]{:S(2)}, u32[]{:S(2)}) %collective-permute-start.9) | collective-permute-done | bytes 40992 | tf_op jit(solution)/shard_map/ppermute | solution.py:36
  63.1 6.5 %shard_map.53 = (f32[72,80,128]{2,1,0:T(8,128)S(1)}, f32[32,32,128]{2,1,0:T(8,128)S(1)}, f32[12,32,128]{2,1,0:T(8,128)S(1)}, f32[12,32,128]{2,1,0:T(8,128)S(1)}) custom-call(f32[64,64,128]{2,1,0:T(8,128)S(1)} %get-tuple-element.52.u_ref, f32[64,64,128]{2,1,0:T(8,128)S(1)} %get-tuple-element.53.f_ref, f32[64,64,128]{2,1,0:T(8,128)S(1)} %get-tuple-element.54.m_ref.m_own, ...), custom_call_target="tpu_custom_call" | custom-call | flops 3000000000 | tf_op jit(solution)/shard_map/pallas_call | solution.py:643
  70.4 1.9 %collective-permute-start.11 = (f32[10,8,128]{2,1,0:T(8,128)S(1)}, f32[10,8,128]{2,1,0:T(8,128)S(1)}, u32[]{:S(2)}, u32[]{:S(2)}) collective-permute-start(f32[10,8,128]{2,1,0:T(8,128)S(1)} %get-tuple-element.63), channel_id=1, source_target_pairs={{1,2},{2,1},{3,4},{4,3},{5,6},{6,5},{9,10},{10,9},{11,12},{12,11},... | collective-permute-start | bytes 122888 | tf_op jit(solution)/shard_map/ppermute | solution.py:36
  72.3 8.8 %collective-permute-start.20 = (f32[12,32,128]{2,1,0:T(8,128)S(1)}, f32[12,32,128]{2,1,0:T(8,128)S(1)}, u32[]{:S(2)}, u32[]{:S(2)}) collective-permute-start(f32[12,32,128]{2,1,0:T(8,128)S(1)} %get-tuple-element.77), channel_id=1, source_target_pairs={{0,8},{8,0},{16,24},{24,16},{32,40},{40,32},{48,56},{56,48},{64,72... | collective-permute-start | bytes 589832 | tf_op jit(solution)/shard_map/ppermute | solution.py:35
  81.1 4.6 %collective-permute-start.21 = (f32[12,32,128]{2,1,0:T(8,128)S(1)}, f32[12,32,128]{2,1,0:T(8,128)S(1)}, u32[]{:S(2)}, u32[]{:S(2)}) collective-permute-start(f32[12,32,128]{2,1,0:T(8,128)S(1)} %get-tuple-element.78), channel_id=1, source_target_pairs={{8,16},{16,8},{24,32},{32,24},{40,48},{48,40},{56,64},{64,56},{72,... | collective-permute-start | bytes 589832 | tf_op jit(solution)/shard_map/ppermute | solution.py:36
  85.7 6.5 %shard_map.55 = (f32[72,80,128]{2,1,0:T(8,128)S(1)}, f32[32,32,128]{2,1,0:T(8,128)S(1)}, f32[12,32,128]{2,1,0:T(8,128)S(1)}, f32[12,32,128]{2,1,0:T(8,128)S(1)}) custom-call(f32[64,64,128]{2,1,0:T(8,128)S(1)} %get-tuple-element.47.u_ref, f32[64,64,128]{2,1,0:T(8,128)S(1)} %get-tuple-element.45.f_ref, f32[64,64,128]{2,1,0:T(8,128)S(1)} %copy-done, ...), custom_call_target="tpu_custom_call" | custom-call | flops 3000000000 | tf_op jit(solution)/shard_map/pallas_call | solution.py:643
  92.4 5.1 %collective-permute-start.13 = (f32[12,32,128]{2,1,0:T(8,128)S(1)}, f32[12,32,128]{2,1,0:T(8,128)S(1)}, u32[]{:S(2)}, u32[]{:S(2)}) collective-permute-start(f32[12,32,128]{2,1,0:T(8,128)S(1)} %get-tuple-element.68), channel_id=1, source_target_pairs={{8,16},{16,8},{24,32},{32,24},{40,48},{48,40},{56,64},{64,56},{72,... | collective-permute-start | bytes 589832 | tf_op jit(solution)/shard_map/ppermute | solution.py:36
  97.7 2.8 %collective-permute-start.22 = (f32[65,8,128]{2,1,0:T(8,128)S(1)}, f32[65,8,128]{2,1,0:T(8,128)S(1)}, u32[]{:S(2)}, u32[]{:S(2)}) collective-permute-start(f32[65,8,128]{2,1,0:T(8,128)S(1)} %get-tuple-element.79), channel_id=1, source_target_pairs={{0,1},{1,0},{2,3},{3,2},{4,5},{5,4},{6,7},{7,6},{8,9},{9,8},{10,11... | collective-permute-start | bytes 798728 | tf_op jit(solution)/shard_map/ppermute | solution.py:35
  100.5 1.9 %collective-permute-start.23 = (f32[65,8,128]{2,1,0:T(8,128)S(1)}, f32[65,8,128]{2,1,0:T(8,128)S(1)}, u32[]{:S(2)}, u32[]{:S(2)}) collective-permute-start(f32[65,8,128]{2,1,0:T(8,128)S(1)} %get-tuple-element.80), channel_id=1, source_target_pairs={{1,2},{2,1},{3,4},{4,3},{5,6},{6,5},{9,10},{10,9},{11,12},{12,11},... | collective-permute-start | bytes 798728 | tf_op jit(solution)/shard_map/ppermute | solution.py:36
  103.2 3.0 %collective-permute-start.14 = (f32[65,8,128]{2,1,0:T(8,128)S(1)}, f32[65,8,128]{2,1,0:T(8,128)S(1)}, u32[]{:S(2)}, u32[]{:S(2)}) collective-permute-start(f32[65,8,128]{2,1,0:T(8,128)S(1)} %get-tuple-element.69), channel_id=1, source_target_pairs={{0,1},{1,0},{2,3},{3,2},{4,5},{5,4},{6,7},{7,6},{8,9},{9,8},{10,11... | collective-permute-start | bytes 798728 | tf_op jit(solution)/shard_map/ppermute | solution.py:35
  106.2 1.9 %collective-permute-start.15 = (f32[65,8,128]{2,1,0:T(8,128)S(1)}, f32[65,8,128]{2,1,0:T(8,128)S(1)}, u32[]{:S(2)}, u32[]{:S(2)}) collective-permute-start(f32[65,8,128]{2,1,0:T(8,128)S(1)} %get-tuple-element.70), channel_id=1, source_target_pairs={{1,2},{2,1},{3,4},{4,3},{5,6},{6,5},{9,10},{10,9},{11,12},{12,11},... | collective-permute-start | bytes 798728 | tf_op jit(solution)/shard_map/ppermute | solution.py:36
  108.2 5.0 %collective-permute-done.23.refs_7_ = f32[65,8,128]{2,1,0:T(8,128)S(1)} collective-permute-done((f32[65,8,128]{2,1,0:T(8,128)S(1)}, f32[65,8,128]{2,1,0:T(8,128)S(1)}, u32[]{:S(2)}, u32[]{:S(2)}) %collective-permute-start.23) | collective-permute-done | bytes 266272 | tf_op jit(solution)/shard_map/ppermute | solution.py:36
  113.2 4.0 %shard_map.60 = (f32[32,32,128]{2,1,0:T(8,128)S(1)}, f32[6,32,128]{2,1,0:T(8,128)S(1)}, f32[6,32,128]{2,1,0:T(8,128)S(1)}) custom-call(f32[32,32,128]{2,1,0:T(8,128)S(1)} %get-tuple-element.61.refs_0_.load_ref, f32[2,32,32,128]{3,2,1,0:T(8,128)S(1)} %get-tuple-element.66.refs_1_, f32[12,32,128]{2,1,0:T(8,128)S(1)} %collective-permute-done.20.got_e.refs_2_, ...), custom_call_target="tpu_custom_call" | custom-call | flops 2000000000 | tf_op jit(solution)/shard_map/pallas_call | solution.py:643
  117.2 3.5 %collective-permute-start.24 = (f32[6,32,128]{2,1,0:T(8,128)S(1)}, f32[6,32,128]{2,1,0:T(8,128)S(1)}, u32[]{:S(2)}, u32[]{:S(2)}) collective-permute-start(f32[6,32,128]{2,1,0:T(8,128)S(1)} %get-tuple-element.82), channel_id=1, source_target_pairs={{0,8},{8,0},{16,24},{24,16},{32,40},{40,32},{48,56},{56,48},{64,72... | collective-permute-start | bytes 294920 | tf_op jit(solution)/shard_map/ppermute | solution.py:35
  120.7 3.5 %collective-permute-start.25 = (f32[6,32,128]{2,1,0:T(8,128)S(1)}, f32[6,32,128]{2,1,0:T(8,128)S(1)}, u32[]{:S(2)}, u32[]{:S(2)}) collective-permute-start(f32[6,32,128]{2,1,0:T(8,128)S(1)} %get-tuple-element.83), channel_id=1, source_target_pairs={{8,16},{16,8},{24,32},{32,24},{40,48},{48,40},{56,64},{64,56},{72,... | collective-permute-start | bytes 294920 | tf_op jit(solution)/shard_map/ppermute | solution.py:36
  124.6 4.0 %shard_map.57 = (f32[32,32,128]{2,1,0:T(8,128)S(1)}, f32[6,32,128]{2,1,0:T(8,128)S(1)}, f32[6,32,128]{2,1,0:T(8,128)S(1)}) custom-call(f32[32,32,128]{2,1,0:T(8,128)S(1)} %get-tuple-element.65.load_ref.refs_0_, f32[2,32,32,128]{3,2,1,0:T(8,128)S(1)} %get-tuple-element.66.refs_1_, f32[12,32,128]{2,1,0:T(8,128)S(1)} %collective-permute-done.12.got_e.refs_2_, ...), custom_call_target="tpu_custom_call" | custom-call | flops 2000000000 | tf_op jit(solution)/shard_map/pallas_call | solution.py:643
  131.7 1.9 %collective-permute-start.27 = (f32[39,8,128]{2,1,0:T(8,128)S(1)}, f32[39,8,128]{2,1,0:T(8,128)S(1)}, u32[]{:S(2)}, u32[]{:S(2)}) collective-permute-start(f32[39,8,128]{2,1,0:T(8,128)S(1)} %get-tuple-element.85), channel_id=1, source_target_pairs={{1,2},{2,1},{3,4},{4,3},{5,6},{6,5},{9,10},{10,9},{11,12},{12,11},... | collective-permute-start | bytes 479240 | tf_op jit(solution)/shard_map/ppermute | solution.py:36
  134.5 4.4 %collective-permute-start.17 = (f32[6,32,128]{2,1,0:T(8,128)S(1)}, f32[6,32,128]{2,1,0:T(8,128)S(1)}, u32[]{:S(2)}, u32[]{:S(2)}) collective-permute-start(f32[6,32,128]{2,1,0:T(8,128)S(1)} %get-tuple-element.73), channel_id=1, source_target_pairs={{8,16},{16,8},{24,32},{32,24},{40,48},{48,40},{56,64},{64,56},{72,... | collective-permute-start | bytes 294920 | tf_op jit(solution)/shard_map/ppermute | solution.py:36
  138.9 5.1 %collective-permute-done.17.got_o.refs_11_ = f32[6,32,128]{2,1,0:T(8,128)S(1)} collective-permute-done((f32[6,32,128]{2,1,0:T(8,128)S(1)}, f32[6,32,128]{2,1,0:T(8,128)S(1)}, u32[]{:S(2)}, u32[]{:S(2)}) %collective-permute-start.17) | collective-permute-done | bytes 98336 | tf_op jit(solution)/shard_map/ppermute | solution.py:36
  144.0 3.7 %collective-permute-start.18 = (f32[39,8,128]{2,1,0:T(8,128)S(1)}, f32[39,8,128]{2,1,0:T(8,128)S(1)}, u32[]{:S(2)}, u32[]{:S(2)}) collective-permute-start(f32[39,8,128]{2,1,0:T(8,128)S(1)} %get-tuple-element.74), channel_id=1, source_target_pairs={{0,1},{1,0},{2,3},{3,2},{4,5},{5,4},{6,7},{7,6},{8,9},{9,8},{10,11... | collective-permute-start | bytes 479240 | tf_op jit(solution)/shard_map/ppermute | solution.py:35
  147.8 1.9 %collective-permute-start.19 = (f32[39,8,128]{2,1,0:T(8,128)S(1)}, f32[39,8,128]{2,1,0:T(8,128)S(1)}, u32[]{:S(2)}, u32[]{:S(2)}) collective-permute-start(f32[39,8,128]{2,1,0:T(8,128)S(1)} %get-tuple-element.75), channel_id=1, source_target_pairs={{1,2},{2,1},{3,4},{4,3},{5,6},{6,5},{9,10},{10,9},{11,12},{12,11},... | collective-permute-start | bytes 479240 | tf_op jit(solution)/shard_map/ppermute | solution.py:36
  149.7 8.5 %shard_map.62 = (f32[64,64,256]{2,1,0:T(8,128)}, f32[64,64,256]{2,1,0:T(8,128)}) custom-call(f32[64,64,128]{2,1,0:T(8,128)S(1)} %get-tuple-element.53.f_ref, f32[64,64,128]{2,1,0:T(8,128)S(1)} %get-tuple-element.54.m_ref.m_own, f32[72,80,128]{2,1,0:T(8,128)S(1)} %get-tuple-element.76.v_ref, f32[32,32,128]{2,1,0:T(8,128)S(1)} %get-tuple-element.81.x_ref, ...), custom_call_target="tpu_custom_call" | custom-call | flops 4000000000 | tf_op jit(solution)/shard_map/pallas_call | solution.py:643
  158.2 8.5 %shard_map.63 = (f32[64,64,256]{2,1,0:T(8,128)}, f32[64,64,256]{2,1,0:T(8,128)}) custom-call(f32[64,64,128]{2,1,0:T(8,128)S(1)} %get-tuple-element.45.f_ref, f32[64,64,128]{2,1,0:T(8,128)S(1)} %copy-done, f32[72,80,128]{2,1,0:T(8,128)S(1)} %get-tuple-element.64.v_ref, ...), custom_call_target="tpu_custom_call", output_to_operand_aliasing={{0}: (24, {}), {1}: (25, {})} | custom-call | flops 4000000000 | tf_op jit(solution)/shard_map/pallas_call | solution.py:643
  (40 shorter events, 11.0 us)
Async XLA Ops:
  3.5 22.8 %collective-permute-start.4 = (f32[10,64,128]{2,1,0:T(8,128)}, f32[10,64,128]{2,1,0:T(8,128)S(1)}, u32[]{:S(2)}, u32[]{:S(2)}) collective-permute-start(f32[10,64,128]{2,1,0:T(8,128)} %get-tuple-element.55), channel_id=1, source_target_pairs={{0,8},{8,0},{16,24},{24,16},{32,40},{40,32},{48,56},{56,48},{64,72... | collective-permute-start | bytes 983048 | tf_op jit(solution)/shard_map/ppermute | solution.py:35
  4.2 23.2 %collective-permute-start.5 = (f32[10,64,128]{2,1,0:T(8,128)}, f32[10,64,128]{2,1,0:T(8,128)S(1)}, u32[]{:S(2)}, u32[]{:S(2)}) collective-permute-start(f32[10,64,128]{2,1,0:T(8,128)} %get-tuple-element.56), channel_id=1, source_target_pairs={{8,16},{16,8},{24,32},{32,24},{40,48},{48,40},{56,64},{64,56},{72,... | collective-permute-start | bytes 983048 | tf_op jit(solution)/shard_map/ppermute | solution.py:36
  8.9 10.8 %collective-permute-start.6 = (f32[64,8,128]{2,1,0:T(8,128)}, f32[64,8,128]{2,1,0:T(8,128)S(1)}, u32[]{:S(2)}, u32[]{:S(2)}) collective-permute-start(f32[64,8,128]{2,1,0:T(8,128)} %get-tuple-element.57), channel_id=1, source_target_pairs={{0,1},{1,0},{2,3},{3,2},{4,5},{5,4},{6,7},{7,6},{8,9},{9,8},{10,11... | collective-permute-start | bytes 786440 | tf_op jit(solution)/shard_map/ppermute | solution.py:35
  10.8 19.0 %collective-permute-start.7 = (f32[64,8,128]{2,1,0:T(8,128)}, f32[64,8,128]{2,1,0:T(8,128)S(1)}, u32[]{:S(2)}, u32[]{:S(2)}) collective-permute-start(f32[64,8,128]{2,1,0:T(8,128)} %get-tuple-element.58), channel_id=1, source_target_pairs={{1,2},{2,1},{3,4},{4,3},{5,6},{6,5},{9,10},{10,9},{11,12},{12,11},... | collective-permute-start | bytes 786440 | tf_op jit(solution)/shard_map/ppermute | solution.py:36
  18.7 50.9 %collective-permute-start = (f32[18,64,128]{2,1,0:T(8,128)S(1)}, f32[18,64,128]{2,1,0:T(8,128)S(1)}, u32[]{:S(2)}, u32[]{:S(2)}) collective-permute-start(f32[18,64,128]{2,1,0:T(8,128)S(1)} %get-tuple-element.48), channel_id=1, source_target_pairs={{0,8},{8,0},{16,24},{24,16},{32,40},{40,32},{48,56},{56,48},{64,72... | collective-permute-start | bytes 1769480 | tf_op jit(solution)/shard_map/ppermute | solution.py:35
  19.7 50.0 %collective-permute-start.1 = (f32[18,64,128]{2,1,0:T(8,128)S(1)}, f32[18,64,128]{2,1,0:T(8,128)S(1)}, u32[]{:S(2)}, u32[]{:S(2)}) collective-permute-start(f32[18,64,128]{2,1,0:T(8,128)S(1)} %get-tuple-element.49), channel_id=1, source_target_pairs={{8,16},{16,8},{24,32},{32,24},{40,48},{48,40},{56,64},{64,56},{72,... | collective-permute-start | bytes 1769480 | tf_op jit(solution)/shard_map/ppermute | solution.py:36
  26.3 54.8 %collective-permute-start.2 = (f32[128,8,128]{2,1,0:T(8,128)S(1)}, f32[128,8,128]{2,1,0:T(8,128)S(1)}, u32[]{:S(2)}, u32[]{:S(2)}) collective-permute-start(f32[128,8,128]{2,1,0:T(8,128)S(1)} %get-tuple-element.50), channel_id=1, source_target_pairs={{0,1},{1,0},{2,3},{3,2},{4,5},{5,4},{6,7},{7,6},{8,9},{9,8},{10,11... | collective-permute-start | bytes 1572872 | tf_op jit(solution)/shard_map/ppermute | solution.py:35
  27.4 58.2 %collective-permute-start.3 = (f32[128,8,128]{2,1,0:T(8,128)S(1)}, f32[128,8,128]{2,1,0:T(8,128)S(1)}, u32[]{:S(2)}, u32[]{:S(2)}) collective-permute-start(f32[128,8,128]{2,1,0:T(8,128)S(1)} %get-tuple-element.51), channel_id=1, source_target_pairs={{1,2},{2,1},{3,4},{4,3},{5,6},{6,5},{9,10},{10,9},{11,12},{12,11},... | collective-permute-start | bytes 1572872 | tf_op jit(solution)/shard_map/ppermute | solution.py:36
  29.8 26.9 %collective-permute-start.8 = (f32[10,8,128]{2,1,0:T(8,128)S(1)}, f32[10,8,128]{2,1,0:T(8,128)S(1)}, u32[]{:S(2)}, u32[]{:S(2)}) collective-permute-start(f32[10,8,128]{2,1,0:T(8,128)S(1)} %get-tuple-element.59), channel_id=1, source_target_pairs={{0,1},{1,0},{2,3},{3,2},{4,5},{5,4},{6,7},{7,6},{8,9},{9,8},{10,11... | collective-permute-start | bytes 122888 | tf_op jit(solution)/shard_map/ppermute | solution.py:35
  56.6 13.0 %copy-start = (f32[64,64,128]{2,1,0:T(8,128)S(1)}, f32[64,64,128]{2,1,0:T(8,128)}, u32[]{:S(2)}) copy-start(f32[64,64,128]{2,1,0:T(8,128)} %get-tuple-element.46.m_ref.m_own) | copy-start | bytes 6291460
  56.6 6.5 %collective-permute-start.9 = (f32[10,8,128]{2,1,0:T(8,128)S(1)}, f32[10,8,128]{2,1,0:T(8,128)S(1)}, u32[]{:S(2)}, u32[]{:S(2)}) collective-permute-start(f32[10,8,128]{2,1,0:T(8,128)S(1)} %get-tuple-element.60), channel_id=1, source_target_pairs={{1,2},{2,1},{3,4},{4,3},{5,6},{6,5},{9,10},{10,9},{11,12},{12,11},... | collective-permute-start | bytes 122888 | tf_op jit(solution)/shard_map/ppermute | solution.py:36
  69.7 15.9 %collective-permute-start.10 = (f32[10,8,128]{2,1,0:T(8,128)S(1)}, f32[10,8,128]{2,1,0:T(8,128)S(1)}, u32[]{:S(2)}, u32[]{:S(2)}) collective-permute-start(f32[10,8,128]{2,1,0:T(8,128)S(1)} %get-tuple-element.62), channel_id=1, source_target_pairs={{0,1},{1,0},{2,3},{3,2},{4,5},{5,4},{6,7},{7,6},{8,9},{9,8},{10,11... | collective-permute-start | bytes 122888 | tf_op jit(solution)/shard_map/ppermute | solution.py:35
  70.4 15.3 %collective-permute-start.11 = (f32[10,8,128]{2,1,0:T(8,128)S(1)}, f32[10,8,128]{2,1,0:T(8,128)S(1)}, u32[]{:S(2)}, u32[]{:S(2)}) collective-permute-start(f32[10,8,128]{2,1,0:T(8,128)S(1)} %get-tuple-element.63), channel_id=1, source_target_pairs={{1,2},{2,1},{3,4},{4,3},{5,6},{6,5},{9,10},{10,9},{11,12},{12,11},... | collective-permute-start | bytes 122888 | tf_op jit(solution)/shard_map/ppermute | solution.py:36
  72.3 25.3 %collective-permute-start.20 = (f32[12,32,128]{2,1,0:T(8,128)S(1)}, f32[12,32,128]{2,1,0:T(8,128)S(1)}, u32[]{:S(2)}, u32[]{:S(2)}) collective-permute-start(f32[12,32,128]{2,1,0:T(8,128)S(1)} %get-tuple-element.77), channel_id=1, source_target_pairs={{0,8},{8,0},{16,24},{24,16},{32,40},{40,32},{48,56},{56,48},{64,72... | collective-permute-start | bytes 589832 | tf_op jit(solution)/shard_map/ppermute | solution.py:35
  81.1 16.5 %collective-permute-start.21 = (f32[12,32,128]{2,1,0:T(8,128)S(1)}, f32[12,32,128]{2,1,0:T(8,128)S(1)}, u32[]{:S(2)}, u32[]{:S(2)}) collective-permute-start(f32[12,32,128]{2,1,0:T(8,128)S(1)} %get-tuple-element.78), channel_id=1, source_target_pairs={{8,16},{16,8},{24,32},{32,24},{40,48},{48,40},{56,64},{64,56},{72,... | collective-permute-start | bytes 589832 | tf_op jit(solution)/shard_map/ppermute | solution.py:36
  92.2 10.2 %collective-permute-start.12 = (f32[12,32,128]{2,1,0:T(8,128)S(1)}, f32[12,32,128]{2,1,0:T(8,128)S(1)}, u32[]{:S(2)}, u32[]{:S(2)}) collective-permute-start(f32[12,32,128]{2,1,0:T(8,128)S(1)} %get-tuple-element.67), channel_id=1, source_target_pairs={{0,8},{8,0},{16,24},{24,16},{32,40},{40,32},{48,56},{56,48},{64,72... | collective-permute-start | bytes 589832 | tf_op jit(solution)/shard_map/ppermute | solution.py:35
  92.4 10.7 %collective-permute-start.13 = (f32[12,32,128]{2,1,0:T(8,128)S(1)}, f32[12,32,128]{2,1,0:T(8,128)S(1)}, u32[]{:S(2)}, u32[]{:S(2)}) collective-permute-start(f32[12,32,128]{2,1,0:T(8,128)S(1)} %get-tuple-element.68), channel_id=1, source_target_pairs={{8,16},{16,8},{24,32},{32,24},{40,48},{48,40},{56,64},{64,56},{72,... | collective-permute-start | bytes 589832 | tf_op jit(solution)/shard_map/ppermute | solution.py:36
  97.7 10.5 %collective-permute-start.22 = (f32[65,8,128]{2,1,0:T(8,128)S(1)}, f32[65,8,128]{2,1,0:T(8,128)S(1)}, u32[]{:S(2)}, u32[]{:S(2)}) collective-permute-start(f32[65,8,128]{2,1,0:T(8,128)S(1)} %get-tuple-element.79), channel_id=1, source_target_pairs={{0,1},{1,0},{2,3},{3,2},{4,5},{5,4},{6,7},{7,6},{8,9},{9,8},{10,11... | collective-permute-start | bytes 798728 | tf_op jit(solution)/shard_map/ppermute | solution.py:35
  100.5 12.7 %collective-permute-start.23 = (f32[65,8,128]{2,1,0:T(8,128)S(1)}, f32[65,8,128]{2,1,0:T(8,128)S(1)}, u32[]{:S(2)}, u32[]{:S(2)}) collective-permute-start(f32[65,8,128]{2,1,0:T(8,128)S(1)} %get-tuple-element.80), channel_id=1, source_target_pairs={{1,2},{2,1},{3,4},{4,3},{5,6},{6,5},{9,10},{10,9},{11,12},{12,11},... | collective-permute-start | bytes 798728 | tf_op jit(solution)/shard_map/ppermute | solution.py:36
  103.2 21.0 %collective-permute-start.14 = (f32[65,8,128]{2,1,0:T(8,128)S(1)}, f32[65,8,128]{2,1,0:T(8,128)S(1)}, u32[]{:S(2)}, u32[]{:S(2)}) collective-permute-start(f32[65,8,128]{2,1,0:T(8,128)S(1)} %get-tuple-element.69), channel_id=1, source_target_pairs={{0,1},{1,0},{2,3},{3,2},{4,5},{5,4},{6,7},{7,6},{8,9},{9,8},{10,11... | collective-permute-start | bytes 798728 | tf_op jit(solution)/shard_map/ppermute | solution.py:35
  106.2 18.3 %collective-permute-start.15 = (f32[65,8,128]{2,1,0:T(8,128)S(1)}, f32[65,8,128]{2,1,0:T(8,128)S(1)}, u32[]{:S(2)}, u32[]{:S(2)}) collective-permute-start(f32[65,8,128]{2,1,0:T(8,128)S(1)} %get-tuple-element.70), channel_id=1, source_target_pairs={{1,2},{2,1},{3,4},{4,3},{5,6},{6,5},{9,10},{10,9},{11,12},{12,11},... | collective-permute-start | bytes 798728 | tf_op jit(solution)/shard_map/ppermute | solution.py:36
  117.2 11.4 %collective-permute-start.24 = (f32[6,32,128]{2,1,0:T(8,128)S(1)}, f32[6,32,128]{2,1,0:T(8,128)S(1)}, u32[]{:S(2)}, u32[]{:S(2)}) collective-permute-start(f32[6,32,128]{2,1,0:T(8,128)S(1)} %get-tuple-element.82), channel_id=1, source_target_pairs={{0,8},{8,0},{16,24},{24,16},{32,40},{40,32},{48,56},{56,48},{64,72... | collective-permute-start | bytes 294920 | tf_op jit(solution)/shard_map/ppermute | solution.py:35
  120.7 9.5 %collective-permute-start.25 = (f32[6,32,128]{2,1,0:T(8,128)S(1)}, f32[6,32,128]{2,1,0:T(8,128)S(1)}, u32[]{:S(2)}, u32[]{:S(2)}) collective-permute-start(f32[6,32,128]{2,1,0:T(8,128)S(1)} %get-tuple-element.83), channel_id=1, source_target_pairs={{8,16},{16,8},{24,32},{32,24},{40,48},{48,40},{56,64},{64,56},{72,... | collective-permute-start | bytes 294920 | tf_op jit(solution)/shard_map/ppermute | solution.py:36
  130.3 19.4 %collective-permute-start.26 = (f32[39,8,128]{2,1,0:T(8,128)S(1)}, f32[39,8,128]{2,1,0:T(8,128)S(1)}, u32[]{:S(2)}, u32[]{:S(2)}) collective-permute-start(f32[39,8,128]{2,1,0:T(8,128)S(1)} %get-tuple-element.84), channel_id=1, source_target_pairs={{0,1},{1,0},{2,3},{3,2},{4,5},{5,4},{6,7},{7,6},{8,9},{9,8},{10,11... | collective-permute-start | bytes 479240 | tf_op jit(solution)/shard_map/ppermute | solution.py:35
  131.7 18.0 %collective-permute-start.27 = (f32[39,8,128]{2,1,0:T(8,128)S(1)}, f32[39,8,128]{2,1,0:T(8,128)S(1)}, u32[]{:S(2)}, u32[]{:S(2)}) collective-permute-start(f32[39,8,128]{2,1,0:T(8,128)S(1)} %get-tuple-element.85), channel_id=1, source_target_pairs={{1,2},{2,1},{3,4},{4,3},{5,6},{6,5},{9,10},{10,9},{11,12},{12,11},... | collective-permute-start | bytes 479240 | tf_op jit(solution)/shard_map/ppermute | solution.py:36
  133.6 5.3 %collective-permute-start.16 = (f32[6,32,128]{2,1,0:T(8,128)S(1)}, f32[6,32,128]{2,1,0:T(8,128)S(1)}, u32[]{:S(2)}, u32[]{:S(2)}) collective-permute-start(f32[6,32,128]{2,1,0:T(8,128)S(1)} %get-tuple-element.72), channel_id=1, source_target_pairs={{0,8},{8,0},{16,24},{24,16},{32,40},{40,32},{48,56},{56,48},{64,72... | collective-permute-start | bytes 294920 | tf_op jit(solution)/shard_map/ppermute | solution.py:35
  134.5 9.5 %collective-permute-start.17 = (f32[6,32,128]{2,1,0:T(8,128)S(1)}, f32[6,32,128]{2,1,0:T(8,128)S(1)}, u32[]{:S(2)}, u32[]{:S(2)}) collective-permute-start(f32[6,32,128]{2,1,0:T(8,128)S(1)} %get-tuple-element.73), channel_id=1, source_target_pairs={{8,16},{16,8},{24,32},{32,24},{40,48},{48,40},{56,64},{64,56},{72,... | collective-permute-start | bytes 294920 | tf_op jit(solution)/shard_map/ppermute | solution.py:36
  144.0 14.2 %collective-permute-start.18 = (f32[39,8,128]{2,1,0:T(8,128)S(1)}, f32[39,8,128]{2,1,0:T(8,128)S(1)}, u32[]{:S(2)}, u32[]{:S(2)}) collective-permute-start(f32[39,8,128]{2,1,0:T(8,128)S(1)} %get-tuple-element.74), channel_id=1, source_target_pairs={{0,1},{1,0},{2,3},{3,2},{4,5},{5,4},{6,7},{7,6},{8,9},{9,8},{10,11... | collective-permute-start | bytes 479240 | tf_op jit(solution)/shard_map/ppermute | solution.py:35
  147.8 10.4 %collective-permute-start.19 = (f32[39,8,128]{2,1,0:T(8,128)S(1)}, f32[39,8,128]{2,1,0:T(8,128)S(1)}, u32[]{:S(2)}, u32[]{:S(2)}) collective-permute-start(f32[39,8,128]{2,1,0:T(8,128)S(1)} %get-tuple-element.75), channel_id=1, source_target_pairs={{1,2},{2,1},{3,4},{4,3},{5,6},{6,5},{9,10},{10,9},{11,12},{12,11},... | collective-permute-start | bytes 479240 | tf_op jit(solution)/shard_map/ppermute | solution.py:36

commit v4 on v3

--- a/solution.py
+++ b/solution.py
@@ -315,7 +315,7 @@
 
 def before_kernel(
     chain, u_ref, f_ref, m_own, got_e, got_o, lane_e, lane_o, corner_e, corner_o,
-    v_ref, load_ref, even_ref, odd_ref, a, b, load, w, pairs,
+    v_ref, load_ref, even_ref, odd_ref, load, w, a, b, pairs,
 ):
     even_b, even_l = place("band")[0], place("lane")[0]
     rows, columns = m_own.shape[0], m_own.shape[1]
@@ -470,7 +470,7 @@
 
 
 def coarse_kernel(chain, *refs):
-    fields, (x_ref, even_ref, odd_ref, a, b, load, w) = refs[:10], refs[10:]
+    fields, (x_ref, even_ref, odd_ref, load, w, a, b) = refs[:10], refs[10:]
     rows, columns = x_ref.shape[0], x_ref.shape[1]
     coarse_fields(chain, *fields, load, w)
     total = rows + 2 * DEEP
@@ -510,18 +510,17 @@
 
 
 def after_kernel(
-    chain, f_ref, m_own, v_ref, x_ref, fine_e, fine_o, lane_e, lane_o, corner_e, corner_o, *refs
+    chain, m_own, v_ref, x_ref, load, w, coarse_load, coarse_w,
+    coarse_e, coarse_o, coarse_lane_e, coarse_lane_o,
+    value_e, value_o, value_lane_e, value_lane_o, *rest,
 ):
-    fields, (value_e, value_o, value_lane_e, value_lane_o), rest = refs[:10], refs[10:14], refs[14:]
-    u_hbm, d_hbm, a, b, load, w, x, y, coarse_load, coarse_w, spread, sems = rest[-12:]
-    coarse_e, coarse_o, _, _, coarse_lane_e, coarse_lane_o = fields[2:8]
+    u_hbm, d_hbm, a, b, x, y, spread, sems = rest[-8:]
     even_b, even_l = place("band")[0], place("lane")[0]
     rows, columns = m_own.shape[0], m_own.shape[1]
     half_rows, half_columns = rows // 2, columns // 2
     layers = pl.ds(chain * LANES, LANES)
     fine_own = pl.ds(TILE, columns)
     left, right = pl.ds(0, TILE), pl.ds(TILE + columns, TILE)
-    coarse_fields(chain, *fields, coarse_load, coarse_w)
     own = pl.ds(TILE, half_columns)
     total = half_rows + 2 * DEEP
     low, high = by_side(even_b, value_e[...], value_o[...])
@@ -547,9 +546,6 @@
         edge = DEEP - SECOND + step
         sweep(source, target, coarse_load, coarse_w, edge, total - edge)
         source, target = target, source
-
-    own_fields(f_ref, m_own, load, w)
-    fine_halo(rows, columns, fine_e, fine_o, (lane_e, lane_o, corner_e, corner_o), load, w)
 
     a[FINE - 1] = v_ref[FINE - 1]
     a[FINE + rows] = v_ref[FINE + rows]
@@ -684,18 +680,20 @@
     send((m_e, m_o, n_e, n_o))
     masses, mass_lanes = fines[-1], fine_lanes[-1]
     owns = [owns[3 * c : 3 * c + 3] for c in chains]
-    fine_corners, values, loads, coarses = [], [], [], []
+    fine_corners, values, loads, coarses, fields = [], [], [], [], []
     for c in chains:
         strips = call(
             fine_corner_kernel, c, [(2 * CORNER, TILE, LANES)] * 2, (*owns[c], *fines[c], *loads), 4
         )
         fine_corners.append(swap("lane", *strips))
-        v, load, *strips = call(
+        v, load, *strips, load_wide, w_wide = call(
             before_kernel, c,
-            [(end, wide, LANES), coarse_block] + [(DEEP + 4, half_columns, LANES)] * 2,
-            (*owns[c], *fines[c], *fine_lanes[c], *fine_corners[c]), 16, us=6,
-            scratch=[(end, wide)] * 4 + [(half_rows, columns)],
-        )
+            [(end, wide, LANES), coarse_block] + [(DEEP + 4, half_columns, LANES)] * 2
+            + [(end, wide, LANES)] * 2,
+            (*owns[c], *fines[c], *fine_lanes[c], *fine_corners[c]), 10, us=6,
+            scratch=[(end, wide)] * 2 + [(half_rows, columns)],
+        )
+        fields.append((load_wide, w_wide))
         values.append(v)
         loads.append(load)
         coarses.append(swap("band", *strips))
@@ -706,13 +704,15 @@
             coarse_pack_kernel, c, [(lane_rows, TILE, LANES)] * 2, (loads[c], values[c], *coarses[c], *masses, *loads[c + 1 :]), 4
         )
         coarse_lanes.append(swap("lane", *strips))
-    fields, xs, nexts = [], [], []
+    xs, nexts = [], []
     for c in chains:
-        fields.append((loads[c], mass, *coarses[c], *masses, *coarse_lanes[c], *mass_lanes))
-        x, *strips = call(
-            coarse_kernel, c, [coarse_block] + [(SECOND, half_columns, LANES)] * 2,
-            fields[c], 8, us=4, scratch=[(total, half_wide)] * 4,
-        )
+        x, *strips, load_wide, w_wide = call(
+            coarse_kernel, c,
+            [coarse_block] + [(SECOND, half_columns, LANES)] * 2 + [(total, half_wide, LANES)] * 2,
+            (loads[c], mass, *coarses[c], *masses, *coarse_lanes[c], *mass_lanes), 6, us=4,
+            scratch=[(total, half_wide)] * 2,
+        )
+        fields[c] += (load_wide, w_wide)
         xs.append(x)
         nexts.append(swap("band", *strips))
     next_lanes = []
@@ -724,13 +724,12 @@
     results = ()
     for c in chains:
         args = (
-            *owns[c][1:], values[c], xs[c], *fines[c], *fine_lanes[c], *fine_corners[c],
-            *fields[c], *nexts[c], *next_lanes[c],
+            owns[c][2], values[c], xs[c], *fields[c], *coarses[c], *coarse_lanes[c], *nexts[c], *next_lanes[c],
         )
         results = tuple(
             call(
-                after_kernel, c, [(rows, columns, layers)] * 2, args + results, 20, us=8,
-                scratch=[(end, wide)] * 4 + [(total, half_wide)] * 4 + [(half_rows + 4, wide)],
+                after_kernel, c, [(rows, columns, layers)] * 2, args + results, 12, us=8,
+                scratch=[(end, wide)] * 2 + [(total, half_wide)] * 2 + [(half_rows + 4, wide)],
                 sems=2 * CHUNKS, hbm_out=True, extra=len(results),
                 aliases={len(args) + k: k for k in range(len(results))},
             )

time: 169 us -> 165 us (0.976)
  Pallas kernels: 47.3 us -> 44.1 us
    pallas_call x14, Pallas kernels: 47.3 us -> 44.1 us  [call(): pl.pallas_call(functools.partial(kernel, chain), in_specs=[far] * hbm + [...]
  transfers between devices with their start and end apart: 28 -> 28, of which waited for: 8 -> 7; matrix products, arithmetic and copies ran while one was open for 0% -> 0% of each run, Pallas kernels for 22% -> 21%
where the time goes in v4:
time: 165 us; the launch traced here: 163 us
  starting transfers between devices  75.3 us (46%)
  Pallas kernels  44.1 us (27%)
  waiting for transfers between devices  42.8 us (26%)
    ppermute x14, starting transfers between devices, swap(): lax.ppermute(odd, axis, swaps(count, 1))  44.5 us
    pallas_call x14, Pallas kernels, call(): pl.pallas_call(functools.partial(kernel, chain), in_specs=[far] * hbm + [...  44.1 us
    ppermute x14, starting transfers between devices, swap(): lax.ppermute(even, axis, swaps(count, 0))  30.8 us
    ppermute x14, waiting for transfers between devices, swap(): lax.ppermute(even, axis, swaps(count, 0))  25.5 us
    ppermute x14, waiting for transfers between devices, swap(): lax.ppermute(odd, axis, swaps(count, 1))  17.2 us
  transfers between devices with their start and end apart: 28, of which 7 were waited for; matrix products, arithmetic and copies ran while one was open for 0% of the time, Pallas kernels for 21%

profile of v4, /device:TPU:109, one launch (start us, length us, event | category | flops | bytes accessed | tf_op | source)
XLA Modules:
  0.0 163.2 jit_solution(12296796898067322680)
XLA Ops:
  0.6 2.8 %shard_map.51 = (f32[10,64,128]{2,1,0:T(8,128)}, f32[10,64,128]{2,1,0:T(8,128)}, f32[64,8,128]{2,1,0:T(8,128)}, f32[64,8,128]{2,1,0:T(8,128)}) custom-call(f32[64,64,256]{2,1,0:T(8,128)} %u_hbm.3, f32[64,64,256]{2,1,0:T(8,128)} %f_hbm.3, f32[64,64,256]{2,1,0:T(8,128)} %m_hbm.3), custom_call_target="tpu_custom_call" | custom-call | flops 2000000000 | tf_op jit(solution)/shard_map/pallas_call | solution.py:639
  4.2 4.6 %collective-permute-start.5 = (f32[10,64,128]{2,1,0:T(8,128)}, f32[10,64,128]{2,1,0:T(8,128)S(1)}, u32[]{:S(2)}, u32[]{:S(2)}) collective-permute-start(f32[10,64,128]{2,1,0:T(8,128)} %get-tuple-element.64), channel_id=1, source_target_pairs={{8,16},{16,8},{24,32},{32,24},{40,48},{48,40},{56,64},{64,56},{72,... | collective-permute-start | bytes 983048 | tf_op jit(solution)/shard_map/ppermute | solution.py:36
  12.7 6.0 %shard_map.50 = (f32[64,64,128]{2,1,0:T(8,128)S(1)}, f32[64,64,128]{2,1,0:T(8,128)S(1)}, f32[64,64,128]{2,1,0:T(8,128)S(1)}, f32[64,64,128]{2,1,0:T(8,128)S(1)},...) custom-call(f32[64,64,256]{2,1,0:T(8,128)} %u_hbm.3, ...), custom_call_target="tpu_custom_call" | custom-call | flops 4000000000 | tf_op jit(solution)/shard_map/pallas_call | solution.py:639
  19.7 6.6 %collective-permute-start.1 = (f32[18,64,128]{2,1,0:T(8,128)S(1)}, f32[18,64,128]{2,1,0:T(8,128)S(1)}, u32[]{:S(2)}, u32[]{:S(2)}) collective-permute-start(f32[18,64,128]{2,1,0:T(8,128)S(1)} %get-tuple-element.57), channel_id=1, source_target_pairs={{8,16},{16,8},{24,32},{32,24},{40,48},{48,40},{56,64},{64,56},{72,... | collective-permute-start | bytes 1769480 | tf_op jit(solution)/shard_map/ppermute | solution.py:36
  27.4 2.2 %collective-permute-start.3 = (f32[128,8,128]{2,1,0:T(8,128)S(1)}, f32[128,8,128]{2,1,0:T(8,128)S(1)}, u32[]{:S(2)}, u32[]{:S(2)}) collective-permute-start(f32[128,8,128]{2,1,0:T(8,128)S(1)} %get-tuple-element.59), channel_id=1, source_target_pairs={{1,2},{2,1},{3,4},{4,3},{5,6},{6,5},{9,10},{10,9},{11,12},{12,11},... | collective-permute-start | bytes 1572872 | tf_op jit(solution)/shard_map/ppermute | solution.py:36
  29.8 2.2 %collective-permute-start.8 = (f32[10,8,128]{2,1,0:T(8,128)S(1)}, f32[10,8,128]{2,1,0:T(8,128)S(1)}, u32[]{:S(2)}, u32[]{:S(2)}) collective-permute-start(f32[10,8,128]{2,1,0:T(8,128)S(1)} %get-tuple-element.67), channel_id=1, source_target_pairs={{0,1},{1,0},{2,3},{3,2},{4,5},{5,4},{6,7},{7,6},{8,9},{9,8},{10,11... | collective-permute-start | bytes 122888 | tf_op jit(solution)/shard_map/ppermute | solution.py:35
  32.0 24.7 %collective-permute-done.8.corner_e = f32[10,8,128]{2,1,0:T(8,128)S(1)} collective-permute-done((f32[10,8,128]{2,1,0:T(8,128)S(1)}, f32[10,8,128]{2,1,0:T(8,128)S(1)}, u32[]{:S(2)}, u32[]{:S(2)}) %collective-permute-start.8) | collective-permute-done | bytes 40992 | tf_op jit(solution)/shard_map/ppermute | solution.py:35
  56.6 2.0 %collective-permute-start.9 = (f32[10,8,128]{2,1,0:T(8,128)S(1)}, f32[10,8,128]{2,1,0:T(8,128)S(1)}, u32[]{:S(2)}, u32[]{:S(2)}) collective-permute-start(f32[10,8,128]{2,1,0:T(8,128)S(1)} %get-tuple-element.68), channel_id=1, source_target_pairs={{1,2},{2,1},{3,4},{4,3},{5,6},{6,5},{9,10},{10,9},{11,12},{12,11},... | collective-permute-start | bytes 122888 | tf_op jit(solution)/shard_map/ppermute | solution.py:36
  58.7 4.4 %collective-permute-done.9.corner_o = f32[10,8,128]{2,1,0:T(8,128)S(1)} collective-permute-done((f32[10,8,128]{2,1,0:T(8,128)S(1)}, f32[10,8,128]{2,1,0:T(8,128)S(1)}, u32[]{:S(2)}, u32[]{:S(2)}) %collective-permute-start.9) | collective-permute-done | bytes 40992 | tf_op jit(solution)/shard_map/ppermute | solution.py:36
  63.1 6.5 %shard_map.53 = (f32[72,80,128]{2,1,0:T(8,128)S(1)}, f32[32,32,128]{2,1,0:T(8,128)S(1)}, f32[12,32,128]{2,1,0:T(8,128)S(1)}, f32[12,32,128]{2,1,0:T(8,128)S(1)},...) custom-call(f32[64,64,128]{2,1,0:T(8,128)S(1)} %get-tuple-element.60.u_ref, ...), custom_call_target="tpu_custom_call" | custom-call | flops 3000000000 | tf_op jit(solution)/shard_map/pallas_call | solution.py:639
  70.4 1.9 %collective-permute-start.11 = (f32[10,8,128]{2,1,0:T(8,128)S(1)}, f32[10,8,128]{2,1,0:T(8,128)S(1)}, u32[]{:S(2)}, u32[]{:S(2)}) collective-permute-start(f32[10,8,128]{2,1,0:T(8,128)S(1)} %get-tuple-element.71), channel_id=1, source_target_pairs={{1,2},{2,1},{3,4},{4,3},{5,6},{6,5},{9,10},{10,9},{11,12},{12,11},... | collective-permute-start | bytes 122888 | tf_op jit(solution)/shard_map/ppermute | solution.py:36
  72.3 8.8 %collective-permute-start.20 = (f32[12,32,128]{2,1,0:T(8,128)S(1)}, f32[12,32,128]{2,1,0:T(8,128)S(1)}, u32[]{:S(2)}, u32[]{:S(2)}) collective-permute-start(f32[12,32,128]{2,1,0:T(8,128)S(1)} %get-tuple-element.89), channel_id=1, source_target_pairs={{0,8},{8,0},{16,24},{24,16},{32,40},{40,32},{48,56},{56,48},{64,72... | collective-permute-start | bytes 589832 | tf_op jit(solution)/shard_map/ppermute | solution.py:35
  81.1 4.5 %collective-permute-start.21 = (f32[12,32,128]{2,1,0:T(8,128)S(1)}, f32[12,32,128]{2,1,0:T(8,128)S(1)}, u32[]{:S(2)}, u32[]{:S(2)}) collective-permute-start(f32[12,32,128]{2,1,0:T(8,128)S(1)} %get-tuple-element.90), channel_id=1, source_target_pairs={{8,16},{16,8},{24,32},{32,24},{40,48},{48,40},{56,64},{64,56},{72,... | collective-permute-start | bytes 589832 | tf_op jit(solution)/shard_map/ppermute | solution.py:36
  85.7 6.5 %shard_map.55 = (f32[72,80,128]{2,1,0:T(8,128)S(1)}, f32[32,32,128]{2,1,0:T(8,128)S(1)}, f32[12,32,128]{2,1,0:T(8,128)S(1)}, f32[12,32,128]{2,1,0:T(8,128)S(1)},...) custom-call(f32[64,64,128]{2,1,0:T(8,128)S(1)} %get-tuple-element.54.u_ref, ...), custom_call_target="tpu_custom_call" | custom-call | flops 3000000000 | tf_op jit(solution)/shard_map/pallas_call | solution.py:639
  92.5 5.1 %collective-permute-start.13 = (f32[12,32,128]{2,1,0:T(8,128)S(1)}, f32[12,32,128]{2,1,0:T(8,128)S(1)}, u32[]{:S(2)}, u32[]{:S(2)}) collective-permute-start(f32[12,32,128]{2,1,0:T(8,128)S(1)} %get-tuple-element.76), channel_id=1, source_target_pairs={{8,16},{16,8},{24,32},{32,24},{40,48},{48,40},{56,64},{64,56},{72,... | collective-permute-start | bytes 589832 | tf_op jit(solution)/shard_map/ppermute | solution.py:36
  97.7 2.8 %collective-permute-start.22 = (f32[65,8,128]{2,1,0:T(8,128)S(1)}, f32[65,8,128]{2,1,0:T(8,128)S(1)}, u32[]{:S(2)}, u32[]{:S(2)}) collective-permute-start(f32[65,8,128]{2,1,0:T(8,128)S(1)} %get-tuple-element.91), channel_id=1, source_target_pairs={{0,1},{1,0},{2,3},{3,2},{4,5},{5,4},{6,7},{7,6},{8,9},{9,8},{10,11... | collective-permute-start | bytes 798728 | tf_op jit(solution)/shard_map/ppermute | solution.py:35
  100.5 1.9 %collective-permute-start.23 = (f32[65,8,128]{2,1,0:T(8,128)S(1)}, f32[65,8,128]{2,1,0:T(8,128)S(1)}, u32[]{:S(2)}, u32[]{:S(2)}) collective-permute-start(f32[65,8,128]{2,1,0:T(8,128)S(1)} %get-tuple-element.92), channel_id=1, source_target_pairs={{1,2},{2,1},{3,4},{4,3},{5,6},{6,5},{9,10},{10,9},{11,12},{12,11},... | collective-permute-start | bytes 798728 | tf_op jit(solution)/shard_map/ppermute | solution.py:36
  103.3 3.0 %collective-permute-start.14 = (f32[65,8,128]{2,1,0:T(8,128)S(1)}, f32[65,8,128]{2,1,0:T(8,128)S(1)}, u32[]{:S(2)}, u32[]{:S(2)}) collective-permute-start(f32[65,8,128]{2,1,0:T(8,128)S(1)} %get-tuple-element.77), channel_id=1, source_target_pairs={{0,1},{1,0},{2,3},{3,2},{4,5},{5,4},{6,7},{7,6},{8,9},{9,8},{10,11... | collective-permute-start | bytes 798728 | tf_op jit(solution)/shard_map/ppermute | solution.py:35
  106.3 1.9 %collective-permute-start.15 = (f32[65,8,128]{2,1,0:T(8,128)S(1)}, f32[65,8,128]{2,1,0:T(8,128)S(1)}, u32[]{:S(2)}, u32[]{:S(2)}) collective-permute-start(f32[65,8,128]{2,1,0:T(8,128)S(1)} %get-tuple-element.78), channel_id=1, source_target_pairs={{1,2},{2,1},{3,4},{4,3},{5,6},{6,5},{9,10},{10,9},{11,12},{12,11},... | collective-permute-start | bytes 798728 | tf_op jit(solution)/shard_map/ppermute | solution.py:36
  108.2 5.0 %collective-permute-done.23.refs_7_.coarse_lane_o = f32[65,8,128]{2,1,0:T(8,128)S(1)} collective-permute-done((f32[65,8,128]{2,1,0:T(8,128)S(1)}, f32[65,8,128]{2,1,0:T(8,128)S(1)}, u32[]{:S(2)}, u32[]{:S(2)}) %collective-permute-start.23) | collective-permute-done | bytes 266272 | tf_op jit(solution)/shard_map/ppermute | solution.py:36
  113.2 4.4 %shard_map.60 = (f32[32,32,128]{2,1,0:T(8,128)S(1)}, f32[6,32,128]{2,1,0:T(8,128)S(1)}, f32[6,32,128]{2,1,0:T(8,128)S(1)}, f32[48,48,128]{2,1,0:T(8,128)S(1)}, f32[48,48,128]{2,1,0:T(8,128)S(1)}) custom-call(f32[32,32,128]{2,1,0:T(8,128)S(1)} %get-tuple-element.69.refs_0_.load_ref, f32[2,32,32,128]{3,2,1,0:T(8,128)S(1)} %get-tuple-element.74.refs_1_, ...), custom_call_target="tpu_custom_call" | custom-call | flops 2000000000 | tf_op jit(solution)/shard_map/pallas_call | solution.py:639
  117.6 3.5 %collective-permute-start.24 = (f32[6,32,128]{2,1,0:T(8,128)S(1)}, f32[6,32,128]{2,1,0:T(8,128)S(1)}, u32[]{:S(2)}, u32[]{:S(2)}) collective-permute-start(f32[6,32,128]{2,1,0:T(8,128)S(1)} %get-tuple-element.98), channel_id=1, source_target_pairs={{0,8},{8,0},{16,24},{24,16},{32,40},{40,32},{48,56},{56,48},{64,72... | collective-permute-start | bytes 294920 | tf_op jit(solution)/shard_map/ppermute | solution.py:35
  121.1 3.5 %collective-permute-start.25 = (f32[6,32,128]{2,1,0:T(8,128)S(1)}, f32[6,32,128]{2,1,0:T(8,128)S(1)}, u32[]{:S(2)}, u32[]{:S(2)}) collective-permute-start(f32[6,32,128]{2,1,0:T(8,128)S(1)} %get-tuple-element.99), channel_id=1, source_target_pairs={{8,16},{16,8},{24,32},{32,24},{40,48},{48,40},{56,64},{64,56},{72,... | collective-permute-start | bytes 294920 | tf_op jit(solution)/shard_map/ppermute | solution.py:36
  124.6 4.0 %shard_map.57 = (f32[32,32,128]{2,1,0:T(8,128)S(1)}, f32[6,32,128]{2,1,0:T(8,128)S(1)}, f32[6,32,128]{2,1,0:T(8,128)S(1)}, f32[48,48,128]{2,1,0:T(8,128)S(1)}, f32[48,48,128]{2,1,0:T(8,128)S(1)}) custom-call(f32[32,32,128]{2,1,0:T(8,128)S(1)} %get-tuple-element.73.load_ref.refs_0_, f32[2,32,32,128]{3,2,1,0:T(8,128)S(1)} %get-tuple-element.74.refs_1_, ...), custom_call_target="tpu_custom_call" | custom-call | flops 2000000000 | tf_op jit(solution)/shard_map/pallas_call | solution.py:639
  128.7 1.9 %collective-permute-done.25.got_o.value_o = f32[6,32,128]{2,1,0:T(8,128)S(1)} collective-permute-done((f32[6,32,128]{2,1,0:T(8,128)S(1)}, f32[6,32,128]{2,1,0:T(8,128)S(1)}, u32[]{:S(2)}, u32[]{:S(2)}) %collective-permute-start.25) | collective-permute-done | bytes 98336 | tf_op jit(solution)/shard_map/ppermute | solution.py:36
  132.1 1.9 %collective-permute-start.27 = (f32[39,8,128]{2,1,0:T(8,128)S(1)}, f32[39,8,128]{2,1,0:T(8,128)S(1)}, u32[]{:S(2)}, u32[]{:S(2)}) collective-permute-start(f32[39,8,128]{2,1,0:T(8,128)S(1)} %get-tuple-element.101), channel_id=1, source_target_pairs={{1,2},{2,1},{3,4},{4,3},{5,6},{6,5},{9,10},{10,9},{11,12},{12,11},... | collective-permute-start | bytes 479240 | tf_op jit(solution)/shard_map/ppermute | solution.py:36
  134.5 4.4 %collective-permute-start.17 = (f32[6,32,128]{2,1,0:T(8,128)S(1)}, f32[6,32,128]{2,1,0:T(8,128)S(1)}, u32[]{:S(2)}, u32[]{:S(2)}) collective-permute-start(f32[6,32,128]{2,1,0:T(8,128)S(1)} %get-tuple-element.85), channel_id=1, source_target_pairs={{8,16},{16,8},{24,32},{32,24},{40,48},{48,40},{56,64},{64,56},{72,... | collective-permute-start | bytes 294920 | tf_op jit(solution)/shard_map/ppermute | solution.py:36
  138.9 5.1 %collective-permute-done.17.got_o.value_o = f32[6,32,128]{2,1,0:T(8,128)S(1)} collective-permute-done((f32[6,32,128]{2,1,0:T(8,128)S(1)}, f32[6,32,128]{2,1,0:T(8,128)S(1)}, u32[]{:S(2)}, u32[]{:S(2)}) %collective-permute-start.17) | collective-permute-done | bytes 98336 | tf_op jit(solution)/shard_map/ppermute | solution.py:36
  144.1 3.7 %collective-permute-start.18 = (f32[39,8,128]{2,1,0:T(8,128)S(1)}, f32[39,8,128]{2,1,0:T(8,128)S(1)}, u32[]{:S(2)}, u32[]{:S(2)}) collective-permute-start(f32[39,8,128]{2,1,0:T(8,128)S(1)} %get-tuple-element.86), channel_id=1, source_target_pairs={{0,1},{1,0},{2,3},{3,2},{4,5},{5,4},{6,7},{7,6},{8,9},{9,8},{10,11... | collective-permute-start | bytes 479240 | tf_op jit(solution)/shard_map/ppermute | solution.py:35
  147.8 1.9 %collective-permute-start.19 = (f32[39,8,128]{2,1,0:T(8,128)S(1)}, f32[39,8,128]{2,1,0:T(8,128)S(1)}, u32[]{:S(2)}, u32[]{:S(2)}) collective-permute-start(f32[39,8,128]{2,1,0:T(8,128)S(1)} %get-tuple-element.87), channel_id=1, source_target_pairs={{1,2},{2,1},{3,4},{4,3},{5,6},{6,5},{9,10},{10,9},{11,12},{12,11},... | collective-permute-start | bytes 479240 | tf_op jit(solution)/shard_map/ppermute | solution.py:36
  149.8 6.7 %shard_map.62 = (f32[64,64,256]{2,1,0:T(8,128)}, f32[64,64,256]{2,1,0:T(8,128)}) custom-call(f32[64,64,128]{2,1,0:T(8,128)S(1)} %get-tuple-element.62.m_ref.m_own, f32[72,80,128]{2,1,0:T(8,128)S(1)} %get-tuple-element.88.v_ref, f32[32,32,128]{2,1,0:T(8,128)S(1)} %get-tuple-element.93.x_ref, f32[72,80,128]{2,1,0:T(8,128)S(1)} %get-tuple-element.94.load, ...), custom_call_target="tpu_custom_call" | custom-call | flops 4000000000 | tf_op jit(solution)/shard_map/pallas_call | solution.py:639
  156.5 6.6 %shard_map.63 = (f32[64,64,256]{2,1,0:T(8,128)}, f32[64,64,256]{2,1,0:T(8,128)}) custom-call(f32[64,64,128]{2,1,0:T(8,128)S(1)} %copy-done, f32[72,80,128]{2,1,0:T(8,128)S(1)} %get-tuple-element.72.v_ref, f32[32,32,128]{2,1,0:T(8,128)S(1)} %get-tuple-element.79.x_ref.refs_0_, ...), custom_call_target="tpu_custom_call", output_to_operand_aliasing={{0}: (15, {}), {1}: (16, {})} | custom-call | flops 4000000000 | tf_op jit(solution)/shard_map/pallas_call | solution.py:639
  (40 shorter events, 10.6 us)
Async XLA Ops:
  3.5 22.8 %collective-permute-start.4 = (f32[10,64,128]{2,1,0:T(8,128)}, f32[10,64,128]{2,1,0:T(8,128)S(1)}, u32[]{:S(2)}, u32[]{:S(2)}) collective-permute-start(f32[10,64,128]{2,1,0:T(8,128)} %get-tuple-element.63), channel_id=1, source_target_pairs={{0,8},{8,0},{16,24},{24,16},{32,40},{40,32},{48,56},{56,48},{64,72... | collective-permute-start | bytes 983048 | tf_op jit(solution)/shard_map/ppermute | solution.py:35
  4.2 23.2 %collective-permute-start.5 = (f32[10,64,128]{2,1,0:T(8,128)}, f32[10,64,128]{2,1,0:T(8,128)S(1)}, u32[]{:S(2)}, u32[]{:S(2)}) collective-permute-start(f32[10,64,128]{2,1,0:T(8,128)} %get-tuple-element.64), channel_id=1, source_target_pairs={{8,16},{16,8},{24,32},{32,24},{40,48},{48,40},{56,64},{64,56},{72,... | collective-permute-start | bytes 983048 | tf_op jit(solution)/shard_map/ppermute | solution.py:36
  8.9 10.8 %collective-permute-start.6 = (f32[64,8,128]{2,1,0:T(8,128)}, f32[64,8,128]{2,1,0:T(8,128)S(1)}, u32[]{:S(2)}, u32[]{:S(2)}) collective-permute-start(f32[64,8,128]{2,1,0:T(8,128)} %get-tuple-element.65), channel_id=1, source_target_pairs={{0,1},{1,0},{2,3},{3,2},{4,5},{5,4},{6,7},{7,6},{8,9},{9,8},{10,11... | collective-permute-start | bytes 786440 | tf_op jit(solution)/shard_map/ppermute | solution.py:35
  10.8 19.0 %collective-permute-start.7 = (f32[64,8,128]{2,1,0:T(8,128)}, f32[64,8,128]{2,1,0:T(8,128)S(1)}, u32[]{:S(2)}, u32[]{:S(2)}) collective-permute-start(f32[64,8,128]{2,1,0:T(8,128)} %get-tuple-element.66), channel_id=1, source_target_pairs={{1,2},{2,1},{3,4},{4,3},{5,6},{6,5},{9,10},{10,9},{11,12},{12,11},... | collective-permute-start | bytes 786440 | tf_op jit(solution)/shard_map/ppermute | solution.py:36
  18.7 50.9 %collective-permute-start = (f32[18,64,128]{2,1,0:T(8,128)S(1)}, f32[18,64,128]{2,1,0:T(8,128)S(1)}, u32[]{:S(2)}, u32[]{:S(2)}) collective-permute-start(f32[18,64,128]{2,1,0:T(8,128)S(1)} %get-tuple-element.56), channel_id=1, source_target_pairs={{0,8},{8,0},{16,24},{24,16},{32,40},{40,32},{48,56},{56,48},{64,72... | collective-permute-start | bytes 1769480 | tf_op jit(solution)/shard_map/ppermute | solution.py:35
  19.7 50.0 %collective-permute-start.1 = (f32[18,64,128]{2,1,0:T(8,128)S(1)}, f32[18,64,128]{2,1,0:T(8,128)S(1)}, u32[]{:S(2)}, u32[]{:S(2)}) collective-permute-start(f32[18,64,128]{2,1,0:T(8,128)S(1)} %get-tuple-element.57), channel_id=1, source_target_pairs={{8,16},{16,8},{24,32},{32,24},{40,48},{48,40},{56,64},{64,56},{72,... | collective-permute-start | bytes 1769480 | tf_op jit(solution)/shard_map/ppermute | solution.py:36
  26.3 54.8 %collective-permute-start.2 = (f32[128,8,128]{2,1,0:T(8,128)S(1)}, f32[128,8,128]{2,1,0:T(8,128)S(1)}, u32[]{:S(2)}, u32[]{:S(2)}) collective-permute-start(f32[128,8,128]{2,1,0:T(8,128)S(1)} %get-tuple-element.58), channel_id=1, source_target_pairs={{0,1},{1,0},{2,3},{3,2},{4,5},{5,4},{6,7},{7,6},{8,9},{9,8},{10,11... | collective-permute-start | bytes 1572872 | tf_op jit(solution)/shard_map/ppermute | solution.py:35
  27.4 58.2 %collective-permute-start.3 = (f32[128,8,128]{2,1,0:T(8,128)S(1)}, f32[128,8,128]{2,1,0:T(8,128)S(1)}, u32[]{:S(2)}, u32[]{:S(2)}) collective-permute-start(f32[128,8,128]{2,1,0:T(8,128)S(1)} %get-tuple-element.59), channel_id=1, source_target_pairs={{1,2},{2,1},{3,4},{4,3},{5,6},{6,5},{9,10},{10,9},{11,12},{12,11},... | collective-permute-start | bytes 1572872 | tf_op jit(solution)/shard_map/ppermute | solution.py:36
  29.8 26.9 %collective-permute-start.8 = (f32[10,8,128]{2,1,0:T(8,128)S(1)}, f32[10,8,128]{2,1,0:T(8,128)S(1)}, u32[]{:S(2)}, u32[]{:S(2)}) collective-permute-start(f32[10,8,128]{2,1,0:T(8,128)S(1)} %get-tuple-element.67), channel_id=1, source_target_pairs={{0,1},{1,0},{2,3},{3,2},{4,5},{5,4},{6,7},{7,6},{8,9},{9,8},{10,11... | collective-permute-start | bytes 122888 | tf_op jit(solution)/shard_map/ppermute | solution.py:35
  56.6 13.0 %copy-start = (f32[64,64,128]{2,1,0:T(8,128)S(1)}, f32[64,64,128]{2,1,0:T(8,128)}, u32[]{:S(2)}) copy-start(f32[64,64,128]{2,1,0:T(8,128)} %get-tuple-element.53.m_ref.m_own) | copy-start | bytes 6291460
  56.6 6.5 %collective-permute-start.9 = (f32[10,8,128]{2,1,0:T(8,128)S(1)}, f32[10,8,128]{2,1,0:T(8,128)S(1)}, u32[]{:S(2)}, u32[]{:S(2)}) collective-permute-start(f32[10,8,128]{2,1,0:T(8,128)S(1)} %get-tuple-element.68), channel_id=1, source_target_pairs={{1,2},{2,1},{3,4},{4,3},{5,6},{6,5},{9,10},{10,9},{11,12},{12,11},... | collective-permute-start | bytes 122888 | tf_op jit(solution)/shard_map/ppermute | solution.py:36
  69.8 15.9 %collective-permute-start.10 = (f32[10,8,128]{2,1,0:T(8,128)S(1)}, f32[10,8,128]{2,1,0:T(8,128)S(1)}, u32[]{:S(2)}, u32[]{:S(2)}) collective-permute-start(f32[10,8,128]{2,1,0:T(8,128)S(1)} %get-tuple-element.70), channel_id=1, source_target_pairs={{0,1},{1,0},{2,3},{3,2},{4,5},{5,4},{6,7},{7,6},{8,9},{9,8},{10,11... | collective-permute-start | bytes 122888 | tf_op jit(solution)/shard_map/ppermute | solution.py:35
  70.4 15.3 %collective-permute-start.11 = (f32[10,8,128]{2,1,0:T(8,128)S(1)}, f32[10,8,128]{2,1,0:T(8,128)S(1)}, u32[]{:S(2)}, u32[]{:S(2)}) collective-permute-start(f32[10,8,128]{2,1,0:T(8,128)S(1)} %get-tuple-element.71), channel_id=1, source_target_pairs={{1,2},{2,1},{3,4},{4,3},{5,6},{6,5},{9,10},{10,9},{11,12},{12,11},... | collective-permute-start | bytes 122888 | tf_op jit(solution)/shard_map/ppermute | solution.py:36
  72.3 25.3 %collective-permute-start.20 = (f32[12,32,128]{2,1,0:T(8,128)S(1)}, f32[12,32,128]{2,1,0:T(8,128)S(1)}, u32[]{:S(2)}, u32[]{:S(2)}) collective-permute-start(f32[12,32,128]{2,1,0:T(8,128)S(1)} %get-tuple-element.89), channel_id=1, source_target_pairs={{0,8},{8,0},{16,24},{24,16},{32,40},{40,32},{48,56},{56,48},{64,72... | collective-permute-start | bytes 589832 | tf_op jit(solution)/shard_map/ppermute | solution.py:35
  81.1 16.5 %collective-permute-start.21 = (f32[12,32,128]{2,1,0:T(8,128)S(1)}, f32[12,32,128]{2,1,0:T(8,128)S(1)}, u32[]{:S(2)}, u32[]{:S(2)}) collective-permute-start(f32[12,32,128]{2,1,0:T(8,128)S(1)} %get-tuple-element.90), channel_id=1, source_target_pairs={{8,16},{16,8},{24,32},{32,24},{40,48},{48,40},{56,64},{64,56},{72,... | collective-permute-start | bytes 589832 | tf_op jit(solution)/shard_map/ppermute | solution.py:36
  92.2 10.2 %collective-permute-start.12 = (f32[12,32,128]{2,1,0:T(8,128)S(1)}, f32[12,32,128]{2,1,0:T(8,128)S(1)}, u32[]{:S(2)}, u32[]{:S(2)}) collective-permute-start(f32[12,32,128]{2,1,0:T(8,128)S(1)} %get-tuple-element.75), channel_id=1, source_target_pairs={{0,8},{8,0},{16,24},{24,16},{32,40},{40,32},{48,56},{56,48},{64,72... | collective-permute-start | bytes 589832 | tf_op jit(solution)/shard_map/ppermute | solution.py:35
  92.5 10.7 %collective-permute-start.13 = (f32[12,32,128]{2,1,0:T(8,128)S(1)}, f32[12,32,128]{2,1,0:T(8,128)S(1)}, u32[]{:S(2)}, u32[]{:S(2)}) collective-permute-start(f32[12,32,128]{2,1,0:T(8,128)S(1)} %get-tuple-element.76), channel_id=1, source_target_pairs={{8,16},{16,8},{24,32},{32,24},{40,48},{48,40},{56,64},{64,56},{72,... | collective-permute-start | bytes 589832 | tf_op jit(solution)/shard_map/ppermute | solution.py:36
  97.7 10.5 %collective-permute-start.22 = (f32[65,8,128]{2,1,0:T(8,128)S(1)}, f32[65,8,128]{2,1,0:T(8,128)S(1)}, u32[]{:S(2)}, u32[]{:S(2)}) collective-permute-start(f32[65,8,128]{2,1,0:T(8,128)S(1)} %get-tuple-element.91), channel_id=1, source_target_pairs={{0,1},{1,0},{2,3},{3,2},{4,5},{5,4},{6,7},{7,6},{8,9},{9,8},{10,11... | collective-permute-start | bytes 798728 | tf_op jit(solution)/shard_map/ppermute | solution.py:35
  100.5 12.7 %collective-permute-start.23 = (f32[65,8,128]{2,1,0:T(8,128)S(1)}, f32[65,8,128]{2,1,0:T(8,128)S(1)}, u32[]{:S(2)}, u32[]{:S(2)}) collective-permute-start(f32[65,8,128]{2,1,0:T(8,128)S(1)} %get-tuple-element.92), channel_id=1, source_target_pairs={{1,2},{2,1},{3,4},{4,3},{5,6},{6,5},{9,10},{10,9},{11,12},{12,11},... | collective-permute-start | bytes 798728 | tf_op jit(solution)/shard_map/ppermute | solution.py:36
  103.3 21.3 %collective-permute-start.14 = (f32[65,8,128]{2,1,0:T(8,128)S(1)}, f32[65,8,128]{2,1,0:T(8,128)S(1)}, u32[]{:S(2)}, u32[]{:S(2)}) collective-permute-start(f32[65,8,128]{2,1,0:T(8,128)S(1)} %get-tuple-element.77), channel_id=1, source_target_pairs={{0,1},{1,0},{2,3},{3,2},{4,5},{5,4},{6,7},{7,6},{8,9},{9,8},{10,11... | collective-permute-start | bytes 798728 | tf_op jit(solution)/shard_map/ppermute | solution.py:35
  106.3 18.3 %collective-permute-start.15 = (f32[65,8,128]{2,1,0:T(8,128)S(1)}, f32[65,8,128]{2,1,0:T(8,128)S(1)}, u32[]{:S(2)}, u32[]{:S(2)}) collective-permute-start(f32[65,8,128]{2,1,0:T(8,128)S(1)} %get-tuple-element.78), channel_id=1, source_target_pairs={{1,2},{2,1},{3,4},{4,3},{5,6},{6,5},{9,10},{10,9},{11,12},{12,11},... | collective-permute-start | bytes 798728 | tf_op jit(solution)/shard_map/ppermute | solution.py:36
  117.6 11.1 %collective-permute-start.24 = (f32[6,32,128]{2,1,0:T(8,128)S(1)}, f32[6,32,128]{2,1,0:T(8,128)S(1)}, u32[]{:S(2)}, u32[]{:S(2)}) collective-permute-start(f32[6,32,128]{2,1,0:T(8,128)S(1)} %get-tuple-element.98), channel_id=1, source_target_pairs={{0,8},{8,0},{16,24},{24,16},{32,40},{40,32},{48,56},{56,48},{64,72... | collective-permute-start | bytes 294920 | tf_op jit(solution)/shard_map/ppermute | solution.py:35
  121.1 9.5 %collective-permute-start.25 = (f32[6,32,128]{2,1,0:T(8,128)S(1)}, f32[6,32,128]{2,1,0:T(8,128)S(1)}, u32[]{:S(2)}, u32[]{:S(2)}) collective-permute-start(f32[6,32,128]{2,1,0:T(8,128)S(1)} %get-tuple-element.99), channel_id=1, source_target_pairs={{8,16},{16,8},{24,32},{32,24},{40,48},{48,40},{56,64},{64,56},{72,... | collective-permute-start | bytes 294920 | tf_op jit(solution)/shard_map/ppermute | solution.py:36
  130.7 19.1 %collective-permute-start.26 = (f32[39,8,128]{2,1,0:T(8,128)S(1)}, f32[39,8,128]{2,1,0:T(8,128)S(1)}, u32[]{:S(2)}, u32[]{:S(2)}) collective-permute-start(f32[39,8,128]{2,1,0:T(8,128)S(1)} %get-tuple-element.100), channel_id=1, source_target_pairs={{0,1},{1,0},{2,3},{3,2},{4,5},{5,4},{6,7},{7,6},{8,9},{9,8},{10,11... | collective-permute-start | bytes 479240 | tf_op jit(solution)/shard_map/ppermute | solution.py:35
  132.1 17.7 %collective-permute-start.27 = (f32[39,8,128]{2,1,0:T(8,128)S(1)}, f32[39,8,128]{2,1,0:T(8,128)S(1)}, u32[]{:S(2)}, u32[]{:S(2)}) collective-permute-start(f32[39,8,128]{2,1,0:T(8,128)S(1)} %get-tuple-element.101), channel_id=1, source_target_pairs={{1,2},{2,1},{3,4},{4,3},{5,6},{6,5},{9,10},{10,9},{11,12},{12,11},... | collective-permute-start | bytes 479240 | tf_op jit(solution)/shard_map/ppermute | solution.py:36
  134.0 4.9 %collective-permute-start.16 = (f32[6,32,128]{2,1,0:T(8,128)S(1)}, f32[6,32,128]{2,1,0:T(8,128)S(1)}, u32[]{:S(2)}, u32[]{:S(2)}) collective-permute-start(f32[6,32,128]{2,1,0:T(8,128)S(1)} %get-tuple-element.84), channel_id=1, source_target_pairs={{0,8},{8,0},{16,24},{24,16},{32,40},{40,32},{48,56},{56,48},{64,72... | collective-permute-start | bytes 294920 | tf_op jit(solution)/shard_map/ppermute | solution.py:35
  134.5 9.5 %collective-permute-start.17 = (f32[6,32,128]{2,1,0:T(8,128)S(1)}, f32[6,32,128]{2,1,0:T(8,128)S(1)}, u32[]{:S(2)}, u32[]{:S(2)}) collective-permute-start(f32[6,32,128]{2,1,0:T(8,128)S(1)} %get-tuple-element.85), channel_id=1, source_target_pairs={{8,16},{16,8},{24,32},{32,24},{40,48},{48,40},{56,64},{64,56},{72,... | collective-permute-start | bytes 294920 | tf_op jit(solution)/shard_map/ppermute | solution.py:36
  144.1 12.4 %collective-permute-start.18 = (f32[39,8,128]{2,1,0:T(8,128)S(1)}, f32[39,8,128]{2,1,0:T(8,128)S(1)}, u32[]{:S(2)}, u32[]{:S(2)}) collective-permute-start(f32[39,8,128]{2,1,0:T(8,128)S(1)} %get-tuple-element.86), channel_id=1, source_target_pairs={{0,1},{1,0},{2,3},{3,2},{4,5},{5,4},{6,7},{7,6},{8,9},{9,8},{10,11... | collective-permute-start | bytes 479240 | tf_op jit(solution)/shard_map/ppermute | solution.py:35
  147.8 8.7 %collective-permute-start.19 = (f32[39,8,128]{2,1,0:T(8,128)S(1)}, f32[39,8,128]{2,1,0:T(8,128)S(1)}, u32[]{:S(2)}, u32[]{:S(2)}) collective-permute-start(f32[39,8,128]{2,1,0:T(8,128)S(1)} %get-tuple-element.87), channel_id=1, source_target_pairs={{1,2},{2,1},{3,4},{4,3},{5,6},{6,5},{9,10},{10,9},{11,12},{12,11},... | collective-permute-start | bytes 479240 | tf_op jit(solution)/shard_map/ppermute | solution.py:36

commit v5 on v4

--- a/solution.py
+++ b/solution.py
@@ -31,10 +31,9 @@
 
 def swap(axis, even, odd):
     count = lax.axis_size(axis)
-    return (
-        lax.ppermute(even, axis, swaps(count, 0)),
-        lax.ppermute(odd, axis, swaps(count, 1)),
-    )
+    got_even = lax.ppermute(even, axis, swaps(count, 0))
+    got_odd = lax.ppermute(odd, axis, swaps(count, 1))
+    return got_even, got_odd
 
 
 def place(axis):

time: 165 us -> 165 us (level)
  no operation moved by 1% of the time
where the time goes in v5:
time: 165 us; the launch traced here: 163 us
  starting transfers between devices  75.3 us (46%)
  Pallas kernels  44.1 us (27%)
  waiting for transfers between devices  42.8 us (26%)
    ppermute x14, starting transfers between devices, swap(): got_odd = lax.ppermute(odd, axis, swaps(count, 1))  44.5 us
    pallas_call x14, Pallas kernels, call(): pl.pallas_call(functools.partial(kernel, chain), in_specs=[far] * hbm + [...  44.1 us
    ppermute x14, starting transfers between devices, swap(): got_even = lax.ppermute(even, axis, swaps(count, 0))  30.8 us
    ppermute x14, waiting for transfers between devices, swap(): got_even = lax.ppermute(even, axis, swaps(count, 0))  25.5 us
    ppermute x14, waiting for transfers between devices, swap(): got_odd = lax.ppermute(odd, axis, swaps(count, 1))  17.2 us
  transfers between devices with their start and end apart: 28, of which 7 were waited for; matrix products, arithmetic and copies ran while one was open for 0% of the time, Pallas kernels for 21%

profile of v5, /device:TPU:109, one launch (start us, length us, event | category | flops | bytes accessed | tf_op | source)
XLA Modules:
  0.0 163.2 jit_solution(12296796898067322680)
XLA Ops:
  0.6 2.8 %shard_map.51 = (f32[10,64,128]{2,1,0:T(8,128)}, f32[10,64,128]{2,1,0:T(8,128)}, f32[64,8,128]{2,1,0:T(8,128)}, f32[64,8,128]{2,1,0:T(8,128)}) custom-call(f32[64,64,256]{2,1,0:T(8,128)} %u_hbm.3, f32[64,64,256]{2,1,0:T(8,128)} %f_hbm.3, f32[64,64,256]{2,1,0:T(8,128)} %m_hbm.3), custom_call_target="tpu_custom_call" | custom-call | flops 2000000000 | tf_op jit(solution)/shard_map/pallas_call | solution.py:638
  4.2 4.6 %collective-permute-start.5 = (f32[10,64,128]{2,1,0:T(8,128)}, f32[10,64,128]{2,1,0:T(8,128)S(1)}, u32[]{:S(2)}, u32[]{:S(2)}) collective-permute-start(f32[10,64,128]{2,1,0:T(8,128)} %get-tuple-element.64), channel_id=1, source_target_pairs={{8,16},{16,8},{24,32},{32,24},{40,48},{48,40},{56,64},{64,56},{72,... | collective-permute-start | bytes 983048 | tf_op jit(solution)/shard_map/ppermute | solution.py:35
  12.7 6.0 %shard_map.50 = (f32[64,64,128]{2,1,0:T(8,128)S(1)}, f32[64,64,128]{2,1,0:T(8,128)S(1)}, f32[64,64,128]{2,1,0:T(8,128)S(1)}, f32[64,64,128]{2,1,0:T(8,128)S(1)},...) custom-call(f32[64,64,256]{2,1,0:T(8,128)} %u_hbm.3, ...), custom_call_target="tpu_custom_call" | custom-call | flops 4000000000 | tf_op jit(solution)/shard_map/pallas_call | solution.py:638
  19.7 6.6 %collective-permute-start.1 = (f32[18,64,128]{2,1,0:T(8,128)S(1)}, f32[18,64,128]{2,1,0:T(8,128)S(1)}, u32[]{:S(2)}, u32[]{:S(2)}) collective-permute-start(f32[18,64,128]{2,1,0:T(8,128)S(1)} %get-tuple-element.57), channel_id=1, source_target_pairs={{8,16},{16,8},{24,32},{32,24},{40,48},{48,40},{56,64},{64,56},{72,... | collective-permute-start | bytes 1769480 | tf_op jit(solution)/shard_map/ppermute | solution.py:35
  27.4 2.2 %collective-permute-start.3 = (f32[128,8,128]{2,1,0:T(8,128)S(1)}, f32[128,8,128]{2,1,0:T(8,128)S(1)}, u32[]{:S(2)}, u32[]{:S(2)}) collective-permute-start(f32[128,8,128]{2,1,0:T(8,128)S(1)} %get-tuple-element.59), channel_id=1, source_target_pairs={{1,2},{2,1},{3,4},{4,3},{5,6},{6,5},{9,10},{10,9},{11,12},{12,11},... | collective-permute-start | bytes 1572872 | tf_op jit(solution)/shard_map/ppermute | solution.py:35
  29.8 2.2 %collective-permute-start.8 = (f32[10,8,128]{2,1,0:T(8,128)S(1)}, f32[10,8,128]{2,1,0:T(8,128)S(1)}, u32[]{:S(2)}, u32[]{:S(2)}) collective-permute-start(f32[10,8,128]{2,1,0:T(8,128)S(1)} %get-tuple-element.67), channel_id=1, source_target_pairs={{0,1},{1,0},{2,3},{3,2},{4,5},{5,4},{6,7},{7,6},{8,9},{9,8},{10,11... | collective-permute-start | bytes 122888 | tf_op jit(solution)/shard_map/ppermute | solution.py:34
  32.0 24.7 %collective-permute-done.8.corner_e = f32[10,8,128]{2,1,0:T(8,128)S(1)} collective-permute-done((f32[10,8,128]{2,1,0:T(8,128)S(1)}, f32[10,8,128]{2,1,0:T(8,128)S(1)}, u32[]{:S(2)}, u32[]{:S(2)}) %collective-permute-start.8) | collective-permute-done | bytes 40992 | tf_op jit(solution)/shard_map/ppermute | solution.py:34
  56.6 2.0 %collective-permute-start.9 = (f32[10,8,128]{2,1,0:T(8,128)S(1)}, f32[10,8,128]{2,1,0:T(8,128)S(1)}, u32[]{:S(2)}, u32[]{:S(2)}) collective-permute-start(f32[10,8,128]{2,1,0:T(8,128)S(1)} %get-tuple-element.68), channel_id=1, source_target_pairs={{1,2},{2,1},{3,4},{4,3},{5,6},{6,5},{9,10},{10,9},{11,12},{12,11},... | collective-permute-start | bytes 122888 | tf_op jit(solution)/shard_map/ppermute | solution.py:35
  58.7 4.4 %collective-permute-done.9.corner_o = f32[10,8,128]{2,1,0:T(8,128)S(1)} collective-permute-done((f32[10,8,128]{2,1,0:T(8,128)S(1)}, f32[10,8,128]{2,1,0:T(8,128)S(1)}, u32[]{:S(2)}, u32[]{:S(2)}) %collective-permute-start.9) | collective-permute-done | bytes 40992 | tf_op jit(solution)/shard_map/ppermute | solution.py:35
  63.1 6.5 %shard_map.53 = (f32[72,80,128]{2,1,0:T(8,128)S(1)}, f32[32,32,128]{2,1,0:T(8,128)S(1)}, f32[12,32,128]{2,1,0:T(8,128)S(1)}, f32[12,32,128]{2,1,0:T(8,128)S(1)},...) custom-call(f32[64,64,128]{2,1,0:T(8,128)S(1)} %get-tuple-element.60.u_ref, ...), custom_call_target="tpu_custom_call" | custom-call | flops 3000000000 | tf_op jit(solution)/shard_map/pallas_call | solution.py:638
  70.4 1.9 %collective-permute-start.11 = (f32[10,8,128]{2,1,0:T(8,128)S(1)}, f32[10,8,128]{2,1,0:T(8,128)S(1)}, u32[]{:S(2)}, u32[]{:S(2)}) collective-permute-start(f32[10,8,128]{2,1,0:T(8,128)S(1)} %get-tuple-element.71), channel_id=1, source_target_pairs={{1,2},{2,1},{3,4},{4,3},{5,6},{6,5},{9,10},{10,9},{11,12},{12,11},... | collective-permute-start | bytes 122888 | tf_op jit(solution)/shard_map/ppermute | solution.py:35
  72.3 8.8 %collective-permute-start.20 = (f32[12,32,128]{2,1,0:T(8,128)S(1)}, f32[12,32,128]{2,1,0:T(8,128)S(1)}, u32[]{:S(2)}, u32[]{:S(2)}) collective-permute-start(f32[12,32,128]{2,1,0:T(8,128)S(1)} %get-tuple-element.89), channel_id=1, source_target_pairs={{0,8},{8,0},{16,24},{24,16},{32,40},{40,32},{48,56},{56,48},{64,72... | collective-permute-start | bytes 589832 | tf_op jit(solution)/shard_map/ppermute | solution.py:34
  81.1 4.5 %collective-permute-start.21 = (f32[12,32,128]{2,1,0:T(8,128)S(1)}, f32[12,32,128]{2,1,0:T(8,128)S(1)}, u32[]{:S(2)}, u32[]{:S(2)}) collective-permute-start(f32[12,32,128]{2,1,0:T(8,128)S(1)} %get-tuple-element.90), channel_id=1, source_target_pairs={{8,16},{16,8},{24,32},{32,24},{40,48},{48,40},{56,64},{64,56},{72,... | collective-permute-start | bytes 589832 | tf_op jit(solution)/shard_map/ppermute | solution.py:35
  85.7 6.5 %shard_map.55 = (f32[72,80,128]{2,1,0:T(8,128)S(1)}, f32[32,32,128]{2,1,0:T(8,128)S(1)}, f32[12,32,128]{2,1,0:T(8,128)S(1)}, f32[12,32,128]{2,1,0:T(8,128)S(1)},...) custom-call(f32[64,64,128]{2,1,0:T(8,128)S(1)} %get-tuple-element.54.u_ref, ...), custom_call_target="tpu_custom_call" | custom-call | flops 3000000000 | tf_op jit(solution)/shard_map/pallas_call | solution.py:638
  92.5 5.1 %collective-permute-start.13 = (f32[12,32,128]{2,1,0:T(8,128)S(1)}, f32[12,32,128]{2,1,0:T(8,128)S(1)}, u32[]{:S(2)}, u32[]{:S(2)}) collective-permute-start(f32[12,32,128]{2,1,0:T(8,128)S(1)} %get-tuple-element.76), channel_id=1, source_target_pairs={{8,16},{16,8},{24,32},{32,24},{40,48},{48,40},{56,64},{64,56},{72,... | collective-permute-start | bytes 589832 | tf_op jit(solution)/shard_map/ppermute | solution.py:35
  97.7 2.8 %collective-permute-start.22 = (f32[65,8,128]{2,1,0:T(8,128)S(1)}, f32[65,8,128]{2,1,0:T(8,128)S(1)}, u32[]{:S(2)}, u32[]{:S(2)}) collective-permute-start(f32[65,8,128]{2,1,0:T(8,128)S(1)} %get-tuple-element.91), channel_id=1, source_target_pairs={{0,1},{1,0},{2,3},{3,2},{4,5},{5,4},{6,7},{7,6},{8,9},{9,8},{10,11... | collective-permute-start | bytes 798728 | tf_op jit(solution)/shard_map/ppermute | solution.py:34
  100.5 1.9 %collective-permute-start.23 = (f32[65,8,128]{2,1,0:T(8,128)S(1)}, f32[65,8,128]{2,1,0:T(8,128)S(1)}, u32[]{:S(2)}, u32[]{:S(2)}) collective-permute-start(f32[65,8,128]{2,1,0:T(8,128)S(1)} %get-tuple-element.92), channel_id=1, source_target_pairs={{1,2},{2,1},{3,4},{4,3},{5,6},{6,5},{9,10},{10,9},{11,12},{12,11},... | collective-permute-start | bytes 798728 | tf_op jit(solution)/shard_map/ppermute | solution.py:35
  103.3 3.0 %collective-permute-start.14 = (f32[65,8,128]{2,1,0:T(8,128)S(1)}, f32[65,8,128]{2,1,0:T(8,128)S(1)}, u32[]{:S(2)}, u32[]{:S(2)}) collective-permute-start(f32[65,8,128]{2,1,0:T(8,128)S(1)} %get-tuple-element.77), channel_id=1, source_target_pairs={{0,1},{1,0},{2,3},{3,2},{4,5},{5,4},{6,7},{7,6},{8,9},{9,8},{10,11... | collective-permute-start | bytes 798728 | tf_op jit(solution)/shard_map/ppermute | solution.py:34
  106.3 1.9 %collective-permute-start.15 = (f32[65,8,128]{2,1,0:T(8,128)S(1)}, f32[65,8,128]{2,1,0:T(8,128)S(1)}, u32[]{:S(2)}, u32[]{:S(2)}) collective-permute-start(f32[65,8,128]{2,1,0:T(8,128)S(1)} %get-tuple-element.78), channel_id=1, source_target_pairs={{1,2},{2,1},{3,4},{4,3},{5,6},{6,5},{9,10},{10,9},{11,12},{12,11},... | collective-permute-start | bytes 798728 | tf_op jit(solution)/shard_map/ppermute | solution.py:35
  108.2 5.0 %collective-permute-done.23.refs_7_.coarse_lane_o = f32[65,8,128]{2,1,0:T(8,128)S(1)} collective-permute-done((f32[65,8,128]{2,1,0:T(8,128)S(1)}, f32[65,8,128]{2,1,0:T(8,128)S(1)}, u32[]{:S(2)}, u32[]{:S(2)}) %collective-permute-start.23) | collective-permute-done | bytes 266272 | tf_op jit(solution)/shard_map/ppermute | solution.py:35
  113.2 4.4 %shard_map.60 = (f32[32,32,128]{2,1,0:T(8,128)S(1)}, f32[6,32,128]{2,1,0:T(8,128)S(1)}, f32[6,32,128]{2,1,0:T(8,128)S(1)}, f32[48,48,128]{2,1,0:T(8,128)S(1)}, f32[48,48,128]{2,1,0:T(8,128)S(1)}) custom-call(f32[32,32,128]{2,1,0:T(8,128)S(1)} %get-tuple-element.69.refs_0_.load_ref, f32[2,32,32,128]{3,2,1,0:T(8,128)S(1)} %get-tuple-element.74.refs_1_, ...), custom_call_target="tpu_custom_call" | custom-call | flops 2000000000 | tf_op jit(solution)/shard_map/pallas_call | solution.py:638
  117.6 3.5 %collective-permute-start.24 = (f32[6,32,128]{2,1,0:T(8,128)S(1)}, f32[6,32,128]{2,1,0:T(8,128)S(1)}, u32[]{:S(2)}, u32[]{:S(2)}) collective-permute-start(f32[6,32,128]{2,1,0:T(8,128)S(1)} %get-tuple-element.98), channel_id=1, source_target_pairs={{0,8},{8,0},{16,24},{24,16},{32,40},{40,32},{48,56},{56,48},{64,72... | collective-permute-start | bytes 294920 | tf_op jit(solution)/shard_map/ppermute | solution.py:34
  121.1 3.5 %collective-permute-start.25 = (f32[6,32,128]{2,1,0:T(8,128)S(1)}, f32[6,32,128]{2,1,0:T(8,128)S(1)}, u32[]{:S(2)}, u32[]{:S(2)}) collective-permute-start(f32[6,32,128]{2,1,0:T(8,128)S(1)} %get-tuple-element.99), channel_id=1, source_target_pairs={{8,16},{16,8},{24,32},{32,24},{40,48},{48,40},{56,64},{64,56},{72,... | collective-permute-start | bytes 294920 | tf_op jit(solution)/shard_map/ppermute | solution.py:35
  124.6 4.0 %shard_map.57 = (f32[32,32,128]{2,1,0:T(8,128)S(1)}, f32[6,32,128]{2,1,0:T(8,128)S(1)}, f32[6,32,128]{2,1,0:T(8,128)S(1)}, f32[48,48,128]{2,1,0:T(8,128)S(1)}, f32[48,48,128]{2,1,0:T(8,128)S(1)}) custom-call(f32[32,32,128]{2,1,0:T(8,128)S(1)} %get-tuple-element.73.load_ref.refs_0_, f32[2,32,32,128]{3,2,1,0:T(8,128)S(1)} %get-tuple-element.74.refs_1_, ...), custom_call_target="tpu_custom_call" | custom-call | flops 2000000000 | tf_op jit(solution)/shard_map/pallas_call | solution.py:638
  128.7 1.9 %collective-permute-done.25.got_o.value_o = f32[6,32,128]{2,1,0:T(8,128)S(1)} collective-permute-done((f32[6,32,128]{2,1,0:T(8,128)S(1)}, f32[6,32,128]{2,1,0:T(8,128)S(1)}, u32[]{:S(2)}, u32[]{:S(2)}) %collective-permute-start.25) | collective-permute-done | bytes 98336 | tf_op jit(solution)/shard_map/ppermute | solution.py:35
  132.1 1.9 %collective-permute-start.27 = (f32[39,8,128]{2,1,0:T(8,128)S(1)}, f32[39,8,128]{2,1,0:T(8,128)S(1)}, u32[]{:S(2)}, u32[]{:S(2)}) collective-permute-start(f32[39,8,128]{2,1,0:T(8,128)S(1)} %get-tuple-element.101), channel_id=1, source_target_pairs={{1,2},{2,1},{3,4},{4,3},{5,6},{6,5},{9,10},{10,9},{11,12},{12,11},... | collective-permute-start | bytes 479240 | tf_op jit(solution)/shard_map/ppermute | solution.py:35
  134.5 4.4 %collective-permute-start.17 = (f32[6,32,128]{2,1,0:T(8,128)S(1)}, f32[6,32,128]{2,1,0:T(8,128)S(1)}, u32[]{:S(2)}, u32[]{:S(2)}) collective-permute-start(f32[6,32,128]{2,1,0:T(8,128)S(1)} %get-tuple-element.85), channel_id=1, source_target_pairs={{8,16},{16,8},{24,32},{32,24},{40,48},{48,40},{56,64},{64,56},{72,... | collective-permute-start | bytes 294920 | tf_op jit(solution)/shard_map/ppermute | solution.py:35
  138.9 5.1 %collective-permute-done.17.got_o.value_o = f32[6,32,128]{2,1,0:T(8,128)S(1)} collective-permute-done((f32[6,32,128]{2,1,0:T(8,128)S(1)}, f32[6,32,128]{2,1,0:T(8,128)S(1)}, u32[]{:S(2)}, u32[]{:S(2)}) %collective-permute-start.17) | collective-permute-done | bytes 98336 | tf_op jit(solution)/shard_map/ppermute | solution.py:35
  144.1 3.7 %collective-permute-start.18 = (f32[39,8,128]{2,1,0:T(8,128)S(1)}, f32[39,8,128]{2,1,0:T(8,128)S(1)}, u32[]{:S(2)}, u32[]{:S(2)}) collective-permute-start(f32[39,8,128]{2,1,0:T(8,128)S(1)} %get-tuple-element.86), channel_id=1, source_target_pairs={{0,1},{1,0},{2,3},{3,2},{4,5},{5,4},{6,7},{7,6},{8,9},{9,8},{10,11... | collective-permute-start | bytes 479240 | tf_op jit(solution)/shard_map/ppermute | solution.py:34
  147.8 1.9 %collective-permute-start.19 = (f32[39,8,128]{2,1,0:T(8,128)S(1)}, f32[39,8,128]{2,1,0:T(8,128)S(1)}, u32[]{:S(2)}, u32[]{:S(2)}) collective-permute-start(f32[39,8,128]{2,1,0:T(8,128)S(1)} %get-tuple-element.87), channel_id=1, source_target_pairs={{1,2},{2,1},{3,4},{4,3},{5,6},{6,5},{9,10},{10,9},{11,12},{12,11},... | collective-permute-start | bytes 479240 | tf_op jit(solution)/shard_map/ppermute | solution.py:35
  149.8 6.7 %shard_map.62 = (f32[64,64,256]{2,1,0:T(8,128)}, f32[64,64,256]{2,1,0:T(8,128)}) custom-call(f32[64,64,128]{2,1,0:T(8,128)S(1)} %get-tuple-element.62.m_ref.m_own, f32[72,80,128]{2,1,0:T(8,128)S(1)} %get-tuple-element.88.v_ref, f32[32,32,128]{2,1,0:T(8,128)S(1)} %get-tuple-element.93.x_ref, f32[72,80,128]{2,1,0:T(8,128)S(1)} %get-tuple-element.94.load, ...), custom_call_target="tpu_custom_call" | custom-call | flops 4000000000 | tf_op jit(solution)/shard_map/pallas_call | solution.py:638
  156.5 6.6 %shard_map.63 = (f32[64,64,256]{2,1,0:T(8,128)}, f32[64,64,256]{2,1,0:T(8,128)}) custom-call(f32[64,64,128]{2,1,0:T(8,128)S(1)} %copy-done, f32[72,80,128]{2,1,0:T(8,128)S(1)} %get-tuple-element.72.v_ref, f32[32,32,128]{2,1,0:T(8,128)S(1)} %get-tuple-element.79.x_ref.refs_0_, ...), custom_call_target="tpu_custom_call", output_to_operand_aliasing={{0}: (15, {}), {1}: (16, {})} | custom-call | flops 4000000000 | tf_op jit(solution)/shard_map/pallas_call | solution.py:638
  (40 shorter events, 10.6 us)
Async XLA Ops:
  3.5 22.8 %collective-permute-start.4 = (f32[10,64,128]{2,1,0:T(8,128)}, f32[10,64,128]{2,1,0:T(8,128)S(1)}, u32[]{:S(2)}, u32[]{:S(2)}) collective-permute-start(f32[10,64,128]{2,1,0:T(8,128)} %get-tuple-element.63), channel_id=1, source_target_pairs={{0,8},{8,0},{16,24},{24,16},{32,40},{40,32},{48,56},{56,48},{64,72... | collective-permute-start | bytes 983048 | tf_op jit(solution)/shard_map/ppermute | solution.py:34
  4.2 23.2 %collective-permute-start.5 = (f32[10,64,128]{2,1,0:T(8,128)}, f32[10,64,128]{2,1,0:T(8,128)S(1)}, u32[]{:S(2)}, u32[]{:S(2)}) collective-permute-start(f32[10,64,128]{2,1,0:T(8,128)} %get-tuple-element.64), channel_id=1, source_target_pairs={{8,16},{16,8},{24,32},{32,24},{40,48},{48,40},{56,64},{64,56},{72,... | collective-permute-start | bytes 983048 | tf_op jit(solution)/shard_map/ppermute | solution.py:35
  8.9 10.8 %collective-permute-start.6 = (f32[64,8,128]{2,1,0:T(8,128)}, f32[64,8,128]{2,1,0:T(8,128)S(1)}, u32[]{:S(2)}, u32[]{:S(2)}) collective-permute-start(f32[64,8,128]{2,1,0:T(8,128)} %get-tuple-element.65), channel_id=1, source_target_pairs={{0,1},{1,0},{2,3},{3,2},{4,5},{5,4},{6,7},{7,6},{8,9},{9,8},{10,11... | collective-permute-start | bytes 786440 | tf_op jit(solution)/shard_map/ppermute | solution.py:34
  10.8 19.0 %collective-permute-start.7 = (f32[64,8,128]{2,1,0:T(8,128)}, f32[64,8,128]{2,1,0:T(8,128)S(1)}, u32[]{:S(2)}, u32[]{:S(2)}) collective-permute-start(f32[64,8,128]{2,1,0:T(8,128)} %get-tuple-element.66), channel_id=1, source_target_pairs={{1,2},{2,1},{3,4},{4,3},{5,6},{6,5},{9,10},{10,9},{11,12},{12,11},... | collective-permute-start | bytes 786440 | tf_op jit(solution)/shard_map/ppermute | solution.py:35
  18.7 50.9 %collective-permute-start = (f32[18,64,128]{2,1,0:T(8,128)S(1)}, f32[18,64,128]{2,1,0:T(8,128)S(1)}, u32[]{:S(2)}, u32[]{:S(2)}) collective-permute-start(f32[18,64,128]{2,1,0:T(8,128)S(1)} %get-tuple-element.56), channel_id=1, source_target_pairs={{0,8},{8,0},{16,24},{24,16},{32,40},{40,32},{48,56},{56,48},{64,72... | collective-permute-start | bytes 1769480 | tf_op jit(solution)/shard_map/ppermute | solution.py:34
  19.7 50.0 %collective-permute-start.1 = (f32[18,64,128]{2,1,0:T(8,128)S(1)}, f32[18,64,128]{2,1,0:T(8,128)S(1)}, u32[]{:S(2)}, u32[]{:S(2)}) collective-permute-start(f32[18,64,128]{2,1,0:T(8,128)S(1)} %get-tuple-element.57), channel_id=1, source_target_pairs={{8,16},{16,8},{24,32},{32,24},{40,48},{48,40},{56,64},{64,56},{72,... | collective-permute-start | bytes 1769480 | tf_op jit(solution)/shard_map/ppermute | solution.py:35
  26.3 54.8 %collective-permute-start.2 = (f32[128,8,128]{2,1,0:T(8,128)S(1)}, f32[128,8,128]{2,1,0:T(8,128)S(1)}, u32[]{:S(2)}, u32[]{:S(2)}) collective-permute-start(f32[128,8,128]{2,1,0:T(8,128)S(1)} %get-tuple-element.58), channel_id=1, source_target_pairs={{0,1},{1,0},{2,3},{3,2},{4,5},{5,4},{6,7},{7,6},{8,9},{9,8},{10,11... | collective-permute-start | bytes 1572872 | tf_op jit(solution)/shard_map/ppermute | solution.py:34
  27.4 58.2 %collective-permute-start.3 = (f32[128,8,128]{2,1,0:T(8,128)S(1)}, f32[128,8,128]{2,1,0:T(8,128)S(1)}, u32[]{:S(2)}, u32[]{:S(2)}) collective-permute-start(f32[128,8,128]{2,1,0:T(8,128)S(1)} %get-tuple-element.59), channel_id=1, source_target_pairs={{1,2},{2,1},{3,4},{4,3},{5,6},{6,5},{9,10},{10,9},{11,12},{12,11},... | collective-permute-start | bytes 1572872 | tf_op jit(solution)/shard_map/ppermute | solution.py:35
  29.8 26.9 %collective-permute-start.8 = (f32[10,8,128]{2,1,0:T(8,128)S(1)}, f32[10,8,128]{2,1,0:T(8,128)S(1)}, u32[]{:S(2)}, u32[]{:S(2)}) collective-permute-start(f32[10,8,128]{2,1,0:T(8,128)S(1)} %get-tuple-element.67), channel_id=1, source_target_pairs={{0,1},{1,0},{2,3},{3,2},{4,5},{5,4},{6,7},{7,6},{8,9},{9,8},{10,11... | collective-permute-start | bytes 122888 | tf_op jit(solution)/shard_map/ppermute | solution.py:34
  56.6 13.0 %copy-start = (f32[64,64,128]{2,1,0:T(8,128)S(1)}, f32[64,64,128]{2,1,0:T(8,128)}, u32[]{:S(2)}) copy-start(f32[64,64,128]{2,1,0:T(8,128)} %get-tuple-element.53.m_ref.m_own) | copy-start | bytes 6291460
  56.6 6.5 %collective-permute-start.9 = (f32[10,8,128]{2,1,0:T(8,128)S(1)}, f32[10,8,128]{2,1,0:T(8,128)S(1)}, u32[]{:S(2)}, u32[]{:S(2)}) collective-permute-start(f32[10,8,128]{2,1,0:T(8,128)S(1)} %get-tuple-element.68), channel_id=1, source_target_pairs={{1,2},{2,1},{3,4},{4,3},{5,6},{6,5},{9,10},{10,9},{11,12},{12,11},... | collective-permute-start | bytes 122888 | tf_op jit(solution)/shard_map/ppermute | solution.py:35
  69.8 15.9 %collective-permute-start.10 = (f32[10,8,128]{2,1,0:T(8,128)S(1)}, f32[10,8,128]{2,1,0:T(8,128)S(1)}, u32[]{:S(2)}, u32[]{:S(2)}) collective-permute-start(f32[10,8,128]{2,1,0:T(8,128)S(1)} %get-tuple-element.70), channel_id=1, source_target_pairs={{0,1},{1,0},{2,3},{3,2},{4,5},{5,4},{6,7},{7,6},{8,9},{9,8},{10,11... | collective-permute-start | bytes 122888 | tf_op jit(solution)/shard_map/ppermute | solution.py:34
  70.4 15.3 %collective-permute-start.11 = (f32[10,8,128]{2,1,0:T(8,128)S(1)}, f32[10,8,128]{2,1,0:T(8,128)S(1)}, u32[]{:S(2)}, u32[]{:S(2)}) collective-permute-start(f32[10,8,128]{2,1,0:T(8,128)S(1)} %get-tuple-element.71), channel_id=1, source_target_pairs={{1,2},{2,1},{3,4},{4,3},{5,6},{6,5},{9,10},{10,9},{11,12},{12,11},... | collective-permute-start | bytes 122888 | tf_op jit(solution)/shard_map/ppermute | solution.py:35
  72.3 25.3 %collective-permute-start.20 = (f32[12,32,128]{2,1,0:T(8,128)S(1)}, f32[12,32,128]{2,1,0:T(8,128)S(1)}, u32[]{:S(2)}, u32[]{:S(2)}) collective-permute-start(f32[12,32,128]{2,1,0:T(8,128)S(1)} %get-tuple-element.89), channel_id=1, source_target_pairs={{0,8},{8,0},{16,24},{24,16},{32,40},{40,32},{48,56},{56,48},{64,72... | collective-permute-start | bytes 589832 | tf_op jit(solution)/shard_map/ppermute | solution.py:34
  81.1 16.5 %collective-permute-start.21 = (f32[12,32,128]{2,1,0:T(8,128)S(1)}, f32[12,32,128]{2,1,0:T(8,128)S(1)}, u32[]{:S(2)}, u32[]{:S(2)}) collective-permute-start(f32[12,32,128]{2,1,0:T(8,128)S(1)} %get-tuple-element.90), channel_id=1, source_target_pairs={{8,16},{16,8},{24,32},{32,24},{40,48},{48,40},{56,64},{64,56},{72,... | collective-permute-start | bytes 589832 | tf_op jit(solution)/shard_map/ppermute | solution.py:35
  92.2 10.2 %collective-permute-start.12 = (f32[12,32,128]{2,1,0:T(8,128)S(1)}, f32[12,32,128]{2,1,0:T(8,128)S(1)}, u32[]{:S(2)}, u32[]{:S(2)}) collective-permute-start(f32[12,32,128]{2,1,0:T(8,128)S(1)} %get-tuple-element.75), channel_id=1, source_target_pairs={{0,8},{8,0},{16,24},{24,16},{32,40},{40,32},{48,56},{56,48},{64,72... | collective-permute-start | bytes 589832 | tf_op jit(solution)/shard_map/ppermute | solution.py:34
  92.5 10.7 %collective-permute-start.13 = (f32[12,32,128]{2,1,0:T(8,128)S(1)}, f32[12,32,128]{2,1,0:T(8,128)S(1)}, u32[]{:S(2)}, u32[]{:S(2)}) collective-permute-start(f32[12,32,128]{2,1,0:T(8,128)S(1)} %get-tuple-element.76), channel_id=1, source_target_pairs={{8,16},{16,8},{24,32},{32,24},{40,48},{48,40},{56,64},{64,56},{72,... | collective-permute-start | bytes 589832 | tf_op jit(solution)/shard_map/ppermute | solution.py:35
  97.7 10.5 %collective-permute-start.22 = (f32[65,8,128]{2,1,0:T(8,128)S(1)}, f32[65,8,128]{2,1,0:T(8,128)S(1)}, u32[]{:S(2)}, u32[]{:S(2)}) collective-permute-start(f32[65,8,128]{2,1,0:T(8,128)S(1)} %get-tuple-element.91), channel_id=1, source_target_pairs={{0,1},{1,0},{2,3},{3,2},{4,5},{5,4},{6,7},{7,6},{8,9},{9,8},{10,11... | collective-permute-start | bytes 798728 | tf_op jit(solution)/shard_map/ppermute | solution.py:34
  100.5 12.7 %collective-permute-start.23 = (f32[65,8,128]{2,1,0:T(8,128)S(1)}, f32[65,8,128]{2,1,0:T(8,128)S(1)}, u32[]{:S(2)}, u32[]{:S(2)}) collective-permute-start(f32[65,8,128]{2,1,0:T(8,128)S(1)} %get-tuple-element.92), channel_id=1, source_target_pairs={{1,2},{2,1},{3,4},{4,3},{5,6},{6,5},{9,10},{10,9},{11,12},{12,11},... | collective-permute-start | bytes 798728 | tf_op jit(solution)/shard_map/ppermute | solution.py:35
  103.3 21.3 %collective-permute-start.14 = (f32[65,8,128]{2,1,0:T(8,128)S(1)}, f32[65,8,128]{2,1,0:T(8,128)S(1)}, u32[]{:S(2)}, u32[]{:S(2)}) collective-permute-start(f32[65,8,128]{2,1,0:T(8,128)S(1)} %get-tuple-element.77), channel_id=1, source_target_pairs={{0,1},{1,0},{2,3},{3,2},{4,5},{5,4},{6,7},{7,6},{8,9},{9,8},{10,11... | collective-permute-start | bytes 798728 | tf_op jit(solution)/shard_map/ppermute | solution.py:34
  106.3 18.3 %collective-permute-start.15 = (f32[65,8,128]{2,1,0:T(8,128)S(1)}, f32[65,8,128]{2,1,0:T(8,128)S(1)}, u32[]{:S(2)}, u32[]{:S(2)}) collective-permute-start(f32[65,8,128]{2,1,0:T(8,128)S(1)} %get-tuple-element.78), channel_id=1, source_target_pairs={{1,2},{2,1},{3,4},{4,3},{5,6},{6,5},{9,10},{10,9},{11,12},{12,11},... | collective-permute-start | bytes 798728 | tf_op jit(solution)/shard_map/ppermute | solution.py:35
  117.6 11.1 %collective-permute-start.24 = (f32[6,32,128]{2,1,0:T(8,128)S(1)}, f32[6,32,128]{2,1,0:T(8,128)S(1)}, u32[]{:S(2)}, u32[]{:S(2)}) collective-permute-start(f32[6,32,128]{2,1,0:T(8,128)S(1)} %get-tuple-element.98), channel_id=1, source_target_pairs={{0,8},{8,0},{16,24},{24,16},{32,40},{40,32},{48,56},{56,48},{64,72... | collective-permute-start | bytes 294920 | tf_op jit(solution)/shard_map/ppermute | solution.py:34
  121.1 9.5 %collective-permute-start.25 = (f32[6,32,128]{2,1,0:T(8,128)S(1)}, f32[6,32,128]{2,1,0:T(8,128)S(1)}, u32[]{:S(2)}, u32[]{:S(2)}) collective-permute-start(f32[6,32,128]{2,1,0:T(8,128)S(1)} %get-tuple-element.99), channel_id=1, source_target_pairs={{8,16},{16,8},{24,32},{32,24},{40,48},{48,40},{56,64},{64,56},{72,... | collective-permute-start | bytes 294920 | tf_op jit(solution)/shard_map/ppermute | solution.py:35
  130.7 19.1 %collective-permute-start.26 = (f32[39,8,128]{2,1,0:T(8,128)S(1)}, f32[39,8,128]{2,1,0:T(8,128)S(1)}, u32[]{:S(2)}, u32[]{:S(2)}) collective-permute-start(f32[39,8,128]{2,1,0:T(8,128)S(1)} %get-tuple-element.100), channel_id=1, source_target_pairs={{0,1},{1,0},{2,3},{3,2},{4,5},{5,4},{6,7},{7,6},{8,9},{9,8},{10,11... | collective-permute-start | bytes 479240 | tf_op jit(solution)/shard_map/ppermute | solution.py:34
  132.1 17.7 %collective-permute-start.27 = (f32[39,8,128]{2,1,0:T(8,128)S(1)}, f32[39,8,128]{2,1,0:T(8,128)S(1)}, u32[]{:S(2)}, u32[]{:S(2)}) collective-permute-start(f32[39,8,128]{2,1,0:T(8,128)S(1)} %get-tuple-element.101), channel_id=1, source_target_pairs={{1,2},{2,1},{3,4},{4,3},{5,6},{6,5},{9,10},{10,9},{11,12},{12,11},... | collective-permute-start | bytes 479240 | tf_op jit(solution)/shard_map/ppermute | solution.py:35
  134.0 4.9 %collective-permute-start.16 = (f32[6,32,128]{2,1,0:T(8,128)S(1)}, f32[6,32,128]{2,1,0:T(8,128)S(1)}, u32[]{:S(2)}, u32[]{:S(2)}) collective-permute-start(f32[6,32,128]{2,1,0:T(8,128)S(1)} %get-tuple-element.84), channel_id=1, source_target_pairs={{0,8},{8,0},{16,24},{24,16},{32,40},{40,32},{48,56},{56,48},{64,72... | collective-permute-start | bytes 294920 | tf_op jit(solution)/shard_map/ppermute | solution.py:34
  134.5 9.5 %collective-permute-start.17 = (f32[6,32,128]{2,1,0:T(8,128)S(1)}, f32[6,32,128]{2,1,0:T(8,128)S(1)}, u32[]{:S(2)}, u32[]{:S(2)}) collective-permute-start(f32[6,32,128]{2,1,0:T(8,128)S(1)} %get-tuple-element.85), channel_id=1, source_target_pairs={{8,16},{16,8},{24,32},{32,24},{40,48},{48,40},{56,64},{64,56},{72,... | collective-permute-start | bytes 294920 | tf_op jit(solution)/shard_map/ppermute | solution.py:35
  144.1 12.4 %collective-permute-start.18 = (f32[39,8,128]{2,1,0:T(8,128)S(1)}, f32[39,8,128]{2,1,0:T(8,128)S(1)}, u32[]{:S(2)}, u32[]{:S(2)}) collective-permute-start(f32[39,8,128]{2,1,0:T(8,128)S(1)} %get-tuple-element.86), channel_id=1, source_target_pairs={{0,1},{1,0},{2,3},{3,2},{4,5},{5,4},{6,7},{7,6},{8,9},{9,8},{10,11... | collective-permute-start | bytes 479240 | tf_op jit(solution)/shard_map/ppermute | solution.py:34
  147.8 8.7 %collective-permute-start.19 = (f32[39,8,128]{2,1,0:T(8,128)S(1)}, f32[39,8,128]{2,1,0:T(8,128)S(1)}, u32[]{:S(2)}, u32[]{:S(2)}) collective-permute-start(f32[39,8,128]{2,1,0:T(8,128)S(1)} %get-tuple-element.87), channel_id=1, source_target_pairs={{1,2},{2,1},{3,4},{4,3},{5,6},{6,5},{9,10},{10,9},{11,12},{12,11},... | collective-permute-start | bytes 479240 | tf_op jit(solution)/shard_map/ppermute | solution.py:35
